TPU v7x, 512 devices: a whole 4x8x8 slice. The times are simulated.
512 devices in a mesh: grid: 64 (over z, y_hi, x), band: 8 (over y_lo, core).
Axes of the slice: x: 4, y: 8 (y_hi: 2, y_lo: 4; y = y_hi * 4 + y_lo), z: 8, core: 2. Of those that a mesh axis runs over, the one named last changes fastest.
Arguments:
- states: float32 [16384, 1024], P('grid', 'band'), may hold values from -6 to 6
- potential: float32 [16384], P('grid'), may hold values from -3 to 0
- bounds: float32 [3], replicated, may hold values from -9 to 26, as said below
- point_count: int32 [64], P('grid'), may hold values from 128 to 256, as said below
- send_rows: int32 [64, 6, 64], P('grid'), may hold values from 0 to 256
- stencil_table: int32 [36, 16384], P(None, 'grid'), may hold values from 0 to 640, as said below
Outputs:
- filtered: float32 [16384, 1024], P('grid', 'band')
- margin: float32 [1024, 1024], P(('grid', 'band'))
Inputs may be any that keep to these rules, and one draw needn't show every extreme that they name: `point_count`: one partition has exactly 256 live points in every draw; rows at or past a partition's count are padding. A block has a length from half of 64 to 64: below it the entries are live rows of g, from it on they are 256; some block is full in every draw. Blocks to partitions that do not exist hold only 256. stencil_table[s, g * 256 + r] indexes E_g: values below 256 are live rows of partition g, 256 is the zero row, 257 + k * 64 + j is row j of the block from partition g - o_k, named only when that partition exists. Padding rows hold only 256; rows r below 160 name no block. bounds holds lower, cutoff and upper in this order: lower between -9 and -5, cutoff between -1.5 and 1.5, upper between 21 and 26.
All inputs are finite; a program needn't handle non-finite values.
Results may differ from a plain program's by a relative error of at most 0.0018.
Values may be sent and summed in bfloat16 or wider, within the bound.
No kernel may reach another device: no remote copies, remote signals or barrier semaphores. Data moves between devices by JAX's collectives and lax.ppermute only.
A program may use at most 64 MiB of HBM per device.

v0:
```python
import jax
import jax.numpy as jnp
from jax import lax
from jax.sharding import PartitionSpec as P

SPAN = 6
DEGREE = 3


DIFFERENCE_WEIGHTS = (
    -5369.0 / 1800.0,
    12.0 / 7.0,
    -15.0 / 56.0,
    10.0 / 189.0,
    -1.0 / 112.0,
    2.0 / 1925.0,
    -1.0 / 16632.0,
)
KINETIC_SCALE = 0.5 / 0.49
CENTRE_WEIGHT = -3.0 * KINETIC_SCALE * DIFFERENCE_WEIGHTS[0]


def passed_along(block, axis, distance):
    devices = range(lax.axis_size(axis))
    route = [(i - distance, i) for i in devices if i - distance in devices]
    return lax.ppermute(block, axis, route)


def in_blocks(shard, dim, peers):
    before, after = (shard.shape[:dim], shard.shape[dim + 1 :])
    return jnp.moveaxis(shard.reshape(*before, peers, -1, *after), dim, 0)


def sum_at_owner(shard, axis, dim):
    peers = lax.axis_size(axis)
    blocks = lax.all_to_all(in_blocks(shard, dim, peers), axis, 0, 0, tiled=True)
    return jnp.sum(blocks.astype(jnp.float32), axis=0)


def apply_stencil(extended, local_table, fields, potentials):
    result = (potentials + CENTRE_WEIGHT)[:, None] * fields
    for neighbour in range(local_table.shape[0]):
        weight = -KINETIC_SCALE * DIFFERENCE_WEIGHTS[neighbour % SPAN + 1]
        result = result + weight * jnp.take(extended, local_table[neighbour], axis=0)
    return result


def boundary_blocks(own_rows, send_rows):
    half_slots = send_rows.shape[1] // 2
    received = []
    for slot_index in range(2 * half_slots):
        offset = slot_index - half_slots if slot_index < half_slots else slot_index - half_slots + 1
        outgoing = jnp.take(own_rows, send_rows[0, slot_index], axis=0)
        received.append(
            passed_along(outgoing.astype(jnp.bfloat16), "grid", offset).astype(outgoing.dtype)
        )
    return jnp.concatenate(received, axis=0)


def operate(fields, potential, send_rows, stencil_table):
    zero_row = jnp.zeros((1, fields.shape[1]), jnp.float32)
    own_rows = jnp.concatenate([fields, zero_row], axis=0)
    extended = jnp.concatenate([own_rows, boundary_blocks(own_rows, send_rows)], axis=0)
    image = apply_stencil(extended, stencil_table, fields, potential)
    return image


def on_device(states, potential, bounds, point_count, send_rows, stencil_table):
    row_count = states.shape[0]
    live_rows = lax.broadcasted_iota(jnp.int32, (row_count, 1), 0) < point_count[0]
    previous = jnp.where(live_rows, states, 0.0)
    lower_bound = bounds[0]
    cutoff = bounds[1]
    upper_bound = bounds[2]
    half_width = (upper_bound - cutoff) / 2.0
    middle = (upper_bound + cutoff) / 2.0
    sigma_now = half_width / (lower_bound - middle)
    twice_inverse = 2.0 / sigma_now
    applied = operate(previous, potential, send_rows, stencil_table)
    current = (applied - middle * previous) * (sigma_now / half_width)
    for degree_index in range(DEGREE - 1):
        sigma_next = 1.0 / (twice_inverse - sigma_now)
        applied = operate(current, potential, send_rows, stencil_table)
        following = (applied - middle * current) * (
            2.0 * sigma_next / half_width
        ) - sigma_now * sigma_next * previous
        previous = current
        current = following
        sigma_now = sigma_next
    rounded = current.astype(jnp.bfloat16)
    grid_count = lax.axis_size("grid")
    band_count = lax.axis_size("band")
    scaling = 1.0 / (grid_count * row_count)
    every_band = lax.all_gather(rounded, "band", axis=1, tiled=True)
    per_device = rounded.shape[1] // grid_count
    arranged = every_band.reshape(row_count, grid_count, band_count, per_device)
    chosen = lax.dynamic_index_in_dim(arranged, lax.axis_index("band"), 2, keepdims=False).reshape(
        row_count, grid_count * per_device
    )
    partial_sums = jnp.einsum("pi,pj->ij", chosen, every_band, preferred_element_type=jnp.float32)
    summed = sum_at_owner(partial_sums.astype(jnp.bfloat16), "grid", 0)
    return (current, summed * scaling)


def solution(mesh):
    placed = (P("grid", "band"), P("grid"), P(), P("grid"), P("grid", None, None), P(None, "grid"))
    return jax.shard_map(
        on_device,
        mesh=mesh,
        in_specs=placed,
        out_specs=(P("grid", "band"), P(("grid", "band"), None)),
        check_vma=False,
    )
```

profile of v0, /device:TPU:16, one launch (start us, length us, event | category | flops | bytes accessed | tf_op | source)
XLA Modules:
  0.0 322.6 jit_solution(11595144537545633421)
XLA Ops:
  8.6 4.5 %collective-permute-start.3 = (bf16[64,128]{1,0:T(8,128)(2,1)S(1)}, bf16[64,128]{1,0:T(8,128)(2,1)S(1)}, u32[]{:S(2)}, u32[]{:S(2)}) collective-permute-start(bf16[64,128]{1,0:T(8,128)(2,1)S(1)} %select_convert_fusion.14), channel_id=1, source_target_pairs={{0,8},{8,16},{16,24},{24,32},{32,40},{40,48},{48,56},{56,64},{64,7... | collective-permute-start | bytes 49160 | tf_op jit(solution)/shard_map/ppermute | solution.py:26
  13.9 6.1 %collective-permute-start.4 = (bf16[64,128]{1,0:T(8,128)(2,1)S(1)}, bf16[64,128]{1,0:T(8,128)(2,1)S(1)}, u32[]{:S(2)}, u32[]{:S(2)}) collective-permute-start(bf16[64,128]{1,0:T(8,128)(2,1)S(1)} %select_convert_fusion.13), channel_id=1, source_target_pairs={{0,16},{8,24},{16,32},{24,40},{32,48},{40,56},{48,64},{56,72},{64,... | collective-permute-start | bytes 49160 | tf_op jit(solution)/shard_map/ppermute | solution.py:26
  20.8 9.4 %collective-permute-start.5 = (bf16[64,128]{1,0:T(8,128)(2,1)S(1)}, bf16[64,128]{1,0:T(8,128)(2,1)S(1)}, u32[]{:S(2)}, u32[]{:S(2)}) collective-permute-start(bf16[64,128]{1,0:T(8,128)(2,1)S(1)} %select_convert_fusion.12), channel_id=1, source_target_pairs={{0,24},{8,32},{16,40},{24,48},{32,56},{40,64},{48,72},{56,80},{64,... | collective-permute-start | bytes 49160 | tf_op jit(solution)/shard_map/ppermute | solution.py:26
  48.3 3.8 %collective-permute-done = bf16[64,128]{1,0:T(8,128)(2,1)S(1)} collective-permute-done((bf16[64,128]{1,0:T(8,128)(2,1)S(1)}, bf16[64,128]{1,0:T(8,128)(2,1)S(1)}, u32[]{:S(2)}, u32[]{:S(2)}) %collective-permute-start) | collective-permute-done | bytes 16416 | tf_op jit(solution)/shard_map/ppermute | solution.py:26
  86.8 1.6 gather_fusion.41
  89.1 5.2 %fusion.80 = f32[256,128]{1,0:T(8,128)S(1)} fusion(f32[256,128]{1,0:T(8,128)} %gather_fusion.41, f32[256,128]{1,0:T(8,128)} %gather_fusion.40, f32[256,128]{1,0:T(8,128)S(1)} %gather_fusion.39, f32[256,128]{1,0:T(8,128)S(1)} %gather_fusion.38, f32[256,128]{1,0:T(8,128)S(1)} %gather_fusion.37, f32[256,128]{1,0:T(8,128)S(1)} %gather_fusion.36, ...), kind=kLoop, calls=%fused_computation.281 | loop fusion | flops 3702784 | bytes 4991240 | tf_op jit(solution)/shard_map/mul | solution.py:80
  99.1 9.9 %collective-permute-start.10 = (bf16[64,128]{1,0:T(8,128)(2,1)S(1)}, bf16[64,128]{1,0:T(8,128)(2,1)S(1)}, u32[]{:S(2)}, u32[]{:S(2)}) collective-permute-start(bf16[64,128]{1,0:T(8,128)(2,1)S(1)} %select_convert_fusion.7), channel_id=1, source_target_pairs={{0,16},{8,24},{16,32},{24,40},{32,48},{40,56},{48,64},{56,72},{64,... | collective-permute-start | bytes 49160 | tf_op jit(solution)/shard_map/ppermute | solution.py:26
  109.1 4.5 %collective-permute-start.11 = (bf16[64,128]{1,0:T(8,128)(2,1)S(1)}, bf16[64,128]{1,0:T(8,128)(2,1)S(1)}, u32[]{:S(2)}, u32[]{:S(2)}) collective-permute-start(bf16[64,128]{1,0:T(8,128)(2,1)S(1)} %select_convert_fusion.6), channel_id=1, source_target_pairs={{0,24},{8,32},{16,40},{24,48},{32,56},{40,64},{48,72},{56,80},{64,... | collective-permute-start | bytes 49160 | tf_op jit(solution)/shard_map/ppermute | solution.py:26
  116.6 5.1 %collective-permute-start.9 = (bf16[64,128]{1,0:T(8,128)(2,1)S(1)}, bf16[64,128]{1,0:T(8,128)(2,1)S(1)}, u32[]{:S(2)}, u32[]{:S(2)}) collective-permute-start(bf16[64,128]{1,0:T(8,128)(2,1)S(1)} %select_convert_fusion.8), channel_id=1, source_target_pairs={{0,8},{8,16},{16,24},{24,32},{32,40},{40,48},{48,56},{56,64},{64,7... | collective-permute-start | bytes 49160 | tf_op jit(solution)/shard_map/ppermute | solution.py:26
  121.7 1.5 collective-permute-start.6
  123.4 13.2 %collective-permute-done.6 = bf16[64,128]{1,0:T(8,128)(2,1)S(1)} collective-permute-done((bf16[64,128]{1,0:T(8,128)(2,1)S(1)}, bf16[64,128]{1,0:T(8,128)(2,1)S(1)}, u32[]{:S(2)}, u32[]{:S(2)}) %collective-permute-start.6) | collective-permute-done | bytes 16416 | tf_op jit(solution)/shard_map/ppermute | solution.py:26
  154.4 1.5 gather_fusion.52
  155.9 1.5 gather_fusion.53
  157.3 1.5 gather_fusion.54
  158.8 1.5 gather_fusion.55
  160.3 1.5 gather_fusion.56
  161.8 1.5 gather_fusion.57
  163.3 1.5 gather_fusion.58
  164.7 1.5 gather_fusion.59
  166.2 1.5 gather_fusion.60
  167.7 1.5 gather_fusion.61
  169.1 1.5 gather_fusion.62
  170.6 1.5 gather_fusion.63
  172.1 1.5 gather_fusion.82
  173.6 1.5 gather_fusion.83
  175.1 5.3 %fusion.42 = f32[256,128]{1,0:T(8,128)S(1)} fusion(f32[256,128]{1,0:T(8,128)} %gather_fusion.83, f32[256,128]{1,0:T(8,128)} %gather_fusion.82, f32[256,128]{1,0:T(8,128)S(1)} %gather_fusion.81, f32[256,128]{1,0:T(8,128)S(1)} %gather_fusion.80, f32[256,128]{1,0:T(8,128)S(1)} %gather_fusion.79, f32[256,128]{1,0:T(8,128)S(1)} %gather_fusion.78, ...), kind=kLoop, calls=%fused_computation.207 | loop fusion | flops 3768320 | bytes 5122316 | tf_op jit(solution)/shard_map/sub | solution.py:84
  188.0 4.5 %collective-permute-start.15 = (bf16[64,128]{1,0:T(8,128)(2,1)S(1)}, bf16[64,128]{1,0:T(8,128)(2,1)S(1)}, u32[]{:S(2)}, u32[]{:S(2)}) collective-permute-start(bf16[64,128]{1,0:T(8,128)(2,1)S(1)} %select_convert_fusion.2), channel_id=1, source_target_pairs={{0,8},{8,16},{16,24},{24,32},{32,40},{40,48},{48,56},{56,64},{64,7... | collective-permute-start | bytes 49160 | tf_op jit(solution)/shard_map/ppermute | solution.py:26
  192.6 8.8 %collective-permute-start.16 = (bf16[64,128]{1,0:T(8,128)(2,1)S(1)}, bf16[64,128]{1,0:T(8,128)(2,1)S(1)}, u32[]{:S(2)}, u32[]{:S(2)}) collective-permute-start(bf16[64,128]{1,0:T(8,128)(2,1)S(1)} %select_convert_fusion.1), channel_id=1, source_target_pairs={{0,16},{8,24},{16,32},{24,40},{32,48},{40,56},{48,64},{56,72},{64,... | collective-permute-start | bytes 49160 | tf_op jit(solution)/shard_map/ppermute | solution.py:26
  201.5 10.8 %collective-permute-start.17 = (bf16[64,128]{1,0:T(8,128)(2,1)S(1)}, bf16[64,128]{1,0:T(8,128)(2,1)S(1)}, u32[]{:S(2)}, u32[]{:S(2)}) collective-permute-start(bf16[64,128]{1,0:T(8,128)(2,1)S(1)} %select_convert_fusion), channel_id=1, source_target_pairs={{0,24},{8,32},{16,40},{24,48},{32,56},{40,64},{48,72},{56,80},{64,... | collective-permute-start | bytes 49160 | tf_op jit(solution)/shard_map/ppermute | solution.py:26
  212.4 1.5 collective-permute-start.12
  214.1 7.5 %collective-permute-done.12 = bf16[64,128]{1,0:T(8,128)(2,1)S(1)} collective-permute-done((bf16[64,128]{1,0:T(8,128)(2,1)S(1)}, bf16[64,128]{1,0:T(8,128)(2,1)S(1)}, u32[]{:S(2)}, u32[]{:S(2)}) %collective-permute-start.12) | collective-permute-done | bytes 16416 | tf_op jit(solution)/shard_map/ppermute | solution.py:26
  239.3 1.5 gather_fusion.94
  240.8 1.5 gather_fusion.95
  242.3 1.5 gather_fusion.96
  243.8 1.5 gather_fusion.97
  245.2 1.5 gather_fusion.98
  246.7 1.5 gather_fusion.99
  248.2 1.5 gather_fusion.100
  249.6 1.5 gather_fusion.101
  251.1 1.5 gather_fusion.102
  252.6 1.5 gather_fusion.103
  254.1 1.5 gather_fusion.104
  255.6 1.5 gather_fusion.105
  257.0 1.5 gather_fusion.124
  258.7 1.5 gather_fusion.125
  260.3 6.2 %fusion.116 = (bf16[256,128]{1,0:T(8,128)(2,1)S(1)}, f32[256,128]{1,0:T(8,128)}) fusion(f32[256,128]{1,0:T(8,128)S(1)} %fusion.80, f32[]{:T(128)S(6)} %mul.533, f32[]{:T(128)S(6)} %div.41, f32[256,128]{1,0:T(8,128)S(1)} %fusion.42, f32[]{:T(128)} %bitcast.43, f32[256,128]{1,0:T(8,128)} %gather_fusion.125, pred[256]{0:T(512)(128)(4,1)} %get-tuple-element.67, ...), kind=kLoop, calls=%fused_computation.501 | loop fusion | flops 3768320 | bytes 5187596 | tf_op jit(solution)/shard_map/convert_element_type | solution.py:90
  266.5 14.1 %all_gather.3 = bf16[256,1024]{1,0:T(8,128)(2,1)S(1)} all-gather(bf16[256,128]{1,0:T(8,128)(2,1)S(1)} %get-tuple-element.4), channel_id=1, replica_groups=mesh['grid'=64,'band'=8] {'band'}, dimensions={1}, use_global_device_ids=true | all-gather | bytes 589824 | tf_op jit(solution)/shard_map/all_gather | solution.py:94
  281.4 40.3 %all_to_all.5 = bf16[64,2,1024]{2,1,0:T(2,128)(2,1)S(1)} all-to-all(bf16[64,2,1024]{2,1,0:T(2,128)(2,1)S(1)} %reshape.38), channel_id=1, replica_groups=mesh['grid'=64,'band'=8] {'grid'}, dimensions={0} | all-to-all | bytes 524288 | tf_op jit(solution)/shard_map/all_to_all | solution.py:36
  (395 shorter events, 111.0 us)
Async XLA Ops:
  1.4 7.1 %copy-start.28 = (pred[64]{0:T(512)(128)(4,1)}, pred[64]{0:T(512)(128)(4,1)S(1)}, u32[]{:S(2)}) copy-start(pred[64]{0:T(512)(128)(4,1)S(1)} %get-tuple-element.54) | copy-start | bytes 196
  1.4 12.4 %copy-start.25 = (pred[64]{0:T(512)(128)(4,1)}, pred[64]{0:T(512)(128)(4,1)S(1)}, u32[]{:S(2)}) copy-start(pred[64]{0:T(512)(128)(4,1)S(1)} %get-tuple-element.62) | copy-start | bytes 196
  1.4 19.2 %copy-start.22 = (pred[64]{0:T(512)(128)(4,1)}, pred[64]{0:T(512)(128)(4,1)S(1)}, u32[]{:S(2)}) copy-start(pred[64]{0:T(512)(128)(4,1)S(1)} %get-tuple-element.6) | copy-start | bytes 196
  1.4 41.8 %copy-start.19 = (pred[64]{0:T(512)(128)(4,1)}, pred[64]{0:T(512)(128)(4,1)S(1)}, u32[]{:S(2)}) copy-start(pred[64]{0:T(512)(128)(4,1)S(1)} %get-tuple-element.60) | copy-start | bytes 196
  4.5 38.8 %collective-permute-start.1 = (bf16[64,128]{1,0:T(8,128)(2,1)S(1)}, bf16[64,128]{1,0:T(8,128)(2,1)S(1)}, u32[]{:S(2)}, u32[]{:S(2)}) collective-permute-start(bf16[64,128]{1,0:T(8,128)(2,1)S(1)} %select_convert_fusion.16), channel_id=1, source_target_pairs={{16,0},{24,8},{32,16},{40,24},{48,32},{56,40},{64,48},{72,56},{80,... | collective-permute-start | bytes 49160 | tf_op jit(solution)/shard_map/ppermute | solution.py:26
  6.5 41.7 %collective-permute-start.2 = (bf16[64,128]{1,0:T(8,128)(2,1)S(1)}, bf16[64,128]{1,0:T(8,128)(2,1)S(1)}, u32[]{:S(2)}, u32[]{:S(2)}) collective-permute-start(bf16[64,128]{1,0:T(8,128)(2,1)S(1)} %select_convert_fusion.15), channel_id=1, source_target_pairs={{8,0},{16,8},{24,16},{32,24},{40,32},{48,40},{56,48},{64,56},{72,6... | collective-permute-start | bytes 49160 | tf_op jit(solution)/shard_map/ppermute | solution.py:26
  8.6 39.7 %collective-permute-start.3 = (bf16[64,128]{1,0:T(8,128)(2,1)S(1)}, bf16[64,128]{1,0:T(8,128)(2,1)S(1)}, u32[]{:S(2)}, u32[]{:S(2)}) collective-permute-start(bf16[64,128]{1,0:T(8,128)(2,1)S(1)} %select_convert_fusion.14), channel_id=1, source_target_pairs={{0,8},{8,16},{16,24},{24,32},{32,40},{40,48},{48,56},{56,64},{64,7... | collective-permute-start | bytes 49160 | tf_op jit(solution)/shard_map/ppermute | solution.py:26
  13.9 34.4 %collective-permute-start.4 = (bf16[64,128]{1,0:T(8,128)(2,1)S(1)}, bf16[64,128]{1,0:T(8,128)(2,1)S(1)}, u32[]{:S(2)}, u32[]{:S(2)}) collective-permute-start(bf16[64,128]{1,0:T(8,128)(2,1)S(1)} %select_convert_fusion.13), channel_id=1, source_target_pairs={{0,16},{8,24},{16,32},{24,40},{32,48},{40,56},{48,64},{56,72},{64,... | collective-permute-start | bytes 49160 | tf_op jit(solution)/shard_map/ppermute | solution.py:26
  20.0 10.1 %copy-start.1 = (s32[36,256]{1,0:T(8,128)S(1)}, s32[36,256]{1,0:T(8,128)}, u32[]{:S(2)}) copy-start(s32[36,256]{1,0:T(8,128)} %param.15) | copy-start | bytes 110596
  20.8 27.5 %collective-permute-start.5 = (bf16[64,128]{1,0:T(8,128)(2,1)S(1)}, bf16[64,128]{1,0:T(8,128)(2,1)S(1)}, u32[]{:S(2)}, u32[]{:S(2)}) collective-permute-start(bf16[64,128]{1,0:T(8,128)(2,1)S(1)} %select_convert_fusion.12), channel_id=1, source_target_pairs={{0,24},{8,32},{16,40},{24,48},{32,56},{40,64},{48,72},{56,80},{64,... | collective-permute-start | bytes 49160 | tf_op jit(solution)/shard_map/ppermute | solution.py:26
  41.6 24.8 %copy-start.2 = (s32[1024]{0:T(1024)}, s32[1024]{0:T(1024)S(1)}, u32[]{:S(2)}) copy-start(s32[1024]{0:T(1024)S(1)} %pad_clamp_fusion.2) | copy-start | bytes 12292
  41.6 25.5 %copy-start.3 = (s32[1024]{0:T(1024)}, s32[1024]{0:T(1024)S(1)}, u32[]{:S(2)}) copy-start(s32[1024]{0:T(1024)S(1)} %pad_clamp_fusion.34) | copy-start | bytes 12292
  41.6 26.2 %copy-start.4 = (s32[1024]{0:T(1024)}, s32[1024]{0:T(1024)S(1)}, u32[]{:S(2)}) copy-start(s32[1024]{0:T(1024)S(1)} %pad_clamp_fusion.33) | copy-start | bytes 12292
  41.7 26.9 %copy-start.5 = (s32[1024]{0:T(1024)}, s32[1024]{0:T(1024)S(1)}, u32[]{:S(2)}) copy-start(s32[1024]{0:T(1024)S(1)} %pad_clamp_fusion.32) | copy-start | bytes 12292
  41.7 27.6 %copy-start.6 = (s32[1024]{0:T(1024)}, s32[1024]{0:T(1024)S(1)}, u32[]{:S(2)}) copy-start(s32[1024]{0:T(1024)S(1)} %pad_clamp_fusion.31) | copy-start | bytes 12292
  41.7 28.9 %copy-start.7 = (s32[1024]{0:T(1024)}, s32[1024]{0:T(1024)S(1)}, u32[]{:S(2)}) copy-start(s32[1024]{0:T(1024)S(1)} %pad_clamp_fusion.30) | copy-start | bytes 12292
  41.7 30.3 %copy-start.8 = (s32[1024]{0:T(1024)}, s32[1024]{0:T(1024)S(1)}, u32[]{:S(2)}) copy-start(s32[1024]{0:T(1024)S(1)} %pad_clamp_fusion.29) | copy-start | bytes 12292
  41.8 31.6 %copy-start.9 = (s32[1024]{0:T(1024)}, s32[1024]{0:T(1024)S(1)}, u32[]{:S(2)}) copy-start(s32[1024]{0:T(1024)S(1)} %pad_clamp_fusion.28) | copy-start | bytes 12292
  41.8 32.9 %copy-start.10 = (s32[1024]{0:T(1024)}, s32[1024]{0:T(1024)S(1)}, u32[]{:S(2)}) copy-start(s32[1024]{0:T(1024)S(1)} %pad_clamp_fusion.27) | copy-start | bytes 12292
  41.8 34.2 %copy-start.11 = (s32[1024]{0:T(1024)}, s32[1024]{0:T(1024)S(1)}, u32[]{:S(2)}) copy-start(s32[1024]{0:T(1024)S(1)} %pad_clamp_fusion.26) | copy-start | bytes 12292
  41.8 35.6 %copy-start.12 = (s32[1024]{0:T(1024)}, s32[1024]{0:T(1024)S(1)}, u32[]{:S(2)}) copy-start(s32[1024]{0:T(1024)S(1)} %pad_clamp_fusion.25) | copy-start | bytes 12292
  41.9 36.9 %copy-start.13 = (s32[1024]{0:T(1024)}, s32[1024]{0:T(1024)S(1)}, u32[]{:S(2)}) copy-start(s32[1024]{0:T(1024)S(1)} %pad_clamp_fusion.24) | copy-start | bytes 12292
  41.9 38.2 %copy-start.14 = (s32[1024]{0:T(1024)}, s32[1024]{0:T(1024)S(1)}, u32[]{:S(2)}) copy-start(s32[1024]{0:T(1024)S(1)} %pad_clamp_fusion.23) | copy-start | bytes 12292
  41.9 39.5 %copy-start.15 = (s32[1024]{0:T(1024)}, s32[1024]{0:T(1024)S(1)}, u32[]{:S(2)}) copy-start(s32[1024]{0:T(1024)S(1)} %pad_clamp_fusion.22) | copy-start | bytes 12292
  41.9 40.8 %copy-start.16 = (s32[1024]{0:T(1024)}, s32[1024]{0:T(1024)S(1)}, u32[]{:S(2)}) copy-start(s32[1024]{0:T(1024)S(1)} %pad_clamp_fusion.21) | copy-start | bytes 12292
  42.5 41.6 %copy-start.17 = (s32[1024]{0:T(1024)}, s32[1024]{0:T(1024)S(1)}, u32[]{:S(2)}) copy-start(s32[1024]{0:T(1024)S(1)} %pad_clamp_fusion.20) | copy-start | bytes 12292
  43.3 42.2 %copy-start.18 = (s32[1024]{0:T(1024)}, s32[1024]{0:T(1024)S(1)}, u32[]{:S(2)}) copy-start(s32[1024]{0:T(1024)S(1)} %pad_clamp_fusion.1) | copy-start | bytes 12292
  43.3 8.8 %collective-permute-start = (bf16[64,128]{1,0:T(8,128)(2,1)S(1)}, bf16[64,128]{1,0:T(8,128)(2,1)S(1)}, u32[]{:S(2)}, u32[]{:S(2)}) collective-permute-start(bf16[64,128]{1,0:T(8,128)(2,1)S(1)} %select_convert_fusion.17), channel_id=1, source_target_pairs={{24,0},{32,8},{40,16},{48,24},{56,32},{64,40},{72,48},{80,56},{88,... | collective-permute-start | bytes 49160 | tf_op jit(solution)/shard_map/ppermute | solution.py:26
  99.0 10.0 %copy-start.23 = (pred[64]{0:T(512)(128)(4,1)S(1)}, pred[64]{0:T(512)(128)(4,1)}, u32[]{:S(2)}) copy-start(pred[64]{0:T(512)(128)(4,1)} %copy-done.22) | copy-start | bytes 196
  99.1 14.6 %copy-start.35 = (pred[64]{0:T(512)(128)(4,1)S(1)}, pred[64]{0:T(512)(128)(4,1)}, u32[]{:S(2)}) copy-start(pred[64]{0:T(512)(128)(4,1)} %copy-done.34) | copy-start | bytes 196
  99.1 22.6 %collective-permute-start.10 = (bf16[64,128]{1,0:T(8,128)(2,1)S(1)}, bf16[64,128]{1,0:T(8,128)(2,1)S(1)}, u32[]{:S(2)}, u32[]{:S(2)}) collective-permute-start(bf16[64,128]{1,0:T(8,128)(2,1)S(1)} %select_convert_fusion.7), channel_id=1, source_target_pairs={{0,16},{8,24},{16,32},{24,40},{32,48},{40,56},{48,64},{56,72},{64,... | collective-permute-start | bytes 49160 | tf_op jit(solution)/shard_map/ppermute | solution.py:26
  109.1 14.2 %collective-permute-start.11 = (bf16[64,128]{1,0:T(8,128)(2,1)S(1)}, bf16[64,128]{1,0:T(8,128)(2,1)S(1)}, u32[]{:S(2)}, u32[]{:S(2)}) collective-permute-start(bf16[64,128]{1,0:T(8,128)(2,1)S(1)} %select_convert_fusion.6), channel_id=1, source_target_pairs={{0,24},{8,32},{16,40},{24,48},{32,56},{40,64},{48,72},{56,80},{64,... | collective-permute-start | bytes 49160 | tf_op jit(solution)/shard_map/ppermute | solution.py:26
  113.8 9.6 %collective-permute-start.7 = (bf16[64,128]{1,0:T(8,128)(2,1)S(1)}, bf16[64,128]{1,0:T(8,128)(2,1)S(1)}, u32[]{:S(2)}, u32[]{:S(2)}) collective-permute-start(bf16[64,128]{1,0:T(8,128)(2,1)S(1)} %select_convert_fusion.10), channel_id=1, source_target_pairs={{16,0},{24,8},{32,16},{40,24},{48,32},{56,40},{64,48},{72,56},{80,... | collective-permute-start | bytes 49160 | tf_op jit(solution)/shard_map/ppermute | solution.py:26
  115.2 6.5 %copy-start.20 = (pred[64]{0:T(512)(128)(4,1)S(1)}, pred[64]{0:T(512)(128)(4,1)}, u32[]{:S(2)}) copy-start(pred[64]{0:T(512)(128)(4,1)} %copy-done.19) | copy-start | bytes 196
  115.2 8.2 %collective-permute-start.8 = (bf16[64,128]{1,0:T(8,128)(2,1)S(1)}, bf16[64,128]{1,0:T(8,128)(2,1)S(1)}, u32[]{:S(2)}, u32[]{:S(2)}) collective-permute-start(bf16[64,128]{1,0:T(8,128)(2,1)S(1)} %select_convert_fusion.9), channel_id=1, source_target_pairs={{8,0},{16,8},{24,16},{32,24},{40,32},{48,40},{56,48},{64,56},{72,6... | collective-permute-start | bytes 49160 | tf_op jit(solution)/shard_map/ppermute | solution.py:26
  116.6 6.9 %collective-permute-start.9 = (bf16[64,128]{1,0:T(8,128)(2,1)S(1)}, bf16[64,128]{1,0:T(8,128)(2,1)S(1)}, u32[]{:S(2)}, u32[]{:S(2)}) collective-permute-start(bf16[64,128]{1,0:T(8,128)(2,1)S(1)} %select_convert_fusion.8), channel_id=1, source_target_pairs={{0,8},{8,16},{16,24},{24,32},{32,40},{40,48},{48,56},{56,64},{64,7... | collective-permute-start | bytes 49160 | tf_op jit(solution)/shard_map/ppermute | solution.py:26
  121.7 14.9 %collective-permute-start.6 = (bf16[64,128]{1,0:T(8,128)(2,1)S(1)}, bf16[64,128]{1,0:T(8,128)(2,1)S(1)}, u32[]{:S(2)}, u32[]{:S(2)}) collective-permute-start(bf16[64,128]{1,0:T(8,128)(2,1)S(1)} %select_convert_fusion.11), channel_id=1, source_target_pairs={{24,0},{32,8},{40,16},{48,24},{56,32},{64,40},{72,48},{80,56},{88,... | collective-permute-start | bytes 49160 | tf_op jit(solution)/shard_map/ppermute | solution.py:26
  123.3 13.3 %copy-start.66 = (f32[1,128]{1,0:T(1,128)S(1)}, f32[1,128]{1,0:T(1,128)}, u32[]{:S(2)}) copy-start(f32[1,128]{1,0:T(1,128)} %copy-done.65) | copy-start | bytes 1540
  185.2 27.2 %collective-permute-start.13 = (bf16[64,128]{1,0:T(8,128)(2,1)S(1)}, bf16[64,128]{1,0:T(8,128)(2,1)S(1)}, u32[]{:S(2)}, u32[]{:S(2)}) collective-permute-start(bf16[64,128]{1,0:T(8,128)(2,1)S(1)} %select_convert_fusion.4), channel_id=1, source_target_pairs={{16,0},{24,8},{32,16},{40,24},{48,32},{56,40},{64,48},{72,56},{80,... | collective-permute-start | bytes 49160 | tf_op jit(solution)/shard_map/ppermute | solution.py:26
  186.6 6.0 %copy-start.27 = (pred[64]{0:T(512)(128)(4,1)S(1)}, pred[64]{0:T(512)(128)(4,1)}, u32[]{:S(2)}) copy-start(pred[64]{0:T(512)(128)(4,1)} %copy-done.25) | copy-start | bytes 196
  186.6 27.4 %collective-permute-start.14 = (bf16[64,128]{1,0:T(8,128)(2,1)S(1)}, bf16[64,128]{1,0:T(8,128)(2,1)S(1)}, u32[]{:S(2)}, u32[]{:S(2)}) collective-permute-start(bf16[64,128]{1,0:T(8,128)(2,1)S(1)} %select_convert_fusion.3), channel_id=1, source_target_pairs={{8,0},{16,8},{24,16},{32,24},{40,32},{48,40},{56,48},{64,56},{72,6... | collective-permute-start | bytes 49160 | tf_op jit(solution)/shard_map/ppermute | solution.py:26
  188.0 13.5 %copy-start.24 = (pred[64]{0:T(512)(128)(4,1)S(1)}, pred[64]{0:T(512)(128)(4,1)}, u32[]{:S(2)}) copy-start(pred[64]{0:T(512)(128)(4,1)} %copy-done.22) | copy-start | bytes 196
  188.0 26.1 %collective-permute-start.15 = (bf16[64,128]{1,0:T(8,128)(2,1)S(1)}, bf16[64,128]{1,0:T(8,128)(2,1)S(1)}, u32[]{:S(2)}, u32[]{:S(2)}) collective-permute-start(bf16[64,128]{1,0:T(8,128)(2,1)S(1)} %select_convert_fusion.2), channel_id=1, source_target_pairs={{0,8},{8,16},{16,24},{24,32},{32,40},{40,48},{48,56},{56,64},{64,7... | collective-permute-start | bytes 49160 | tf_op jit(solution)/shard_map/ppermute | solution.py:26
  192.6 19.7 %copy-start.21 = (pred[64]{0:T(512)(128)(4,1)S(1)}, pred[64]{0:T(512)(128)(4,1)}, u32[]{:S(2)}) copy-start(pred[64]{0:T(512)(128)(4,1)} %copy-done.19) | copy-start | bytes 196
  192.6 21.4 %collective-permute-start.16 = (bf16[64,128]{1,0:T(8,128)(2,1)S(1)}, bf16[64,128]{1,0:T(8,128)(2,1)S(1)}, u32[]{:S(2)}, u32[]{:S(2)}) collective-permute-start(bf16[64,128]{1,0:T(8,128)(2,1)S(1)} %select_convert_fusion.1), channel_id=1, source_target_pairs={{0,16},{8,24},{16,32},{24,40},{32,48},{40,56},{48,64},{56,72},{64,... | collective-permute-start | bytes 49160 | tf_op jit(solution)/shard_map/ppermute | solution.py:26
  201.5 12.5 %collective-permute-start.17 = (bf16[64,128]{1,0:T(8,128)(2,1)S(1)}, bf16[64,128]{1,0:T(8,128)(2,1)S(1)}, u32[]{:S(2)}, u32[]{:S(2)}) collective-permute-start(bf16[64,128]{1,0:T(8,128)(2,1)S(1)} %select_convert_fusion), channel_id=1, source_target_pairs={{0,24},{8,32},{16,40},{24,48},{32,56},{40,64},{48,72},{56,80},{64,... | collective-permute-start | bytes 49160 | tf_op jit(solution)/shard_map/ppermute | solution.py:26
  212.4 9.2 %collective-permute-start.12 = (bf16[64,128]{1,0:T(8,128)(2,1)S(1)}, bf16[64,128]{1,0:T(8,128)(2,1)S(1)}, u32[]{:S(2)}, u32[]{:S(2)}) collective-permute-start(bf16[64,128]{1,0:T(8,128)(2,1)S(1)} %select_convert_fusion.5), channel_id=1, source_target_pairs={{24,0},{32,8},{40,16},{48,24},{56,32},{64,40},{72,48},{80,56},{88,... | collective-permute-start | bytes 49160 | tf_op jit(solution)/shard_map/ppermute | solution.py:26
  214.0 7.6 %copy-start.67 = (f32[1,128]{1,0:T(1,128)S(1)}, f32[1,128]{1,0:T(1,128)}, u32[]{:S(2)}) copy-start(f32[1,128]{1,0:T(1,128)} %copy-done.65) | copy-start | bytes 1540
  (40 other events, 64.4 us)
where the time goes:
time: 325 us; the launch traced here: 323 us
  local copies, waits for them, and re-layouts  129 us (40%)
  starting transfers between devices  75.7 us (23%)
  blocking collectives  54.3 us (17%)
  other arithmetic  32 us (10%)
  waiting for transfers between devices  24.6 us (8%)
  between operations  6.19 us (2%)
    gather x108, local copies, waits for them, and re-layouts, apply_stencil(): jnp.take(extended, local_table[neighbour], axis=0)  110 us
    ppermute x18, starting transfers between devices, passed_along(): return lax.ppermute(block, axis, route)  75.7 us
    all_to_all x1, blocking collectives, sum_at_owner(): lax.all_to_all(in_blocks(shard, dim, peers), axis, 0, 0, tiled=True)  40.3 us
    ppermute x18, waiting for transfers between devices, passed_along(): return lax.ppermute(block, axis, route)  24.6 us
    all_gather x1, blocking collectives, on_device(): every_band = lax.all_gather(rounded, 'band', axis=1, tiled=True)  14.1 us
    gather x18, local copies, waits for them, and re-layouts, boundary_blocks(): outgoing = jnp.take(own_rows, send_rows[0, slot_index], axis=0)  13.2 us
    and x18, other arithmetic, apply_stencil(): jnp.take(extended, local_table[neighbour], axis=0)  10.3 us
  transfers between devices with their start and end apart: 18, of which 3 were waited for; matrix products, arithmetic and copies ran while one was open for 5% of the time, Pallas kernels for 0%

commit v1 on v0

v1 whole, which is shorter than its diff:
```python
import functools

import jax
import jax.numpy as jnp
from jax import lax
from jax.experimental import pallas as pl
from jax.experimental.pallas import tpu as pltpu
from jax.sharding import PartitionSpec as P

SPAN = 6
DEGREE = 3
REACH = 3
GROUP = 8

DIFFERENCE_WEIGHTS = (
    -5369.0 / 1800.0,
    12.0 / 7.0,
    -15.0 / 56.0,
    10.0 / 189.0,
    -1.0 / 112.0,
    2.0 / 1925.0,
    -1.0 / 16632.0,
)
KINETIC_SCALE = 0.5 / 0.49
CENTRE_WEIGHT = -3.0 * KINETIC_SCALE * DIFFERENCE_WEIGHTS[0]
TILE = 128
BF16 = jnp.bfloat16
F32 = jnp.float32
VMEM = pl.BlockSpec(memory_space=pltpu.VMEM)
SMEM = pl.BlockSpec(memory_space=pltpu.SMEM)


def dot(a, b):
    return jnp.dot(a, b, preferred_element_type=F32)


def split(values):
    high = values.astype(BF16)
    return high, (values - high.astype(F32)).astype(BF16)


def select_rows(select_ref, sends_ref, first, blocks, rows):
    for pair in range((blocks + 1) // 2):
        picks = sends_ref[pl.ds(first + 2 * pair, 1), :]
        height = min(TILE, 64 * (blocks - 2 * pair))
        for at in range(0, rows, TILE):
            here = lax.broadcasted_iota(jnp.int32, (TILE, TILE), 0) + at
            hit = jnp.where(here == picks, 1.0, 0.0)
            select_ref[pl.ds(pair * TILE, height), pl.ds(at, TILE)] = jnp.transpose(hit)[:height].astype(BF16)


def begin_kernel(place_ref, count_ref, sends_ref, states_ref, start_ref, own_ref, cross_ref, crossing_ref):
    place = place_ref[0]
    rows = states_ref.shape[0]
    live = lax.broadcasted_iota(jnp.int32, states_ref.shape, 0) < count_ref[0]
    start = jnp.where(live, states_ref[...], 0.0)
    start_ref[...] = start
    first = jnp.where(place >= 5, 15 - place, jnp.maximum(4 - place, 0))
    select_rows(cross_ref, sends_ref, first, REACH, rows)
    crossing_ref[...] = dot(cross_ref[...], start.astype(BF16)).astype(BF16)
    select_rows(own_ref, sends_ref, 7 - place, GROUP, rows)


def local_part(fields, high_ref, low_ref, own_ref, part_ref, outgoing_ref):
    high, low = split(fields)
    part_ref[...] = dot(high_ref[...], high) + dot(low_ref[...], high) + dot(high_ref[...], low)
    outgoing_ref[...] = dot(own_ref[...], high).astype(BF16)


def build_kernel(
    place_ref, bounds_ref, potential_ref, table_ref, start_ref, own_ref,
    high_ref, low_ref, halo_high_ref, halo_low_ref, part_ref, outgoing_ref, halo_table
):
    place = place_ref[0]
    rows = start_ref.shape[0]
    stencil = table_ref.shape[0]
    middle = (bounds_ref[2] + bounds_ref[1]) / 2.0
    table = table_ref[...]
    slot = jnp.right_shift(table - (rows + 1), 6)
    offset = slot - jnp.where(slot < REACH, REACH, REACH - 1)
    source = jnp.bitwise_and(place - offset, GROUP - 1)
    halo = source * 64 + jnp.bitwise_and(table - (rows + 1), 63)
    halo_table[...] = jnp.where(table > rows, halo, -1)

    def gathered(names_ref, column, row):
        here = lax.broadcasted_iota(jnp.int32, (TILE, TILE), 0) + column
        total = jnp.zeros((TILE, TILE), F32)
        for neighbour in range(stencil):
            weight = -KINETIC_SCALE * DIFFERENCE_WEIGHTS[neighbour % SPAN + 1]
            names = names_ref[neighbour : neighbour + 1, row : row + TILE]
            total = total + jnp.where(here == names, weight, 0.0)
        return total, here

    for row in range(0, rows, TILE):
        diagonal = potential_ref[:, row : row + TILE] + (CENTRE_WEIGHT - middle)

        @pl.loop(0, rows // TILE)
        def _(block, row=row, diagonal=diagonal):
            column = pl.multiple_of(block * TILE, TILE)
            total, here = gathered(table_ref, column, row)
            right = lax.broadcasted_iota(jnp.int32, (TILE, TILE), 1) + row
            total = total + jnp.where(here == right, diagonal, 0.0)
            high, low = split(jnp.transpose(total))
            high_ref[pl.ds(row, TILE), pl.ds(column, TILE)] = high
            low_ref[pl.ds(row, TILE), pl.ds(column, TILE)] = low

    @pl.loop(0, GROUP * 64 // TILE)
    def _(block):
        column = pl.multiple_of(block * TILE, TILE)
        total, _ = gathered(halo_table, column, rows - TILE)
        high, low = split(jnp.transpose(total))
        halo_high_ref[:, pl.ds(column, TILE)] = high
        halo_low_ref[:, pl.ds(column, TILE)] = low

    local_part(start_ref[...], high_ref, low_ref, own_ref, part_ref, outgoing_ref)


def local_kernel(fields_ref, high_ref, low_ref, own_ref, part_ref, outgoing_ref):
    local_part(fields_ref[...], high_ref, low_ref, own_ref, part_ref, outgoing_ref)


def update_kernel(degree, bounds_ref, part_ref, halo_ref, halo_high_ref, halo_low_ref, *rest):
    refs = list(rest)
    before_ref = refs.pop(0) if degree > 0 else None
    cross_ref = refs.pop(0) if degree < DEGREE - 1 else None
    fields_ref, extra_ref = refs
    spread = lambda at: jnp.full((8, TILE), bounds_ref[at], F32)
    lower, cutoff, upper = spread(0), spread(1), spread(2)
    half = (upper - cutoff) / 2.0
    middle = (upper + cutoff) / 2.0
    sigma = half / (lower - middle)
    twice = 2.0 / sigma
    scale, carried = sigma / half, None
    for _ in range(degree):
        following = 1.0 / (twice - sigma)
        scale, carried = 2.0 * following / half, sigma * following
        sigma = following
    rows = part_ref.shape[0]
    halo = halo_ref[...]
    reached = dot(halo_high_ref[...], halo) + dot(halo_low_ref[...], halo)
    for at in range(0, rows, TILE):
        image = part_ref[pl.ds(at, TILE), :]
        if at == rows - TILE:
            image = image + reached
        image = image * scale[:1]
        if degree > 0:
            image = image - carried[:1] * before_ref[pl.ds(at, TILE), :]
        fields_ref[pl.ds(at, TILE), :] = image
        if degree == DEGREE - 1:
            extra_ref[pl.ds(at, TILE), :] = image.astype(BF16)
    if degree < DEGREE - 1:
        extra_ref[...] = dot(cross_ref[...], fields_ref[...].astype(BF16)).astype(BF16)


def margin_kernel(band_ref, every_ref, partial_ref):
    bands, _, width = every_ref.shape
    wanted = 2 * bands
    row = lax.broadcasted_iota(jnp.int32, (wanted, width), 0)
    column = lax.broadcasted_iota(jnp.int32, (wanted, width), 1)
    target = jnp.right_shift(row, 1) * wanted + 2 * band_ref[0] + jnp.bitwise_and(row, 1)
    pick = jnp.where(column == target, 1.0, 0.0).astype(BF16)
    chosen = [
        lax.dot_general(pick, every_ref[band], (((1,), (1,)), ((), ())), preferred_element_type=F32).astype(BF16)
        for band in range(bands)
    ]
    chosen = jnp.concatenate(chosen, axis=0)
    for band in range(bands):
        partial_ref[:, pl.ds(band * width, width)] = dot(chosen, every_ref[band]).astype(BF16)


def call(kernel, operands, specs, outs, flops, scratch=()):
    moved = sum(x.size * x.dtype.itemsize for x in (*operands, *outs))
    return pl.pallas_call(
        kernel,
        out_shape=tuple(outs),
        in_specs=specs,
        out_specs=tuple(VMEM for _ in outs),
        scratch_shapes=list(scratch),
        compiler_params=pltpu.CompilerParams(vmem_limit_bytes=16 * 1024 * 1024),
        cost_estimate=pl.CostEstimate(flops=flops, bytes_accessed=moved, transcendentals=0),
    )(*operands)


def shape(dims, dtype=F32):
    return jax.ShapeDtypeStruct(dims, dtype)


def across(crossing, parts):
    route = []
    for at in range(parts):
        place = at % GROUP
        if place >= 5 and at + GROUP < parts:
            route.append((at, at + GROUP))
        if place <= 2 and at >= GROUP:
            route.append((at, at - GROUP))
    return lax.ppermute(crossing, "grid", route)


def exchanged(outgoing, relayed, place, parts):
    zeros = jnp.zeros_like(relayed)
    down = jnp.where(place >= 5, relayed, zeros)
    up = jnp.where(place <= 2, relayed, zeros)
    gap = jnp.zeros((outgoing.shape[0] - 2 * relayed.shape[0], relayed.shape[1]), BF16)
    message = (outgoing + jnp.concatenate([down, gap, up], axis=0)).reshape(GROUP, -1, outgoing.shape[1])
    groups = [list(range(first, first + GROUP)) for first in range(0, parts, GROUP)]
    received = lax.all_to_all(message, "grid", 0, 0, axis_index_groups=groups, tiled=True)
    return received.reshape(outgoing.shape)


def on_device(states, potential, bounds, point_count, send_rows, stencil_table):
    rows, width = states.shape
    stencil = stencil_table.shape[0]
    parts = lax.axis_size("grid")
    bands = lax.axis_size("band")
    slots = GROUP * 64
    place = lax.rem(lax.axis_index("grid"), GROUP).reshape(1)
    none = jnp.full((4, 64), rows, jnp.int32)
    lined = jnp.concatenate([none, send_rows[0, :REACH], none[:1], send_rows[0, REACH:], none, none[:1]], axis=0)
    paired = jnp.concatenate([lined, jnp.concatenate([lined[1:], none[:1]], axis=0)], axis=1)

    start, own, cross, crossing = call(
        begin_kernel,
        (place, point_count, paired, states),
        [SMEM, SMEM, VMEM, VMEM],
        [shape((rows, width)), shape((slots, rows), BF16), shape((REACH * 64, rows), BF16), shape((REACH * 64, width), BF16)],
        10_000_000,
    )
    relayed = across(crossing, parts)
    high, low, halo_high, halo_low, part, outgoing = call(
        build_kernel,
        (place, bounds, potential.reshape(1, rows), stencil_table, start, own),
        [SMEM, SMEM, VMEM, VMEM, VMEM, VMEM],
        [
            shape((rows, rows), BF16),
            shape((rows, rows), BF16),
            shape((TILE, slots), BF16),
            shape((TILE, slots), BF16),
            shape((rows, width)),
            shape((slots, width), BF16),
        ],
        50_000_000,
        [pltpu.VMEM((stencil, rows), jnp.int32)],
    )
    before, fields = None, start
    for degree in range(DEGREE):
        if degree > 0:
            relayed = across(extra, parts)
            part, outgoing = call(
                local_kernel,
                (fields, high, low, own),
                [VMEM] * 4,
                [shape((rows, width)), shape((slots, width), BF16)],
                80_000_000,
            )
        halo = exchanged(outgoing, relayed, place[0], parts)
        operands = [bounds, part, halo, halo_high, halo_low]
        if degree > 0:
            operands.append(before)
        if degree < DEGREE - 1:
            operands.append(cross)
            after = shape((REACH * 64, width), BF16)
        else:
            after = shape((rows, width), BF16)
        before = fields
        fields, extra = call(
            functools.partial(update_kernel, degree),
            operands,
            [SMEM] + [VMEM] * (len(operands) - 1),
            [shape((rows, width)), after],
            40_000_000,
        )
    every_band = lax.all_gather(extra, "band", axis=0)
    (partial_sums,) = call(
        margin_kernel,
        (lax.axis_index("band").reshape(1), every_band),
        [SMEM, VMEM],
        [shape((2 * parts, bands * width), BF16)],
        80_000_000,
    )
    blocks = lax.all_to_all(partial_sums.reshape(parts, 2, bands * width), "grid", 0, 0, tiled=True)
    summed = jnp.sum(blocks.astype(F32), axis=0)
    return fields, summed * (1.0 / (parts * rows))


def solution(mesh):
    placed = (P("grid", "band"), P("grid"), P(), P("grid"), P("grid", None, None), P(None, "grid"))
    return jax.shard_map(
        on_device,
        mesh=mesh,
        in_specs=placed,
        out_specs=(P("grid", "band"), P(("grid", "band"), None)),
        check_vma=False,
    )
```

time: 325 us -> 120 us (0.37)
  local copies, waits for them, and re-layouts: 129 us -> 1.86 us
  starting transfers between devices: 75.7 us -> 7.25 us
  other arithmetic: 32 us -> 2.03 us
  blocking collectives: 54.3 us -> 78.5 us
  Pallas kernels: 0 us -> 8.06 us
  between operations: 6.19 us -> 1.45 us
  waiting for transfers between devices: 24.6 us -> 20.7 us
    gather x126 -> x0, local copies, waits for them, and re-layouts: 123 us -> none  [the longest x108 110 us: apply_stencil(): jnp.take(extended, local_table[neighbour], axis=0)]
    ppermute x18 -> x3, starting transfers between devices: 75.7 us -> 3.88 us  [across(): return lax.ppermute(crossing, 'grid', route)]
    all_to_all x1 -> x3, blocking collectives: 40.3 us -> 64.4 us  [the longest x2 33.7 us: exchanged(): lax.all_to_all(message, 'grid', 0, 0, axis_index_groups=groups, tiled=True)]
    ppermute x18 -> x3, waiting for transfers between devices: 24.6 us -> 10.2 us  [across(): return lax.ppermute(crossing, 'grid', route)]
    and x19 -> x0, other arithmetic: 11.1 us -> none  [the longest x18 10.3 us: apply_stencil(): jnp.take(extended, local_table[neighbour], axis=0)]
    all_to_all x0 -> x1, waiting for transfers between devices: none -> 10.4 us  [exchanged(): lax.all_to_all(message, 'grid', 0, 0, axis_index_groups=groups, tiled=True)]
    pallas_call x0 -> x8, Pallas kernels: none -> 8.06 us  [call(): pl.pallas_call(kernel, out_shape=tuple(outs), in_specs=specs, out_specs=t...]
    convert_element_type x19 -> x0, other arithmetic: 7.54 us -> none  [the longest x1 6.18 us: on_device(): rounded = current.astype(jnp.bfloat16)]
  transfers between devices with their start and end apart: 18 -> 4, of which waited for: 3 -> 4; matrix products, arithmetic and copies ran while one was open for 5% -> 0% of each run, Pallas kernels for 0% -> 3%
where the time goes in v1:
time: 120 us
  blocking collectives  78.5 us (65%)
  waiting for transfers between devices  20.7 us (17%)
  Pallas kernels  8.06 us (7%)
  starting transfers between devices  7.25 us (6%)
  other arithmetic  2.03 us (2%)
  local copies, waits for them, and re-layouts  1.86 us (2%)
  between operations  1.45 us (1%)
    all_to_all x2, blocking collectives, exchanged(): lax.all_to_all(message, 'grid', 0, 0, axis_index_groups=groups, tiled=True)  33.7 us
    all_to_all x1, blocking collectives, on_device(): lax.all_to_all(partial_sums.reshape(parts, 2, bands * width), 'grid', 0,...  30.7 us
    all_gather x1, blocking collectives, on_device(): every_band = lax.all_gather(extra, 'band', axis=0)  14.1 us
    all_to_all x1, waiting for transfers between devices, exchanged(): lax.all_to_all(message, 'grid', 0, 0, axis_index_groups=groups, tiled=True)  10.4 us
    ppermute x3, waiting for transfers between devices, across(): return lax.ppermute(crossing, 'grid', route)  10.2 us
    pallas_call x8, Pallas kernels, call(): pl.pallas_call(kernel, out_shape=tuple(outs), in_specs=specs, out_specs=t...  8.06 us
    ppermute x3, starting transfers between devices, across(): return lax.ppermute(crossing, 'grid', route)  3.88 us
    all_to_all x1, starting transfers between devices, exchanged(): lax.all_to_all(message, 'grid', 0, 0, axis_index_groups=groups, tiled=True)  3.37 us
  transfers between devices with their start and end apart: 4, of which 4 were waited for; matrix products, arithmetic and copies ran while one was open for 0% of the time, Pallas kernels for 3%

profile of v1, /device:TPU:16, one launch (start us, length us, event | category | flops | bytes accessed | tf_op | source)
XLA Modules:
  0.0 119.8 jit_solution(13715110845316614094)
XLA Ops:
  0.6 0.0 copy-start.4
  1.3 0.0 copy-done.4
  1.4 0.1 select_add_fusion.sends_ref
  1.5 0.0 copy-start
  1.5 0.9 copy-done
  2.4 0.0 copy-start.1
  2.4 0.3 shard_map.77
  2.7 1.3 %collective-permute-start = (bf16[192,128]{1,0:T(8,128)(2,1)S(1)}, bf16[192,128]{1,0:T(8,128)(2,1)S(1)}, u32[]{:S(2)}, u32[]{:S(2)}) collective-permute-start(bf16[192,128]{1,0:T(8,128)(2,1)S(1)} %get-tuple-element.26), channel_id=1, source_target_pairs={{40,104},{48,112},{56,120},{64,0},{72,8},{80,16},{104,168},{112,17... | collective-permute-start | bytes 147464 | tf_op jit(solution)/shard_map/ppermute | solution.py:196
  4.0 0.1 pad.8.clone
  4.1 0.0 copy-start.2
  4.1 0.0 copy-start.3
  4.1 0.0 copy-done.1
  4.1 0.6 copy-done.2
  4.7 0.0 copy-done.3
  4.8 3.4 %shard_map.78 = (bf16[256,256]{1,0:T(8,128)(2,1)S(1)}, bf16[256,256]{1,0:T(8,128)(2,1)S(1)}, bf16[128,512]{1,0:T(8,128)(2,1)S(1)}, bf16[128,512]{1,0:T(8,128)(2,...) custom-call(s32[1]{0:T(128)} %bitcast.place_ref, f32[3]{0:T(128)S(1)} %copy-done.2, f32[1,256]{1,0:T(1,128)S(1)} %bitcast.18, ...), custom_call_target="tpu_custom_call" | custom-call | flops 50000000 | bytes 1217552 | tf_op jit(solution)/shard_map/pallas_call | solution.py:173
  8.2 0.8 collective-permute-done
  9.0 0.1 maximum_add_fusion
  9.2 20.8 %all_to_all.20 = bf16[8,64,128]{2,1,0:T(8,128)(2,1)S(1)} all-to-all(bf16[8,64,128]{2,1,0:T(8,128)(2,1)S(1)} %bitcast.19), channel_id=1, replica_groups={{0,8,16,24,32,40,48,56},{64,72,80,88,96,104,112,120},{128,136,144,152,1..., dimensions={0} | all-to-all | bytes 262144 | tf_op jit(solution)/shard_map/all_to_all | solution.py:206
  30.0 0.9 shard_map.79
  30.9 1.3 %collective-permute-start.1 = (bf16[192,128]{1,0:T(8,128)(2,1)S(1)}, bf16[192,128]{1,0:T(8,128)(2,1)S(1)}, u32[]{:S(2)}, u32[]{:S(2)}) collective-permute-start(bf16[192,128]{1,0:T(8,128)(2,1)S(1)} %get-tuple-element.35), channel_id=1, source_target_pairs={{40,104},{48,112},{56,120},{64,0},{72,8},{80,16},{104,168},{112,17... | collective-permute-start | bytes 147464 | tf_op jit(solution)/shard_map/ppermute | solution.py:196
  32.2 0.3 shard_map.80
  32.5 4.7 %collective-permute-done.1 = bf16[192,128]{1,0:T(8,128)(2,1)S(1)} collective-permute-done((bf16[192,128]{1,0:T(8,128)(2,1)S(1)}, bf16[192,128]{1,0:T(8,128)(2,1)S(1)}, u32[]{:S(2)}, u32[]{:S(2)}) %collective-permute-start.1) | collective-permute-done | bytes 49184 | tf_op jit(solution)/shard_map/ppermute | solution.py:196
  37.3 0.1 maximum_add_fusion.1
  37.4 12.9 %all_to_all.21 = bf16[8,64,128]{2,1,0:T(8,128)(2,1)S(1)} all-to-all(bf16[8,64,128]{2,1,0:T(8,128)(2,1)S(1)} %bitcast.20), channel_id=1, replica_groups={{0,8,16,24,32,40,48,56},{64,72,80,88,96,104,112,120},{128,136,144,152,1..., dimensions={0} | all-to-all | bytes 262144 | tf_op jit(solution)/shard_map/all_to_all | solution.py:206
  50.3 0.9 shard_map.81
  51.2 1.3 %collective-permute-start.2 = (bf16[192,128]{1,0:T(8,128)(2,1)S(1)}, bf16[192,128]{1,0:T(8,128)(2,1)S(1)}, u32[]{:S(2)}, u32[]{:S(2)}) collective-permute-start(bf16[192,128]{1,0:T(8,128)(2,1)S(1)} %get-tuple-element.39), channel_id=1, source_target_pairs={{40,104},{48,112},{56,120},{64,0},{72,8},{80,16},{104,168},{112,17... | collective-permute-start | bytes 147464 | tf_op jit(solution)/shard_map/ppermute | solution.py:196
  52.5 0.3 shard_map.82
  52.8 4.7 %collective-permute-done.2 = bf16[192,128]{1,0:T(8,128)(2,1)S(1)} collective-permute-done((bf16[192,128]{1,0:T(8,128)(2,1)S(1)}, bf16[192,128]{1,0:T(8,128)(2,1)S(1)}, u32[]{:S(2)}, u32[]{:S(2)}) %collective-permute-start.2) | collective-permute-done | bytes 49184 | tf_op jit(solution)/shard_map/ppermute | solution.py:196
  57.5 0.8 maximum_add_fusion.2
  58.3 3.4 %all-to-all-start.2 = ((bf16[8,64,128]{2,1,0:T(8,128)(2,1)}), bf16[8,64,128]{2,1,0:T(8,128)(2,1)S(1)}, u32[]{:S(2)}, u32[]{:S(2)}) async-start(bf16[8,64,128]{2,1,0:T(8,128)(2,1)} %bitcast.8), calls=%async_computation.2 | async-start | bytes 262144 | tf_op jit(solution)/shard_map/all_to_all | solution.py:206
  61.7 10.4 %all-to-all-done.2 = bf16[8,64,128]{2,1,0:T(8,128)(2,1)S(1)} async-done(((bf16[8,64,128]{2,1,0:T(8,128)(2,1)}), bf16[8,64,128]{2,1,0:T(8,128)(2,1)S(1)}, u32[]{:S(2)}, u32[]{:S(2)}) %all-to-all-start.2) | async-done | bytes 131104 | tf_op jit(solution)/shard_map/all_to_all | solution.py:206
  72.1 1.4 %shard_map.83 = (f32[256,128]{1,0:T(8,128)}, bf16[256,128]{1,0:T(8,128)(2,1)S(1)}) custom-call(f32[3]{0:T(128)S(1)} %copy-done.2, f32[256,128]{1,0:T(8,128)S(1)} %get-tuple-element.37.part_ref, bf16[512,128]{1,0:T(8,128)(2,1)S(1)} %bitcast.16, bf16[128,512]{1,0:T(8,128)(2,1)S(1)} %get-tuple-element.27.halo_high_ref, ...), custom_call_target="tpu_custom_call" | custom-call | flops 40000000 | bytes 851980 | tf_op jit(solution)/shard_map/pallas_call | solution.py:173
  73.6 14.1 %all-gather = bf16[2048,128]{1,0:T(8,128)(2,1)S(1)} all-gather(bf16[256,128]{1,0:T(8,128)(2,1)S(1)} %get-tuple-element.41), channel_id=2, replica_groups=mesh['grid'=64,'band'=8] {'band'}, dimensions={0}, use_global_device_ids=true | all-gather | bytes 589824 | tf_op jit(solution)/shard_map/all_gather | solution.py:272
  87.7 0.5 shard_map.84
  88.2 0.1 reshape.43
  88.3 30.7 %all_to_all.22 = bf16[64,2,1024]{2,1,0:T(2,128)(2,1)S(1)} all-to-all(bf16[64,2,1024]{2,1,0:T(2,128)(2,1)S(1)} %reshape.43), channel_id=1, replica_groups=mesh['grid'=64,'band'=8] {'grid'}, dimensions={0} | all-to-all | bytes 524288 | tf_op jit(solution)/shard_map/all_to_all | solution.py:280
  119.0 0.2 convert_reduce_fusion
  119.2 0.6 broadcast_multiply_fusion
  (10 shorter events, 0.1 us)
Async XLA Ops:
  0.6 0.7 copy-start.4
  1.5 0.9 copy-start
  2.4 1.7 %copy-start.1 = (s32[36,256]{1,0:T(8,128)S(1)}, s32[36,256]{1,0:T(8,128)}, u32[]{:S(2)}) copy-start(s32[36,256]{1,0:T(8,128)} %table_ref.1) | copy-start | bytes 110596
  2.7 6.3 %collective-permute-start = (bf16[192,128]{1,0:T(8,128)(2,1)S(1)}, bf16[192,128]{1,0:T(8,128)(2,1)S(1)}, u32[]{:S(2)}, u32[]{:S(2)}) collective-permute-start(bf16[192,128]{1,0:T(8,128)(2,1)S(1)} %get-tuple-element.26), channel_id=1, source_target_pairs={{40,104},{48,112},{56,120},{64,0},{72,8},{80,16},{104,168},{112,17... | collective-permute-start | bytes 147464 | tf_op jit(solution)/shard_map/ppermute | solution.py:196
  4.1 0.7 copy-start.2
  4.1 0.7 copy-start.3
  30.9 6.3 %collective-permute-start.1 = (bf16[192,128]{1,0:T(8,128)(2,1)S(1)}, bf16[192,128]{1,0:T(8,128)(2,1)S(1)}, u32[]{:S(2)}, u32[]{:S(2)}) collective-permute-start(bf16[192,128]{1,0:T(8,128)(2,1)S(1)} %get-tuple-element.35), channel_id=1, source_target_pairs={{40,104},{48,112},{56,120},{64,0},{72,8},{80,16},{104,168},{112,17... | collective-permute-start | bytes 147464 | tf_op jit(solution)/shard_map/ppermute | solution.py:196
  51.2 6.3 %collective-permute-start.2 = (bf16[192,128]{1,0:T(8,128)(2,1)S(1)}, bf16[192,128]{1,0:T(8,128)(2,1)S(1)}, u32[]{:S(2)}, u32[]{:S(2)}) collective-permute-start(bf16[192,128]{1,0:T(8,128)(2,1)S(1)} %get-tuple-element.39), channel_id=1, source_target_pairs={{40,104},{48,112},{56,120},{64,0},{72,8},{80,16},{104,168},{112,17... | collective-permute-start | bytes 147464 | tf_op jit(solution)/shard_map/ppermute | solution.py:196
  58.3 13.8 %all-to-all-start.2 = ((bf16[8,64,128]{2,1,0:T(8,128)(2,1)}), bf16[8,64,128]{2,1,0:T(8,128)(2,1)S(1)}, u32[]{:S(2)}, u32[]{:S(2)}) async-start(bf16[8,64,128]{2,1,0:T(8,128)(2,1)} %bitcast.8), calls=%async_computation.2 | async-start | bytes 262144 | tf_op jit(solution)/shard_map/all_to_all | solution.py:206

commit v2 on v1

--- a/solution.py
+++ b/solution.py
@@ -39,26 +39,36 @@
     return high, (values - high.astype(F32)).astype(BF16)
 
 
-def select_rows(select_ref, sends_ref, first, blocks, rows):
-    for pair in range((blocks + 1) // 2):
-        picks = sends_ref[pl.ds(first + 2 * pair, 1), :]
-        height = min(TILE, 64 * (blocks - 2 * pair))
+def select_rows(select_ref, sends_ref, offsets, rows):
+    def block(offset):
+        picks = jnp.full((1, 64), rows, jnp.int32)
+        for slot in range(2 * REACH):
+            kept = slot - REACH if slot < REACH else slot - REACH + 1
+            picks = jnp.where(offset == kept, sends_ref[slot], picks)
+        return picks
+
+    for pair in range((len(offsets) + 1) // 2):
+        two = [block(offset) for offset in offsets[2 * pair : 2 * pair + 2]]
+        height = 64 * len(two)
+        picks = jnp.concatenate([two[0], two[-1]], axis=1)
         for at in range(0, rows, TILE):
             here = lax.broadcasted_iota(jnp.int32, (TILE, TILE), 0) + at
             hit = jnp.where(here == picks, 1.0, 0.0)
             select_ref[pl.ds(pair * TILE, height), pl.ds(at, TILE)] = jnp.transpose(hit)[:height].astype(BF16)
 
 
-def begin_kernel(place_ref, count_ref, sends_ref, states_ref, start_ref, own_ref, cross_ref, crossing_ref):
+def begin_kernel(
+    place_ref, band_ref, count_ref, sends_ref, states_ref, start_ref, own_ref, cross_ref, crossing_ref
+):
     place = place_ref[0]
     rows = states_ref.shape[0]
+    first = jnp.where(place >= 5, GROUP - place, -REACH - place)
+    select_rows(cross_ref, sends_ref, [first + at for at in range(REACH)], rows)
     live = lax.broadcasted_iota(jnp.int32, states_ref.shape, 0) < count_ref[0]
     start = jnp.where(live, states_ref[...], 0.0)
     start_ref[...] = start
-    first = jnp.where(place >= 5, 15 - place, jnp.maximum(4 - place, 0))
-    select_rows(cross_ref, sends_ref, first, REACH, rows)
     crossing_ref[...] = dot(cross_ref[...], start.astype(BF16)).astype(BF16)
-    select_rows(own_ref, sends_ref, 7 - place, GROUP, rows)
+    select_rows(own_ref, sends_ref, [at - place for at in range(GROUP)], rows)
 
 
 def local_part(fields, high_ref, low_ref, own_ref, part_ref, outgoing_ref):
@@ -69,12 +79,24 @@
 
 def build_kernel(
     place_ref, bounds_ref, potential_ref, table_ref, start_ref, own_ref,
-    high_ref, low_ref, halo_high_ref, halo_low_ref, part_ref, outgoing_ref, halo_table
+    high_ref, low_ref, halos_ref, factors_ref, part_ref, outgoing_ref, halo_table
 ):
     place = place_ref[0]
     rows = start_ref.shape[0]
     stencil = table_ref.shape[0]
-    middle = (bounds_ref[2] + bounds_ref[1]) / 2.0
+    lower, cutoff, upper = (jnp.broadcast_to(bounds_ref[:, at : at + 1], (8, TILE)) for at in range(3))
+    half = (upper - cutoff) / 2.0
+    middle = (upper + cutoff) / 2.0
+    sigma = half / (lower - middle)
+    twice = 2.0 / sigma
+    factors_ref[0] = sigma / half
+    factors_ref[1] = jnp.zeros_like(sigma)
+    for degree in range(1, DEGREE):
+        following = 1.0 / (twice - sigma)
+        factors_ref[2 * degree] = 2.0 * following / half
+        factors_ref[2 * degree + 1] = sigma * following
+        sigma = following
+    middle = middle[:1]
     table = table_ref[...]
     slot = jnp.right_shift(table - (rows + 1), 6)
     offset = slot - jnp.where(slot < REACH, REACH, REACH - 1)
@@ -109,8 +131,8 @@
         column = pl.multiple_of(block * TILE, TILE)
         total, _ = gathered(halo_table, column, rows - TILE)
         high, low = split(jnp.transpose(total))
-        halo_high_ref[:, pl.ds(column, TILE)] = high
-        halo_low_ref[:, pl.ds(column, TILE)] = low
+        halos_ref[pl.ds(0, TILE), pl.ds(column, TILE)] = high
+        halos_ref[pl.ds(TILE, TILE), pl.ds(column, TILE)] = low
 
     local_part(start_ref[...], high_ref, low_ref, own_ref, part_ref, outgoing_ref)
 
@@ -119,37 +141,33 @@
     local_part(fields_ref[...], high_ref, low_ref, own_ref, part_ref, outgoing_ref)
 
 
-def update_kernel(degree, bounds_ref, part_ref, halo_ref, halo_high_ref, halo_low_ref, *rest):
+def update_kernel(degree, factors_ref, part_ref, halo_ref, halos_ref, *rest):
     refs = list(rest)
     before_ref = refs.pop(0) if degree > 0 else None
     cross_ref = refs.pop(0) if degree < DEGREE - 1 else None
     fields_ref, extra_ref = refs
-    spread = lambda at: jnp.full((8, TILE), bounds_ref[at], F32)
-    lower, cutoff, upper = spread(0), spread(1), spread(2)
-    half = (upper - cutoff) / 2.0
-    middle = (upper + cutoff) / 2.0
-    sigma = half / (lower - middle)
-    twice = 2.0 / sigma
-    scale, carried = sigma / half, None
-    for _ in range(degree):
-        following = 1.0 / (twice - sigma)
-        scale, carried = 2.0 * following / half, sigma * following
-        sigma = following
+    scale = factors_ref[2 * degree][:1]
+    carried = factors_ref[2 * degree + 1][:1]
     rows = part_ref.shape[0]
-    halo = halo_ref[...]
-    reached = dot(halo_high_ref[...], halo) + dot(halo_low_ref[...], halo)
+    reached = dot(halos_ref[...], halo_ref[...])
+    reached = reached[:TILE] + reached[TILE:]
     for at in range(0, rows, TILE):
         image = part_ref[pl.ds(at, TILE), :]
         if at == rows - TILE:
             image = image + reached
-        image = image * scale[:1]
+        image = image * scale
         if degree > 0:
-            image = image - carried[:1] * before_ref[pl.ds(at, TILE), :]
+            image = image - carried * before_ref[pl.ds(at, TILE), :]
         fields_ref[pl.ds(at, TILE), :] = image
         if degree == DEGREE - 1:
             extra_ref[pl.ds(at, TILE), :] = image.astype(BF16)
     if degree < DEGREE - 1:
         extra_ref[...] = dot(cross_ref[...], fields_ref[...].astype(BF16)).astype(BF16)
+
+
+def end_kernel(scaling, fields_ref, summed_ref, filtered_ref, margin_ref):
+    filtered_ref[...] = fields_ref[...]
+    margin_ref[...] = summed_ref[...] * scaling
 
 
 def margin_kernel(band_ref, every_ref, partial_ref):
@@ -213,28 +231,26 @@
     parts = lax.axis_size("grid")
     bands = lax.axis_size("band")
     slots = GROUP * 64
-    place = lax.rem(lax.axis_index("grid"), GROUP).reshape(1)
-    none = jnp.full((4, 64), rows, jnp.int32)
-    lined = jnp.concatenate([none, send_rows[0, :REACH], none[:1], send_rows[0, REACH:], none, none[:1]], axis=0)
-    paired = jnp.concatenate([lined, jnp.concatenate([lined[1:], none[:1]], axis=0)], axis=1)
+    place = jnp.bitwise_and(lax.axis_index("grid"), GROUP - 1).reshape(1)
+    band = lax.axis_index("band").reshape(1)
 
     start, own, cross, crossing = call(
         begin_kernel,
-        (place, point_count, paired, states),
-        [SMEM, SMEM, VMEM, VMEM],
+        (place, band, point_count, jnp.swapaxes(send_rows, 0, 1), states),
+        [SMEM, SMEM, SMEM, VMEM, VMEM],
         [shape((rows, width)), shape((slots, rows), BF16), shape((REACH * 64, rows), BF16), shape((REACH * 64, width), BF16)],
         10_000_000,
     )
     relayed = across(crossing, parts)
-    high, low, halo_high, halo_low, part, outgoing = call(
+    high, low, halos, factors, part, outgoing = call(
         build_kernel,
-        (place, bounds, potential.reshape(1, rows), stencil_table, start, own),
-        [SMEM, SMEM, VMEM, VMEM, VMEM, VMEM],
+        (place, bounds.reshape(1, 3), potential.reshape(1, rows), stencil_table, start, own),
+        [SMEM, VMEM, VMEM, VMEM, VMEM, VMEM],
         [
             shape((rows, rows), BF16),
             shape((rows, rows), BF16),
-            shape((TILE, slots), BF16),
-            shape((TILE, slots), BF16),
+            shape((2 * TILE, slots), BF16),
+            shape((2 * DEGREE, 8, TILE)),
             shape((rows, width)),
             shape((slots, width), BF16),
         ],
@@ -253,7 +269,7 @@
                 80_000_000,
             )
         halo = exchanged(outgoing, relayed, place[0], parts)
-        operands = [bounds, part, halo, halo_high, halo_low]
+        operands = [factors, part, halo, halos]
         if degree > 0:
             operands.append(before)
         if degree < DEGREE - 1:
@@ -265,21 +281,27 @@
         fields, extra = call(
             functools.partial(update_kernel, degree),
             operands,
-            [SMEM] + [VMEM] * (len(operands) - 1),
+            [VMEM] * len(operands),
             [shape((rows, width)), after],
             40_000_000,
         )
     every_band = lax.all_gather(extra, "band", axis=0)
     (partial_sums,) = call(
         margin_kernel,
-        (lax.axis_index("band").reshape(1), every_band),
+        (band, every_band),
         [SMEM, VMEM],
         [shape((2 * parts, bands * width), BF16)],
         80_000_000,
     )
     blocks = lax.all_to_all(partial_sums.reshape(parts, 2, bands * width), "grid", 0, 0, tiled=True)
     summed = jnp.sum(blocks.astype(F32), axis=0)
-    return fields, summed * (1.0 / (parts * rows))
+    return call(
+        functools.partial(end_kernel, 1.0 / (parts * rows)),
+        (fields, summed),
+        [VMEM, VMEM],
+        [shape((rows, width)), shape(summed.shape)],
+        1000,
+    )
 
 
 def solution(mesh):

time: 120 us -> 117 us (0.975)
  blocking collectives: 78.5 us -> 91.7 us
  waiting for transfers between devices: 20.7 us -> 10.7 us
  starting transfers between devices: 7.25 us -> 3.88 us
  Pallas kernels: 8.06 us -> 6.18 us
  other arithmetic: 2.03 us -> 0.68 us
    all_to_all x2 -> x3, blocking collectives: 33.7 us -> 46.1 us  [exchanged(): lax.all_to_all(message, 'grid', 0, 0, axis_index_groups=groups, tiled=True)]
    all_to_all x1 -> x0, waiting for transfers between devices: 10.4 us -> none  [exchanged(): lax.all_to_all(message, 'grid', 0, 0, axis_index_groups=groups, tiled=True)]
    all_to_all x1 -> x0, starting transfers between devices: 3.37 us -> none  [exchanged(): lax.all_to_all(message, 'grid', 0, 0, axis_index_groups=groups, tiled=True)]
    pallas_call x8 -> x9, Pallas kernels: 8.06 us -> 6.18 us  [call(): pl.pallas_call(kernel, out_shape=tuple(outs), in_specs=specs, out_specs=t...]
  transfers between devices with their start and end apart: 4 -> 3, of which waited for: 4 -> 3; matrix products, arithmetic and copies ran while one was open for 0% -> 0% of each run, Pallas kernels for 3% -> 3%
where the time goes in v2:
time: 117 us
  blocking collectives  91.7 us (78%)
  waiting for transfers between devices  10.7 us (9%)
  Pallas kernels  6.18 us (5%)
  starting transfers between devices  3.88 us (3%)
  local copies, waits for them, and re-layouts  2.44 us (2%)
  between operations  1.43 us (1%)
    all_to_all x3, blocking collectives, exchanged(): lax.all_to_all(message, 'grid', 0, 0, axis_index_groups=groups, tiled=True)  46.1 us
    all_to_all x1, blocking collectives, on_device(): lax.all_to_all(partial_sums.reshape(parts, 2, bands * width), 'grid', 0,...  31.4 us
    all_gather x1, blocking collectives, on_device(): every_band = lax.all_gather(extra, 'band', axis=0)  14.2 us
    ppermute x3, waiting for transfers between devices, across(): return lax.ppermute(crossing, 'grid', route)  10.7 us
    pallas_call x9, Pallas kernels, call(): pl.pallas_call(kernel, out_shape=tuple(outs), in_specs=specs, out_specs=t...  6.18 us
    ppermute x3, starting transfers between devices, across(): return lax.ppermute(crossing, 'grid', route)  3.88 us
  transfers between devices with their start and end apart: 3, of which 3 were waited for; matrix products, arithmetic and copies ran while one was open for 0% of the time, Pallas kernels for 3%

profile of v2, /device:TPU:16, one launch (start us, length us, event | category | flops | bytes accessed | tf_op | source)
XLA Modules:
  0.0 117.0 jit_solution(13195385980904544597)
XLA Ops:
  1.3 0.0 copy-start.2
  1.3 0.7 copy-done.2
  2.0 0.0 copy-start
  2.0 0.9 copy-done
  2.9 0.0 copy-start.1
  2.9 0.4 shard_map.77
  3.2 1.3 %collective-permute-start = (bf16[192,128]{1,0:T(8,128)(2,1)S(1)}, bf16[192,128]{1,0:T(8,128)(2,1)S(1)}, u32[]{:S(2)}, u32[]{:S(2)}) collective-permute-start(bf16[192,128]{1,0:T(8,128)(2,1)S(1)} %get-tuple-element.27), channel_id=1, source_target_pairs={{40,104},{48,112},{56,120},{64,0},{72,8},{80,16},{104,168},{112,17... | collective-permute-start | bytes 147464 | tf_op jit(solution)/shard_map/ppermute | solution.py:214
  4.6 0.1 pad.7.clone
  4.6 0.0 copy-start.3
  4.6 0.0 copy-start.4
  4.6 0.0 copy-done.1
  4.6 0.7 copy-done.3
  5.3 0.0 copy-done.4
  5.3 3.0 %shard_map.78 = (bf16[256,256]{1,0:T(8,128)(2,1)S(1)}, bf16[256,256]{1,0:T(8,128)(2,1)S(1)}, bf16[256,512]{1,0:T(8,128)(2,1)S(1)}, f32[6,8,128]{2,1,0:T(8,128)S(...) custom-call(s32[1]{0:T(128)} %bitcast.place_ref, f32[1,3]{1,0:T(1,128)S(1)} %bitcast.18, f32[1,256]{1,0:T(1,128)S(1)} %bitcast.17, ...), custom_call_target="tpu_custom_call" | custom-call | flops 50000000 | bytes 1242128 | tf_op jit(solution)/shard_map/pallas_call | solution.py:191
  8.3 1.3 %collective-permute-done = bf16[192,128]{1,0:T(8,128)(2,1)S(1)} collective-permute-done((bf16[192,128]{1,0:T(8,128)(2,1)S(1)}, bf16[192,128]{1,0:T(8,128)(2,1)S(1)}, u32[]{:S(2)}, u32[]{:S(2)}) %collective-permute-start) | collective-permute-done | bytes 49184 | tf_op jit(solution)/shard_map/ppermute | solution.py:214
  9.6 0.1 maximum_add_fusion
  9.7 20.4 %all_to_all.20 = bf16[8,64,128]{2,1,0:T(8,128)(2,1)S(1)} all-to-all(bf16[8,64,128]{2,1,0:T(8,128)(2,1)S(1)} %bitcast.20), channel_id=1, replica_groups={{0,8,16,24,32,40,48,56},{64,72,80,88,96,104,112,120},{128,136,144,152,1..., dimensions={0} | all-to-all | bytes 262144 | tf_op jit(solution)/shard_map/all_to_all | solution.py:224
  30.1 0.4 shard_map.79
  30.5 1.3 %collective-permute-start.1 = (bf16[192,128]{1,0:T(8,128)(2,1)S(1)}, bf16[192,128]{1,0:T(8,128)(2,1)S(1)}, u32[]{:S(2)}, u32[]{:S(2)}) collective-permute-start(bf16[192,128]{1,0:T(8,128)(2,1)S(1)} %get-tuple-element.35), channel_id=1, source_target_pairs={{40,104},{48,112},{56,120},{64,0},{72,8},{80,16},{104,168},{112,17... | collective-permute-start | bytes 147464 | tf_op jit(solution)/shard_map/ppermute | solution.py:214
  31.8 0.3 shard_map.80
  32.1 4.7 %collective-permute-done.1 = bf16[192,128]{1,0:T(8,128)(2,1)S(1)} collective-permute-done((bf16[192,128]{1,0:T(8,128)(2,1)S(1)}, bf16[192,128]{1,0:T(8,128)(2,1)S(1)}, u32[]{:S(2)}, u32[]{:S(2)}) %collective-permute-start.1) | collective-permute-done | bytes 49184 | tf_op jit(solution)/shard_map/ppermute | solution.py:214
  36.9 0.1 maximum_add_fusion.1
  37.0 12.9 %all_to_all.21 = bf16[8,64,128]{2,1,0:T(8,128)(2,1)S(1)} all-to-all(bf16[8,64,128]{2,1,0:T(8,128)(2,1)S(1)} %bitcast.21), channel_id=1, replica_groups={{0,8,16,24,32,40,48,56},{64,72,80,88,96,104,112,120},{128,136,144,152,1..., dimensions={0} | all-to-all | bytes 262144 | tf_op jit(solution)/shard_map/all_to_all | solution.py:224
  49.9 0.4 shard_map.81
  50.3 1.3 %collective-permute-start.2 = (bf16[192,128]{1,0:T(8,128)(2,1)S(1)}, bf16[192,128]{1,0:T(8,128)(2,1)S(1)}, u32[]{:S(2)}, u32[]{:S(2)}) collective-permute-start(bf16[192,128]{1,0:T(8,128)(2,1)S(1)} %get-tuple-element.39), channel_id=1, source_target_pairs={{40,104},{48,112},{56,120},{64,0},{72,8},{80,16},{104,168},{112,17... | collective-permute-start | bytes 147464 | tf_op jit(solution)/shard_map/ppermute | solution.py:214
  51.6 0.3 shard_map.82
  51.9 4.7 %collective-permute-done.2 = bf16[192,128]{1,0:T(8,128)(2,1)S(1)} collective-permute-done((bf16[192,128]{1,0:T(8,128)(2,1)S(1)}, bf16[192,128]{1,0:T(8,128)(2,1)S(1)}, u32[]{:S(2)}, u32[]{:S(2)}) %collective-permute-start.2) | collective-permute-done | bytes 49184 | tf_op jit(solution)/shard_map/ppermute | solution.py:214
  56.7 0.1 maximum_add_fusion.2
  56.8 12.9 %all_to_all.22 = bf16[8,64,128]{2,1,0:T(8,128)(2,1)S(1)} all-to-all(bf16[8,64,128]{2,1,0:T(8,128)(2,1)S(1)} %bitcast.19), channel_id=1, replica_groups={{0,8,16,24,32,40,48,56},{64,72,80,88,96,104,112,120},{128,136,144,152,1..., dimensions={0} | all-to-all | bytes 262144 | tf_op jit(solution)/shard_map/all_to_all | solution.py:224
  69.7 0.2 shard_map.83
  69.9 14.2 %all-gather = bf16[2048,128]{1,0:T(8,128)(2,1)S(1)} all-gather(bf16[256,128]{1,0:T(8,128)(2,1)S(1)} %get-tuple-element.41), channel_id=2, replica_groups=mesh['grid'=64,'band'=8] {'band'}, dimensions={0}, use_global_device_ids=true | all-gather | bytes 589824 | tf_op jit(solution)/shard_map/all_gather | solution.py:288
  84.1 0.5 shard_map.84
  84.6 0.1 reshape.47
  84.7 31.4 %all_to_all.23 = bf16[64,2,1024]{2,1,0:T(2,128)(2,1)S(1)} all-to-all(bf16[64,2,1024]{2,1,0:T(2,128)(2,1)S(1)} %reshape.47), channel_id=1, replica_groups=mesh['grid'=64,'band'=8] {'grid'}, dimensions={0} | all-to-all | bytes 524288 | tf_op jit(solution)/shard_map/all_to_all | solution.py:296
  116.1 0.2 convert_reduce_fusion.summed_ref
  116.3 0.7 shard_map.85
  (4 shorter events, 0.0 us)
Async XLA Ops:
  1.3 0.7 copy-start.2
  2.0 0.9 copy-start
  2.9 1.8 %copy-start.1 = (s32[36,256]{1,0:T(8,128)S(1)}, s32[36,256]{1,0:T(8,128)}, u32[]{:S(2)}) copy-start(s32[36,256]{1,0:T(8,128)} %table_ref.1) | copy-start | bytes 110596
  3.2 6.3 %collective-permute-start = (bf16[192,128]{1,0:T(8,128)(2,1)S(1)}, bf16[192,128]{1,0:T(8,128)(2,1)S(1)}, u32[]{:S(2)}, u32[]{:S(2)}) collective-permute-start(bf16[192,128]{1,0:T(8,128)(2,1)S(1)} %get-tuple-element.27), channel_id=1, source_target_pairs={{40,104},{48,112},{56,120},{64,0},{72,8},{80,16},{104,168},{112,17... | collective-permute-start | bytes 147464 | tf_op jit(solution)/shard_map/ppermute | solution.py:214
  4.6 0.7 copy-start.3
  4.6 0.7 copy-start.4
  30.5 6.3 %collective-permute-start.1 = (bf16[192,128]{1,0:T(8,128)(2,1)S(1)}, bf16[192,128]{1,0:T(8,128)(2,1)S(1)}, u32[]{:S(2)}, u32[]{:S(2)}) collective-permute-start(bf16[192,128]{1,0:T(8,128)(2,1)S(1)} %get-tuple-element.35), channel_id=1, source_target_pairs={{40,104},{48,112},{56,120},{64,0},{72,8},{80,16},{104,168},{112,17... | collective-permute-start | bytes 147464 | tf_op jit(solution)/shard_map/ppermute | solution.py:214
  50.3 6.3 %collective-permute-start.2 = (bf16[192,128]{1,0:T(8,128)(2,1)S(1)}, bf16[192,128]{1,0:T(8,128)(2,1)S(1)}, u32[]{:S(2)}, u32[]{:S(2)}) collective-permute-start(bf16[192,128]{1,0:T(8,128)(2,1)S(1)} %get-tuple-element.39), channel_id=1, source_target_pairs={{40,104},{48,112},{56,120},{64,0},{72,8},{80,16},{104,168},{112,17... | collective-permute-start | bytes 147464 | tf_op jit(solution)/shard_map/ppermute | solution.py:214

commit v3 on v2

--- a/solution.py
+++ b/solution.py
@@ -160,7 +160,8 @@
             image = image - carried * before_ref[pl.ds(at, TILE), :]
         fields_ref[pl.ds(at, TILE), :] = image
         if degree == DEGREE - 1:
-            extra_ref[pl.ds(at, TILE), :] = image.astype(BF16)
+            for copy in range(extra_ref.shape[0]):
+                extra_ref[copy, pl.ds(at, TILE), :] = image.astype(BF16)
     if degree < DEGREE - 1:
         extra_ref[...] = dot(cross_ref[...], fields_ref[...].astype(BF16)).astype(BF16)
 
@@ -173,17 +174,18 @@
 def margin_kernel(band_ref, every_ref, partial_ref):
     bands, _, width = every_ref.shape
     wanted = 2 * bands
+    order = [band % 2 * (bands // 2) + band // 2 for band in range(bands)]
     row = lax.broadcasted_iota(jnp.int32, (wanted, width), 0)
     column = lax.broadcasted_iota(jnp.int32, (wanted, width), 1)
     target = jnp.right_shift(row, 1) * wanted + 2 * band_ref[0] + jnp.bitwise_and(row, 1)
     pick = jnp.where(column == target, 1.0, 0.0).astype(BF16)
     chosen = [
-        lax.dot_general(pick, every_ref[band], (((1,), (1,)), ((), ())), preferred_element_type=F32).astype(BF16)
+        lax.dot_general(pick, every_ref[order[band]], (((1,), (1,)), ((), ())), preferred_element_type=F32).astype(BF16)
         for band in range(bands)
     ]
     chosen = jnp.concatenate(chosen, axis=0)
     for band in range(bands):
-        partial_ref[:, pl.ds(band * width, width)] = dot(chosen, every_ref[band]).astype(BF16)
+        partial_ref[:, pl.ds(band * width, width)] = dot(chosen, every_ref[order[band]]).astype(BF16)
 
 
 def call(kernel, operands, specs, outs, flops, scratch=()):
@@ -276,7 +278,7 @@
             operands.append(cross)
             after = shape((REACH * 64, width), BF16)
         else:
-            after = shape((rows, width), BF16)
+            after = shape((bands // 2, rows, width), BF16)
         before = fields
         fields, extra = call(
             functools.partial(update_kernel, degree),
@@ -285,7 +287,10 @@
             [shape((rows, width)), after],
             40_000_000,
         )
-    every_band = lax.all_gather(extra, "band", axis=0)
+    alike = [list(range(core, bands, 2)) for core in range(2)]
+    chips = [[first, first + 1] for first in range(0, bands, 2)]
+    alike_bands = lax.all_to_all(extra, "band", 0, 0, axis_index_groups=alike, tiled=True)
+    every_band = lax.all_gather(alike_bands, "band", axis=0, axis_index_groups=chips, tiled=True)
     (partial_sums,) = call(
         margin_kernel,
         (band, every_band),

time: 117 us -> 116 us (level)
  the two profiles are of different devices: /device:TPU:16 before, /device:TPU:8 now
where the time goes in v3:
time: 116 us
  blocking collectives  90.6 us (78%)
  waiting for transfers between devices  10.7 us (9%)
  Pallas kernels  6.18 us (5%)
  starting transfers between devices  3.88 us (3%)
  local copies, waits for them, and re-layouts  2.44 us (2%)
  between operations  1.43 us (1%)
    all_to_all x3, blocking collectives, exchanged(): lax.all_to_all(message, 'grid', 0, 0, axis_index_groups=groups, tiled=True)  47.8 us
    all_to_all x1, blocking collectives, on_device(): lax.all_to_all(partial_sums.reshape(parts, 2, bands * width), 'grid', 0,...  31.3 us
    ppermute x3, waiting for transfers between devices, across(): return lax.ppermute(crossing, 'grid', route)  10.7 us
    all_to_all x1, blocking collectives, on_device(): lax.all_to_all(extra, 'band', 0, 0, axis_index_groups=alike, tiled=True)  9.31 us
    pallas_call x9, Pallas kernels, call(): pl.pallas_call(kernel, out_shape=tuple(outs), in_specs=specs, out_specs=t...  6.18 us
    ppermute x3, starting transfers between devices, across(): return lax.ppermute(crossing, 'grid', route)  3.88 us
  transfers between devices with their start and end apart: 3, of which 3 were waited for; matrix products, arithmetic and copies ran while one was open for 0% of the time, Pallas kernels for 3%

profile of v3, /device:TPU:8, one launch (start us, length us, event | category | flops | bytes accessed | tf_op | source)
XLA Modules:
  0.0 115.9 jit_solution(11713337685578782280)
XLA Ops:
  1.3 0.0 copy-start.2
  1.3 0.7 copy-done.2
  2.0 0.0 copy-start
  2.0 0.9 copy-done
  2.9 0.0 copy-start.1
  2.9 0.4 shard_map.77
  3.2 1.3 %collective-permute-start = (bf16[192,128]{1,0:T(8,128)(2,1)S(1)}, bf16[192,128]{1,0:T(8,128)(2,1)S(1)}, u32[]{:S(2)}, u32[]{:S(2)}) collective-permute-start(bf16[192,128]{1,0:T(8,128)(2,1)S(1)} %get-tuple-element.27), channel_id=1, source_target_pairs={{40,104},{48,112},{56,120},{64,0},{72,8},{80,16},{104,168},{112,17... | collective-permute-start | bytes 147464 | tf_op jit(solution)/shard_map/ppermute | solution.py:216
  4.6 0.1 pad.7.clone
  4.6 0.0 copy-start.3
  4.6 0.0 copy-start.4
  4.6 0.0 copy-done.1
  4.6 0.7 copy-done.3
  5.3 0.0 copy-done.4
  5.3 3.0 %shard_map.78 = (bf16[256,256]{1,0:T(8,128)(2,1)S(1)}, bf16[256,256]{1,0:T(8,128)(2,1)S(1)}, bf16[256,512]{1,0:T(8,128)(2,1)S(1)}, f32[6,8,128]{2,1,0:T(8,128)S(...) custom-call(s32[1]{0:T(128)} %bitcast.place_ref, f32[1,3]{1,0:T(1,128)S(1)} %bitcast.16, f32[1,256]{1,0:T(1,128)S(1)} %bitcast.15, ...), custom_call_target="tpu_custom_call" | custom-call | flops 50000000 | bytes 1242128 | tf_op jit(solution)/shard_map/pallas_call | solution.py:193
  8.3 1.3 %collective-permute-done = bf16[192,128]{1,0:T(8,128)(2,1)S(1)} collective-permute-done((bf16[192,128]{1,0:T(8,128)(2,1)S(1)}, bf16[192,128]{1,0:T(8,128)(2,1)S(1)}, u32[]{:S(2)}, u32[]{:S(2)}) %collective-permute-start) | collective-permute-done | bytes 49184 | tf_op jit(solution)/shard_map/ppermute | solution.py:216
  9.6 0.1 maximum_add_fusion
  9.7 21.3 %all_to_all.25 = bf16[8,64,128]{2,1,0:T(8,128)(2,1)S(1)} all-to-all(bf16[8,64,128]{2,1,0:T(8,128)(2,1)S(1)} %bitcast.18), channel_id=1, replica_groups={{0,8,16,24,32,40,48,56},{64,72,80,88,96,104,112,120},{128,136,144,152,1..., dimensions={0} | all-to-all | bytes 262144 | tf_op jit(solution)/shard_map/all_to_all | solution.py:226
  31.1 0.4 shard_map.79
  31.5 1.3 %collective-permute-start.1 = (bf16[192,128]{1,0:T(8,128)(2,1)S(1)}, bf16[192,128]{1,0:T(8,128)(2,1)S(1)}, u32[]{:S(2)}, u32[]{:S(2)}) collective-permute-start(bf16[192,128]{1,0:T(8,128)(2,1)S(1)} %get-tuple-element.35), channel_id=1, source_target_pairs={{40,104},{48,112},{56,120},{64,0},{72,8},{80,16},{104,168},{112,17... | collective-permute-start | bytes 147464 | tf_op jit(solution)/shard_map/ppermute | solution.py:216
  32.8 0.3 shard_map.80
  33.1 4.7 %collective-permute-done.1 = bf16[192,128]{1,0:T(8,128)(2,1)S(1)} collective-permute-done((bf16[192,128]{1,0:T(8,128)(2,1)S(1)}, bf16[192,128]{1,0:T(8,128)(2,1)S(1)}, u32[]{:S(2)}, u32[]{:S(2)}) %collective-permute-start.1) | collective-permute-done | bytes 49184 | tf_op jit(solution)/shard_map/ppermute | solution.py:216
  37.8 0.1 maximum_add_fusion.1
  38.0 13.3 %all_to_all.26 = bf16[8,64,128]{2,1,0:T(8,128)(2,1)S(1)} all-to-all(bf16[8,64,128]{2,1,0:T(8,128)(2,1)S(1)} %bitcast.19), channel_id=1, replica_groups={{0,8,16,24,32,40,48,56},{64,72,80,88,96,104,112,120},{128,136,144,152,1..., dimensions={0} | all-to-all | bytes 262144 | tf_op jit(solution)/shard_map/all_to_all | solution.py:226
  51.3 0.4 shard_map.81
  51.7 1.3 %collective-permute-start.2 = (bf16[192,128]{1,0:T(8,128)(2,1)S(1)}, bf16[192,128]{1,0:T(8,128)(2,1)S(1)}, u32[]{:S(2)}, u32[]{:S(2)}) collective-permute-start(bf16[192,128]{1,0:T(8,128)(2,1)S(1)} %get-tuple-element.39), channel_id=1, source_target_pairs={{40,104},{48,112},{56,120},{64,0},{72,8},{80,16},{104,168},{112,17... | collective-permute-start | bytes 147464 | tf_op jit(solution)/shard_map/ppermute | solution.py:216
  53.0 0.3 shard_map.82
  53.3 4.7 %collective-permute-done.2 = bf16[192,128]{1,0:T(8,128)(2,1)S(1)} collective-permute-done((bf16[192,128]{1,0:T(8,128)(2,1)S(1)}, bf16[192,128]{1,0:T(8,128)(2,1)S(1)}, u32[]{:S(2)}, u32[]{:S(2)}) %collective-permute-start.2) | collective-permute-done | bytes 49184 | tf_op jit(solution)/shard_map/ppermute | solution.py:216
  58.0 0.1 maximum_add_fusion.2
  58.2 13.2 %all_to_all.27 = bf16[8,64,128]{2,1,0:T(8,128)(2,1)S(1)} all-to-all(bf16[8,64,128]{2,1,0:T(8,128)(2,1)S(1)} %bitcast.17), channel_id=1, replica_groups={{0,8,16,24,32,40,48,56},{64,72,80,88,96,104,112,120},{128,136,144,152,1..., dimensions={0} | all-to-all | bytes 262144 | tf_op jit(solution)/shard_map/all_to_all | solution.py:226
  71.4 0.2 shard_map.83
  71.6 9.3 %all_to_all.28 = bf16[4,256,128]{2,1,0:T(8,128)(2,1)S(1)} all-to-all(bf16[4,256,128]{2,1,0:T(8,128)(2,1)S(1)} %get-tuple-element.41), channel_id=1, replica_groups={{0,2,4,6},{1,3,5,7},{8,10,12,14},{9,11,13,15},{16,18,20,22},{17,19,21,2..., dimensions={0} | all-to-all | bytes 524288 | tf_op jit(solution)/shard_map/all_to_all | solution.py:292
  80.9 2.2 %all_gather.3.every_ref = bf16[8,256,128]{2,1,0:T(8,128)(2,1)S(1)} all-gather(bf16[4,256,128]{2,1,0:T(8,128)(2,1)S(1)} %all_to_all.28), channel_id=1, replica_groups={{0,1},{2,3},{4,5},{6,7},{8,9},{10,11},{12,13},{14,15},{16,17},{18,19},{..., dimensions={0}, use_global_device_ids=true | all-gather | bytes 786432 | tf_op jit(solution)/shard_map/all_gather | solution.py:293
  83.1 0.5 shard_map.84
  83.6 0.1 reshape.47
  83.7 31.3 %all_to_all.29 = bf16[64,2,1024]{2,1,0:T(2,128)(2,1)S(1)} all-to-all(bf16[64,2,1024]{2,1,0:T(2,128)(2,1)S(1)} %reshape.47), channel_id=1, replica_groups=mesh['grid'=64,'band'=8] {'grid'}, dimensions={0} | all-to-all | bytes 524288 | tf_op jit(solution)/shard_map/all_to_all | solution.py:301
  115.0 0.2 convert_reduce_fusion.summed_ref
  115.3 0.7 shard_map.85
  (4 shorter events, 0.0 us)
Async XLA Ops:
  1.3 0.7 copy-start.2
  2.0 0.9 copy-start
  2.9 1.8 %copy-start.1 = (s32[36,256]{1,0:T(8,128)S(1)}, s32[36,256]{1,0:T(8,128)}, u32[]{:S(2)}) copy-start(s32[36,256]{1,0:T(8,128)} %table_ref.1) | copy-start | bytes 110596
  3.2 6.3 %collective-permute-start = (bf16[192,128]{1,0:T(8,128)(2,1)S(1)}, bf16[192,128]{1,0:T(8,128)(2,1)S(1)}, u32[]{:S(2)}, u32[]{:S(2)}) collective-permute-start(bf16[192,128]{1,0:T(8,128)(2,1)S(1)} %get-tuple-element.27), channel_id=1, source_target_pairs={{40,104},{48,112},{56,120},{64,0},{72,8},{80,16},{104,168},{112,17... | collective-permute-start | bytes 147464 | tf_op jit(solution)/shard_map/ppermute | solution.py:216
  4.6 0.7 copy-start.3
  4.6 0.7 copy-start.4
  31.5 6.3 %collective-permute-start.1 = (bf16[192,128]{1,0:T(8,128)(2,1)S(1)}, bf16[192,128]{1,0:T(8,128)(2,1)S(1)}, u32[]{:S(2)}, u32[]{:S(2)}) collective-permute-start(bf16[192,128]{1,0:T(8,128)(2,1)S(1)} %get-tuple-element.35), channel_id=1, source_target_pairs={{40,104},{48,112},{56,120},{64,0},{72,8},{80,16},{104,168},{112,17... | collective-permute-start | bytes 147464 | tf_op jit(solution)/shard_map/ppermute | solution.py:216
  51.7 6.3 %collective-permute-start.2 = (bf16[192,128]{1,0:T(8,128)(2,1)S(1)}, bf16[192,128]{1,0:T(8,128)(2,1)S(1)}, u32[]{:S(2)}, u32[]{:S(2)}) collective-permute-start(bf16[192,128]{1,0:T(8,128)(2,1)S(1)} %get-tuple-element.39), channel_id=1, source_target_pairs={{40,104},{48,112},{56,120},{64,0},{72,8},{80,16},{104,168},{112,17... | collective-permute-start | bytes 147464 | tf_op jit(solution)/shard_map/ppermute | solution.py:216

commit v4 on v3

--- a/solution.py
+++ b/solution.py
@@ -58,16 +58,14 @@
 
 
 def begin_kernel(
-    place_ref, band_ref, count_ref, sends_ref, states_ref, start_ref, own_ref, cross_ref, crossing_ref
+    place_ref, band_ref, sends_ref, states_ref, held_ref, own_ref, cross_ref, crossing_ref
 ):
     place = place_ref[0]
     rows = states_ref.shape[0]
     first = jnp.where(place >= 5, GROUP - place, -REACH - place)
     select_rows(cross_ref, sends_ref, [first + at for at in range(REACH)], rows)
-    live = lax.broadcasted_iota(jnp.int32, states_ref.shape, 0) < count_ref[0]
-    start = jnp.where(live, states_ref[...], 0.0)
-    start_ref[...] = start
-    crossing_ref[...] = dot(cross_ref[...], start.astype(BF16)).astype(BF16)
+    crossing_ref[...] = dot(cross_ref[...], states_ref[...].astype(BF16)).astype(BF16)
+    held_ref[...] = states_ref[...]
     select_rows(own_ref, sends_ref, [at - place for at in range(GROUP)], rows)
 
 
@@ -78,11 +76,11 @@
 
 
 def build_kernel(
-    place_ref, bounds_ref, potential_ref, table_ref, start_ref, own_ref,
+    place_ref, count_ref, bounds_ref, potential_ref, table_ref, states_ref, own_ref, start_ref,
     high_ref, low_ref, halos_ref, factors_ref, part_ref, outgoing_ref, halo_table
 ):
     place = place_ref[0]
-    rows = start_ref.shape[0]
+    rows = states_ref.shape[0]
     stencil = table_ref.shape[0]
     lower, cutoff, upper = (jnp.broadcast_to(bounds_ref[:, at : at + 1], (8, TILE)) for at in range(3))
     half = (upper - cutoff) / 2.0
@@ -134,6 +132,8 @@
         halos_ref[pl.ds(0, TILE), pl.ds(column, TILE)] = high
         halos_ref[pl.ds(TILE, TILE), pl.ds(column, TILE)] = low
 
+    live = lax.broadcasted_iota(jnp.int32, states_ref.shape, 0) < count_ref[0]
+    start_ref[...] = jnp.where(live, states_ref[...], 0.0)
     local_part(start_ref[...], high_ref, low_ref, own_ref, part_ref, outgoing_ref)
 
 
@@ -236,19 +236,20 @@
     place = jnp.bitwise_and(lax.axis_index("grid"), GROUP - 1).reshape(1)
     band = lax.axis_index("band").reshape(1)
 
-    start, own, cross, crossing = call(
+    held, own, cross, crossing = call(
         begin_kernel,
-        (place, band, point_count, jnp.swapaxes(send_rows, 0, 1), states),
-        [SMEM, SMEM, SMEM, VMEM, VMEM],
+        (place, band, jnp.swapaxes(send_rows, 0, 1), states),
+        [SMEM, SMEM, VMEM, VMEM],
         [shape((rows, width)), shape((slots, rows), BF16), shape((REACH * 64, rows), BF16), shape((REACH * 64, width), BF16)],
         10_000_000,
     )
     relayed = across(crossing, parts)
-    high, low, halos, factors, part, outgoing = call(
+    start, high, low, halos, factors, part, outgoing = call(
         build_kernel,
-        (place, bounds.reshape(1, 3), potential.reshape(1, rows), stencil_table, start, own),
-        [SMEM, VMEM, VMEM, VMEM, VMEM, VMEM],
+        (place, point_count, bounds.reshape(1, 3), potential.reshape(1, rows), stencil_table, held, own),
+        [SMEM, SMEM, VMEM, VMEM, VMEM, VMEM, VMEM],
         [
+            shape((rows, width)),
             shape((rows, rows), BF16),
             shape((rows, rows), BF16),
             shape((2 * TILE, slots), BF16),

time: 116 us -> 116 us (level)
  no operation moved by 1% of the time
where the time goes in v4:
time: 116 us
  blocking collectives  91.3 us (79%)
  waiting for transfers between devices  10 us (9%)
  Pallas kernels  6.19 us (5%)
  starting transfers between devices  3.88 us (3%)
  local copies, waits for them, and re-layouts  2.44 us (2%)
  between operations  1.43 us (1%)
    all_to_all x3, blocking collectives, exchanged(): lax.all_to_all(message, 'grid', 0, 0, axis_index_groups=groups, tiled=True)  48.5 us
    all_to_all x1, blocking collectives, on_device(): lax.all_to_all(partial_sums.reshape(parts, 2, bands * width), 'grid', 0,...  31.4 us
    ppermute x3, waiting for transfers between devices, across(): return lax.ppermute(crossing, 'grid', route)  10 us
    all_to_all x1, blocking collectives, on_device(): lax.all_to_all(extra, 'band', 0, 0, axis_index_groups=alike, tiled=True)  9.31 us
    pallas_call x9, Pallas kernels, call(): pl.pallas_call(kernel, out_shape=tuple(outs), in_specs=specs, out_specs=t...  6.19 us
    ppermute x3, starting transfers between devices, across(): return lax.ppermute(crossing, 'grid', route)  3.88 us
  transfers between devices with their start and end apart: 3, of which 3 were waited for; matrix products, arithmetic and copies ran while one was open for 0% of the time, Pallas kernels for 3%

profile of v4, /device:TPU:8, one launch (start us, length us, event | category | flops | bytes accessed | tf_op | source)
XLA Modules:
  0.0 116.0 jit_solution(5933900684821592164)
XLA Ops:
  0.6 0.0 copy-start.2
  0.6 0.7 copy-done.2
  1.3 0.0 copy-start
  1.3 0.9 copy-done
  2.2 0.0 copy-start.1
  2.2 0.4 shard_map.77
  2.6 1.3 %collective-permute-start = (bf16[192,128]{1,0:T(8,128)(2,1)S(1)}, bf16[192,128]{1,0:T(8,128)(2,1)S(1)}, u32[]{:S(2)}, u32[]{:S(2)}) collective-permute-start(bf16[192,128]{1,0:T(8,128)(2,1)S(1)} %get-tuple-element.28), channel_id=1, source_target_pairs={{40,104},{48,112},{56,120},{64,0},{72,8},{80,16},{104,168},{112,17... | collective-permute-start | bytes 147464 | tf_op jit(solution)/shard_map/ppermute | solution.py:216
  4.6 0.1 pad.7.clone
  4.6 0.0 copy-start.3
  4.6 0.0 copy-start.4
  4.6 0.0 copy-done.1
  4.6 0.7 copy-done.3
  5.3 0.0 copy-done.4
  5.3 3.0 %shard_map.78 = (f32[256,128]{1,0:T(8,128)S(1)}, bf16[256,256]{1,0:T(8,128)(2,1)S(1)}, bf16[256,256]{1,0:T(8,128)(2,1)S(1)}, bf16[256,512]{1,0:T(8,128)(2,1)S(1)...) custom-call(s32[1]{0:T(128)} %bitcast.place_ref, s32[1]{0:T(128)S(6)} %copy.8.count_ref, ...), custom_call_target="tpu_custom_call" | custom-call | flops 50000000 | bytes 1373204 | tf_op jit(solution)/shard_map/pallas_call | solution.py:193
  8.3 0.6 collective-permute-done
  8.9 0.1 maximum_add_fusion
  9.1 22.0 %all_to_all.25 = bf16[8,64,128]{2,1,0:T(8,128)(2,1)S(1)} all-to-all(bf16[8,64,128]{2,1,0:T(8,128)(2,1)S(1)} %bitcast.18), channel_id=1, replica_groups={{0,8,16,24,32,40,48,56},{64,72,80,88,96,104,112,120},{128,136,144,152,1..., dimensions={0} | all-to-all | bytes 262144 | tf_op jit(solution)/shard_map/all_to_all | solution.py:226
  31.1 0.4 shard_map.79
  31.5 1.3 %collective-permute-start.1 = (bf16[192,128]{1,0:T(8,128)(2,1)S(1)}, bf16[192,128]{1,0:T(8,128)(2,1)S(1)}, u32[]{:S(2)}, u32[]{:S(2)}) collective-permute-start(bf16[192,128]{1,0:T(8,128)(2,1)S(1)} %get-tuple-element.36), channel_id=1, source_target_pairs={{40,104},{48,112},{56,120},{64,0},{72,8},{80,16},{104,168},{112,17... | collective-permute-start | bytes 147464 | tf_op jit(solution)/shard_map/ppermute | solution.py:216
  32.8 0.3 shard_map.80
  33.1 4.7 %collective-permute-done.1 = bf16[192,128]{1,0:T(8,128)(2,1)S(1)} collective-permute-done((bf16[192,128]{1,0:T(8,128)(2,1)S(1)}, bf16[192,128]{1,0:T(8,128)(2,1)S(1)}, u32[]{:S(2)}, u32[]{:S(2)}) %collective-permute-start.1) | collective-permute-done | bytes 49184 | tf_op jit(solution)/shard_map/ppermute | solution.py:216
  37.9 0.1 maximum_add_fusion.1
  38.0 13.3 %all_to_all.26 = bf16[8,64,128]{2,1,0:T(8,128)(2,1)S(1)} all-to-all(bf16[8,64,128]{2,1,0:T(8,128)(2,1)S(1)} %bitcast.19), channel_id=1, replica_groups={{0,8,16,24,32,40,48,56},{64,72,80,88,96,104,112,120},{128,136,144,152,1..., dimensions={0} | all-to-all | bytes 262144 | tf_op jit(solution)/shard_map/all_to_all | solution.py:226
  51.3 0.4 shard_map.81
  51.7 1.3 %collective-permute-start.2 = (bf16[192,128]{1,0:T(8,128)(2,1)S(1)}, bf16[192,128]{1,0:T(8,128)(2,1)S(1)}, u32[]{:S(2)}, u32[]{:S(2)}) collective-permute-start(bf16[192,128]{1,0:T(8,128)(2,1)S(1)} %get-tuple-element.41), channel_id=1, source_target_pairs={{40,104},{48,112},{56,120},{64,0},{72,8},{80,16},{104,168},{112,17... | collective-permute-start | bytes 147464 | tf_op jit(solution)/shard_map/ppermute | solution.py:216
  53.0 0.3 shard_map.82
  53.3 4.7 %collective-permute-done.2 = bf16[192,128]{1,0:T(8,128)(2,1)S(1)} collective-permute-done((bf16[192,128]{1,0:T(8,128)(2,1)S(1)}, bf16[192,128]{1,0:T(8,128)(2,1)S(1)}, u32[]{:S(2)}, u32[]{:S(2)}) %collective-permute-start.2) | collective-permute-done | bytes 49184 | tf_op jit(solution)/shard_map/ppermute | solution.py:216
  58.0 0.1 maximum_add_fusion.2
  58.2 13.2 %all_to_all.27 = bf16[8,64,128]{2,1,0:T(8,128)(2,1)S(1)} all-to-all(bf16[8,64,128]{2,1,0:T(8,128)(2,1)S(1)} %bitcast.17), channel_id=1, replica_groups={{0,8,16,24,32,40,48,56},{64,72,80,88,96,104,112,120},{128,136,144,152,1..., dimensions={0} | all-to-all | bytes 262144 | tf_op jit(solution)/shard_map/all_to_all | solution.py:226
  71.4 0.2 shard_map.83
  71.6 9.3 %all_to_all.28 = bf16[4,256,128]{2,1,0:T(8,128)(2,1)S(1)} all-to-all(bf16[4,256,128]{2,1,0:T(8,128)(2,1)S(1)} %get-tuple-element.43), channel_id=1, replica_groups={{0,2,4,6},{1,3,5,7},{8,10,12,14},{9,11,13,15},{16,18,20,22},{17,19,21,2..., dimensions={0} | all-to-all | bytes 524288 | tf_op jit(solution)/shard_map/all_to_all | solution.py:293
  80.9 2.2 %all_gather.3.every_ref = bf16[8,256,128]{2,1,0:T(8,128)(2,1)S(1)} all-gather(bf16[4,256,128]{2,1,0:T(8,128)(2,1)S(1)} %all_to_all.28), channel_id=1, replica_groups={{0,1},{2,3},{4,5},{6,7},{8,9},{10,11},{12,13},{14,15},{16,17},{18,19},{..., dimensions={0}, use_global_device_ids=true | all-gather | bytes 786432 | tf_op jit(solution)/shard_map/all_gather | solution.py:294
  83.1 0.5 shard_map.84
  83.6 0.1 reshape.47
  83.7 31.4 %all_to_all.29 = bf16[64,2,1024]{2,1,0:T(2,128)(2,1)S(1)} all-to-all(bf16[64,2,1024]{2,1,0:T(2,128)(2,1)S(1)} %reshape.47), channel_id=1, replica_groups=mesh['grid'=64,'band'=8] {'grid'}, dimensions={0} | all-to-all | bytes 524288 | tf_op jit(solution)/shard_map/all_to_all | solution.py:302
  115.1 0.2 convert_reduce_fusion.summed_ref
  115.3 0.7 shard_map.85
  (4 shorter events, 0.0 us)
Async XLA Ops:
  0.6 0.7 copy-start.2
  1.3 0.9 copy-start
  2.2 2.4 %copy-start.1 = (s32[36,256]{1,0:T(8,128)S(1)}, s32[36,256]{1,0:T(8,128)}, u32[]{:S(2)}) copy-start(s32[36,256]{1,0:T(8,128)} %table_ref.1) | copy-start | bytes 110596
  2.6 6.3 %collective-permute-start = (bf16[192,128]{1,0:T(8,128)(2,1)S(1)}, bf16[192,128]{1,0:T(8,128)(2,1)S(1)}, u32[]{:S(2)}, u32[]{:S(2)}) collective-permute-start(bf16[192,128]{1,0:T(8,128)(2,1)S(1)} %get-tuple-element.28), channel_id=1, source_target_pairs={{40,104},{48,112},{56,120},{64,0},{72,8},{80,16},{104,168},{112,17... | collective-permute-start | bytes 147464 | tf_op jit(solution)/shard_map/ppermute | solution.py:216
  4.6 0.7 copy-start.3
  4.6 0.7 copy-start.4
  31.5 6.3 %collective-permute-start.1 = (bf16[192,128]{1,0:T(8,128)(2,1)S(1)}, bf16[192,128]{1,0:T(8,128)(2,1)S(1)}, u32[]{:S(2)}, u32[]{:S(2)}) collective-permute-start(bf16[192,128]{1,0:T(8,128)(2,1)S(1)} %get-tuple-element.36), channel_id=1, source_target_pairs={{40,104},{48,112},{56,120},{64,0},{72,8},{80,16},{104,168},{112,17... | collective-permute-start | bytes 147464 | tf_op jit(solution)/shard_map/ppermute | solution.py:216
  51.7 6.3 %collective-permute-start.2 = (bf16[192,128]{1,0:T(8,128)(2,1)S(1)}, bf16[192,128]{1,0:T(8,128)(2,1)S(1)}, u32[]{:S(2)}, u32[]{:S(2)}) collective-permute-start(bf16[192,128]{1,0:T(8,128)(2,1)S(1)} %get-tuple-element.41), channel_id=1, source_target_pairs={{40,104},{48,112},{56,120},{64,0},{72,8},{80,16},{104,168},{112,17... | collective-permute-start | bytes 147464 | tf_op jit(solution)/shard_map/ppermute | solution.py:216

commit v5 on v4

--- a/solution.py
+++ b/solution.py
@@ -76,10 +76,9 @@
 
 
 def build_kernel(
-    place_ref, count_ref, bounds_ref, potential_ref, table_ref, states_ref, own_ref, start_ref,
-    high_ref, low_ref, halos_ref, factors_ref, part_ref, outgoing_ref, halo_table
+    bounds_ref, potential_ref, table_ref, states_ref, own_ref,
+    high_ref, low_ref, halos_ref, factors_ref, part_ref, outgoing_ref
 ):
-    place = place_ref[0]
     rows = states_ref.shape[0]
     stencil = table_ref.shape[0]
     lower, cutoff, upper = (jnp.broadcast_to(bounds_ref[:, at : at + 1], (8, TILE)) for at in range(3))
@@ -95,19 +94,12 @@
         factors_ref[2 * degree + 1] = sigma * following
         sigma = following
     middle = middle[:1]
-    table = table_ref[...]
-    slot = jnp.right_shift(table - (rows + 1), 6)
-    offset = slot - jnp.where(slot < REACH, REACH, REACH - 1)
-    source = jnp.bitwise_and(place - offset, GROUP - 1)
-    halo = source * 64 + jnp.bitwise_and(table - (rows + 1), 63)
-    halo_table[...] = jnp.where(table > rows, halo, -1)
-
-    def gathered(names_ref, column, row):
+    def gathered(column, row):
         here = lax.broadcasted_iota(jnp.int32, (TILE, TILE), 0) + column
         total = jnp.zeros((TILE, TILE), F32)
         for neighbour in range(stencil):
             weight = -KINETIC_SCALE * DIFFERENCE_WEIGHTS[neighbour % SPAN + 1]
-            names = names_ref[neighbour : neighbour + 1, row : row + TILE]
+            names = table_ref[neighbour : neighbour + 1, row : row + TILE]
             total = total + jnp.where(here == names, weight, 0.0)
         return total, here
 
@@ -117,31 +109,38 @@
         @pl.loop(0, rows // TILE)
         def _(block, row=row, diagonal=diagonal):
             column = pl.multiple_of(block * TILE, TILE)
-            total, here = gathered(table_ref, column, row)
+            total, here = gathered(column, row)
             right = lax.broadcasted_iota(jnp.int32, (TILE, TILE), 1) + row
             total = total + jnp.where(here == right, diagonal, 0.0)
             high, low = split(jnp.transpose(total))
             high_ref[pl.ds(row, TILE), pl.ds(column, TILE)] = high
             low_ref[pl.ds(row, TILE), pl.ds(column, TILE)] = low
 
-    @pl.loop(0, GROUP * 64 // TILE)
+    @pl.loop(0, 2 * REACH * 64 // TILE)
     def _(block):
         column = pl.multiple_of(block * TILE, TILE)
-        total, _ = gathered(halo_table, column, rows - TILE)
+        total, _ = gathered(column + rows + 1, rows - TILE)
         high, low = split(jnp.transpose(total))
         halos_ref[pl.ds(0, TILE), pl.ds(column, TILE)] = high
         halos_ref[pl.ds(TILE, TILE), pl.ds(column, TILE)] = low
 
+    local_part(states_ref[...], high_ref, low_ref, own_ref, part_ref, outgoing_ref)
+
+
+def masking_kernel(
+    count_ref, states_ref, fields_ref, high_ref, low_ref, own_ref, start_ref, masked_ref, part_ref, outgoing_ref
+):
     live = lax.broadcasted_iota(jnp.int32, states_ref.shape, 0) < count_ref[0]
     start_ref[...] = jnp.where(live, states_ref[...], 0.0)
-    local_part(start_ref[...], high_ref, low_ref, own_ref, part_ref, outgoing_ref)
+    masked_ref[...] = jnp.where(live, fields_ref[...], 0.0)
+    local_part(masked_ref[...], high_ref, low_ref, own_ref, part_ref, outgoing_ref)
 
 
 def local_kernel(fields_ref, high_ref, low_ref, own_ref, part_ref, outgoing_ref):
     local_part(fields_ref[...], high_ref, low_ref, own_ref, part_ref, outgoing_ref)
 
 
-def update_kernel(degree, factors_ref, part_ref, halo_ref, halos_ref, *rest):
+def update_kernel(degree, place_ref, factors_ref, part_ref, halo_ref, halos_ref, *rest):
     refs = list(rest)
     before_ref = refs.pop(0) if degree > 0 else None
     cross_ref = refs.pop(0) if degree < DEGREE - 1 else None
@@ -149,7 +148,11 @@
     scale = factors_ref[2 * degree][:1]
     carried = factors_ref[2 * degree + 1][:1]
     rows = part_ref.shape[0]
-    reached = dot(halos_ref[...], halo_ref[...])
+    blocks = []
+    for slot in range(2 * REACH):
+        offset = slot - REACH if slot < REACH else slot - REACH + 1
+        blocks.append(halo_ref[jnp.bitwise_and(place_ref[0] - offset, GROUP - 1)])
+    reached = dot(halos_ref[...], jnp.concatenate(blocks, axis=0))
     reached = reached[:TILE] + reached[TILE:]
     for at in range(0, rows, TILE):
         image = part_ref[pl.ds(at, TILE), :]
@@ -224,12 +227,11 @@
     message = (outgoing + jnp.concatenate([down, gap, up], axis=0)).reshape(GROUP, -1, outgoing.shape[1])
     groups = [list(range(first, first + GROUP)) for first in range(0, parts, GROUP)]
     received = lax.all_to_all(message, "grid", 0, 0, axis_index_groups=groups, tiled=True)
-    return received.reshape(outgoing.shape)
+    return received
 
 
 def on_device(states, potential, bounds, point_count, send_rows, stencil_table):
     rows, width = states.shape
-    stencil = stencil_table.shape[0]
     parts = lax.axis_size("grid")
     bands = lax.axis_size("band")
     slots = GROUP * 64
@@ -244,35 +246,38 @@
         10_000_000,
     )
     relayed = across(crossing, parts)
-    start, high, low, halos, factors, part, outgoing = call(
+    high, low, halos, factors, part, outgoing = call(
         build_kernel,
-        (place, point_count, bounds.reshape(1, 3), potential.reshape(1, rows), stencil_table, held, own),
-        [SMEM, SMEM, VMEM, VMEM, VMEM, VMEM, VMEM],
+        (bounds.reshape(1, 3), potential.reshape(1, rows), stencil_table, held, own),
+        [VMEM] * 5,
         [
-            shape((rows, width)),
             shape((rows, rows), BF16),
             shape((rows, rows), BF16),
-            shape((2 * TILE, slots), BF16),
+            shape((2 * TILE, 2 * REACH * 64), BF16),
             shape((2 * DEGREE, 8, TILE)),
             shape((rows, width)),
             shape((slots, width), BF16),
         ],
         50_000_000,
-        [pltpu.VMEM((stencil, rows), jnp.int32)],
-    )
-    before, fields = None, start
+    )
+    before, fields = None, held
     for degree in range(DEGREE):
         if degree > 0:
             relayed = across(extra, parts)
-            part, outgoing = call(
-                local_kernel,
-                (fields, high, low, own),
-                [VMEM] * 4,
-                [shape((rows, width)), shape((slots, width), BF16)],
-                80_000_000,
-            )
+            operands = [fields, high, low, own]
+            outs = [shape((rows, width)), shape((slots, width), BF16)]
+            if degree == 1:
+                before, fields, part, outgoing = call(
+                    masking_kernel,
+                    [point_count, before] + operands,
+                    [SMEM] + [VMEM] * 5,
+                    [shape((rows, width))] * 2 + outs,
+                    80_000_000,
+                )
+            else:
+                part, outgoing = call(local_kernel, operands, [VMEM] * 4, outs, 80_000_000)
         halo = exchanged(outgoing, relayed, place[0], parts)
-        operands = [factors, part, halo, halos]
+        operands = [place, factors, part, halo, halos]
         if degree > 0:
             operands.append(before)
         if degree < DEGREE - 1:
@@ -284,7 +289,7 @@
         fields, extra = call(
             functools.partial(update_kernel, degree),
             operands,
-            [VMEM] * len(operands),
+            [SMEM] + [VMEM] * (len(operands) - 1),
             [shape((rows, width)), after],
             40_000_000,
         )

time: 116 us -> 115 us (level)
  no operation moved by 1% of the time
where the time goes in v5:
time: 115 us
  blocking collectives  90.2 us (78%)
  waiting for transfers between devices  10.3 us (9%)
  Pallas kernels  5.84 us (5%)
  starting transfers between devices  3.88 us (3%)
  local copies, waits for them, and re-layouts  2.44 us (2%)
  between operations  1.43 us (1%)
    all_to_all x3, blocking collectives, exchanged(): lax.all_to_all(message, 'grid', 0, 0, axis_index_groups=groups, tiled=True)  47.5 us
    all_to_all x1, blocking collectives, on_device(): lax.all_to_all(partial_sums.reshape(parts, 2, bands * width), 'grid', 0,...  31.2 us
    ppermute x3, waiting for transfers between devices, across(): return lax.ppermute(crossing, 'grid', route)  10.3 us
    all_to_all x1, blocking collectives, on_device(): lax.all_to_all(extra, 'band', 0, 0, axis_index_groups=alike, tiled=True)  9.31 us
    pallas_call x9, Pallas kernels, call(): pl.pallas_call(kernel, out_shape=tuple(outs), in_specs=specs, out_specs=t...  5.84 us
    ppermute x3, starting transfers between devices, across(): return lax.ppermute(crossing, 'grid', route)  3.88 us
  transfers between devices with their start and end apart: 3, of which 3 were waited for; matrix products, arithmetic and copies ran while one was open for 0% of the time, Pallas kernels for 3%

profile of v5, /device:TPU:8, one launch (start us, length us, event | category | flops | bytes accessed | tf_op | source)
XLA Modules:
  0.0 114.8 jit_solution(9992075642474203712)
XLA Ops:
  0.6 0.0 copy-start.2
  0.6 0.7 copy-done.2
  1.3 0.0 copy-start
  1.3 0.9 copy-done
  2.2 0.0 copy-start.1
  2.2 0.4 shard_map.77
  2.6 1.3 %collective-permute-start = (bf16[192,128]{1,0:T(8,128)(2,1)S(1)}, bf16[192,128]{1,0:T(8,128)(2,1)S(1)}, u32[]{:S(2)}, u32[]{:S(2)}) collective-permute-start(bf16[192,128]{1,0:T(8,128)(2,1)S(1)} %get-tuple-element.29), channel_id=1, source_target_pairs={{40,104},{48,112},{56,120},{64,0},{72,8},{80,16},{104,168},{112,17... | collective-permute-start | bytes 147464 | tf_op jit(solution)/shard_map/ppermute | solution.py:219
  3.9 0.1 pad.7.clone
  4.0 0.0 copy-start.3
  4.0 0.0 copy-start.4
  4.0 0.0 copy-done.1
  4.0 0.7 copy-done.3
  4.7 0.0 copy-done.4
  4.7 2.7 %shard_map.78 = (bf16[256,256]{1,0:T(8,128)(2,1)S(1)}, bf16[256,256]{1,0:T(8,128)(2,1)S(1)}, bf16[256,384]{1,0:T(8,128)(2,1)S(1)}, f32[6,8,128]{2,1,0:T(8,128)S(...) custom-call(f32[1,3]{1,0:T(1,128)S(1)} %bitcast.10, f32[1,256]{1,0:T(1,128)S(1)} %bitcast.9, ...), custom_call_target="tpu_custom_call" | custom-call | flops 50000000 | bytes 1176588 | tf_op jit(solution)/shard_map/pallas_call | solution.py:196
  7.4 1.6 %collective-permute-done = bf16[192,128]{1,0:T(8,128)(2,1)S(1)} collective-permute-done((bf16[192,128]{1,0:T(8,128)(2,1)S(1)}, bf16[192,128]{1,0:T(8,128)(2,1)S(1)}, u32[]{:S(2)}, u32[]{:S(2)}) %collective-permute-start) | collective-permute-done | bytes 49184 | tf_op jit(solution)/shard_map/ppermute | solution.py:219
  8.9 0.1 maximum_add_fusion
  9.1 21.0 %all_to_all.25.halo_ref = bf16[8,64,128]{2,1,0:T(8,128)(2,1)S(1)} all-to-all(bf16[8,64,128]{2,1,0:T(8,128)(2,1)S(1)} %bitcast.12), channel_id=1, replica_groups={{0,8,16,24,32,40,48,56},{64,72,80,88,96,104,112,120},{128,136,144,152,1..., dimensions={0} | all-to-all | bytes 262144 | tf_op jit(solution)/shard_map/all_to_all | solution.py:229
  30.1 0.4 shard_map.79
  30.5 1.3 %collective-permute-start.1 = (bf16[192,128]{1,0:T(8,128)(2,1)S(1)}, bf16[192,128]{1,0:T(8,128)(2,1)S(1)}, u32[]{:S(2)}, u32[]{:S(2)}) collective-permute-start(bf16[192,128]{1,0:T(8,128)(2,1)S(1)} %get-tuple-element.37), channel_id=1, source_target_pairs={{40,104},{48,112},{56,120},{64,0},{72,8},{80,16},{104,168},{112,17... | collective-permute-start | bytes 147464 | tf_op jit(solution)/shard_map/ppermute | solution.py:219
  32.5 0.3 shard_map.80
  32.8 4.1 %collective-permute-done.1 = bf16[192,128]{1,0:T(8,128)(2,1)S(1)} collective-permute-done((bf16[192,128]{1,0:T(8,128)(2,1)S(1)}, bf16[192,128]{1,0:T(8,128)(2,1)S(1)}, u32[]{:S(2)}, u32[]{:S(2)}) %collective-permute-start.1) | collective-permute-done | bytes 49184 | tf_op jit(solution)/shard_map/ppermute | solution.py:219
  36.9 0.1 maximum_add_fusion.1
  37.0 13.3 %all_to_all.26.halo_ref = bf16[8,64,128]{2,1,0:T(8,128)(2,1)S(1)} all-to-all(bf16[8,64,128]{2,1,0:T(8,128)(2,1)S(1)} %bitcast.13), channel_id=1, replica_groups={{0,8,16,24,32,40,48,56},{64,72,80,88,96,104,112,120},{128,136,144,152,1..., dimensions={0} | all-to-all | bytes 262144 | tf_op jit(solution)/shard_map/all_to_all | solution.py:229
  50.3 0.4 shard_map.81
  50.7 1.3 %collective-permute-start.2 = (bf16[192,128]{1,0:T(8,128)(2,1)S(1)}, bf16[192,128]{1,0:T(8,128)(2,1)S(1)}, u32[]{:S(2)}, u32[]{:S(2)}) collective-permute-start(bf16[192,128]{1,0:T(8,128)(2,1)S(1)} %get-tuple-element.42), channel_id=1, source_target_pairs={{40,104},{48,112},{56,120},{64,0},{72,8},{80,16},{104,168},{112,17... | collective-permute-start | bytes 147464 | tf_op jit(solution)/shard_map/ppermute | solution.py:219
  52.0 0.3 shard_map.82
  52.3 4.7 %collective-permute-done.2 = bf16[192,128]{1,0:T(8,128)(2,1)S(1)} collective-permute-done((bf16[192,128]{1,0:T(8,128)(2,1)S(1)}, bf16[192,128]{1,0:T(8,128)(2,1)S(1)}, u32[]{:S(2)}, u32[]{:S(2)}) %collective-permute-start.2) | collective-permute-done | bytes 49184 | tf_op jit(solution)/shard_map/ppermute | solution.py:219
  57.0 0.1 maximum_add_fusion.2
  57.2 13.2 %all_to_all.27.halo_ref = bf16[8,64,128]{2,1,0:T(8,128)(2,1)S(1)} all-to-all(bf16[8,64,128]{2,1,0:T(8,128)(2,1)S(1)} %bitcast.11), channel_id=1, replica_groups={{0,8,16,24,32,40,48,56},{64,72,80,88,96,104,112,120},{128,136,144,152,1..., dimensions={0} | all-to-all | bytes 262144 | tf_op jit(solution)/shard_map/all_to_all | solution.py:229
  70.4 0.2 shard_map.83
  70.6 9.3 %all_to_all.28 = bf16[4,256,128]{2,1,0:T(8,128)(2,1)S(1)} all-to-all(bf16[4,256,128]{2,1,0:T(8,128)(2,1)S(1)} %get-tuple-element.45), channel_id=1, replica_groups={{0,2,4,6},{1,3,5,7},{8,10,12,14},{9,11,13,15},{16,18,20,22},{17,19,21,2..., dimensions={0} | all-to-all | bytes 524288 | tf_op jit(solution)/shard_map/all_to_all | solution.py:298
  79.9 2.2 %all_gather.3.every_ref = bf16[8,256,128]{2,1,0:T(8,128)(2,1)S(1)} all-gather(bf16[4,256,128]{2,1,0:T(8,128)(2,1)S(1)} %all_to_all.28), channel_id=1, replica_groups={{0,1},{2,3},{4,5},{6,7},{8,9},{10,11},{12,13},{14,15},{16,17},{18,19},{..., dimensions={0}, use_global_device_ids=true | all-gather | bytes 786432 | tf_op jit(solution)/shard_map/all_gather | solution.py:299
  82.1 0.5 shard_map.84
  82.6 0.1 reshape.35
  82.7 31.2 %all_to_all.29 = bf16[64,2,1024]{2,1,0:T(2,128)(2,1)S(1)} all-to-all(bf16[64,2,1024]{2,1,0:T(2,128)(2,1)S(1)} %reshape.35), channel_id=1, replica_groups=mesh['grid'=64,'band'=8] {'grid'}, dimensions={0} | all-to-all | bytes 524288 | tf_op jit(solution)/shard_map/all_to_all | solution.py:307
  113.9 0.2 convert_reduce_fusion.summed_ref
  114.1 0.7 shard_map.85
  (4 shorter events, 0.0 us)
Async XLA Ops:
  0.6 0.7 copy-start.2
  1.3 0.9 copy-start
  2.2 1.8 %copy-start.1 = (s32[36,256]{1,0:T(8,128)S(1)}, s32[36,256]{1,0:T(8,128)}, u32[]{:S(2)}) copy-start(s32[36,256]{1,0:T(8,128)} %table_ref.1) | copy-start | bytes 110596
  2.6 6.3 %collective-permute-start = (bf16[192,128]{1,0:T(8,128)(2,1)S(1)}, bf16[192,128]{1,0:T(8,128)(2,1)S(1)}, u32[]{:S(2)}, u32[]{:S(2)}) collective-permute-start(bf16[192,128]{1,0:T(8,128)(2,1)S(1)} %get-tuple-element.29), channel_id=1, source_target_pairs={{40,104},{48,112},{56,120},{64,0},{72,8},{80,16},{104,168},{112,17... | collective-permute-start | bytes 147464 | tf_op jit(solution)/shard_map/ppermute | solution.py:219
  4.0 0.7 copy-start.3
  4.0 0.7 copy-start.4
  30.5 6.3 %collective-permute-start.1 = (bf16[192,128]{1,0:T(8,128)(2,1)S(1)}, bf16[192,128]{1,0:T(8,128)(2,1)S(1)}, u32[]{:S(2)}, u32[]{:S(2)}) collective-permute-start(bf16[192,128]{1,0:T(8,128)(2,1)S(1)} %get-tuple-element.37), channel_id=1, source_target_pairs={{40,104},{48,112},{56,120},{64,0},{72,8},{80,16},{104,168},{112,17... | collective-permute-start | bytes 147464 | tf_op jit(solution)/shard_map/ppermute | solution.py:219
  50.7 6.3 %collective-permute-start.2 = (bf16[192,128]{1,0:T(8,128)(2,1)S(1)}, bf16[192,128]{1,0:T(8,128)(2,1)S(1)}, u32[]{:S(2)}, u32[]{:S(2)}) collective-permute-start(bf16[192,128]{1,0:T(8,128)(2,1)S(1)} %get-tuple-element.42), channel_id=1, source_target_pairs={{40,104},{48,112},{56,120},{64,0},{72,8},{80,16},{104,168},{112,17... | collective-permute-start | bytes 147464 | tf_op jit(solution)/shard_map/ppermute | solution.py:219

commit v6 on v5

--- a/solution.py
+++ b/solution.py
@@ -40,11 +40,13 @@
 
 
 def select_rows(select_ref, sends_ref, offsets, rows):
+    sends = sends_ref[...].astype(F32).astype(jnp.int32)
+
     def block(offset):
         picks = jnp.full((1, 64), rows, jnp.int32)
         for slot in range(2 * REACH):
             kept = slot - REACH if slot < REACH else slot - REACH + 1
-            picks = jnp.where(offset == kept, sends_ref[slot], picks)
+            picks = jnp.where(offset == kept, sends[slot : slot + 1, :], picks)
         return picks
 
     for pair in range((len(offsets) + 1) // 2):
@@ -58,14 +60,13 @@
 
 
 def begin_kernel(
-    place_ref, band_ref, sends_ref, states_ref, held_ref, own_ref, cross_ref, crossing_ref
+    place_ref, band_ref, sends_ref, states_ref, own_ref, cross_ref, crossing_ref
 ):
     place = place_ref[0]
     rows = states_ref.shape[0]
     first = jnp.where(place >= 5, GROUP - place, -REACH - place)
     select_rows(cross_ref, sends_ref, [first + at for at in range(REACH)], rows)
-    crossing_ref[...] = dot(cross_ref[...], states_ref[...].astype(BF16)).astype(BF16)
-    held_ref[...] = states_ref[...]
+    crossing_ref[...] = dot(cross_ref[...], states_ref[...]).astype(BF16)
     select_rows(own_ref, sends_ref, [at - place for at in range(GROUP)], rows)
 
 
@@ -238,17 +239,17 @@
     place = jnp.bitwise_and(lax.axis_index("grid"), GROUP - 1).reshape(1)
     band = lax.axis_index("band").reshape(1)
 
-    held, own, cross, crossing = call(
+    own, cross, crossing = call(
         begin_kernel,
-        (place, band, jnp.swapaxes(send_rows, 0, 1), states),
+        (place, band, send_rows[0].astype(BF16), states.astype(BF16)),
         [SMEM, SMEM, VMEM, VMEM],
-        [shape((rows, width)), shape((slots, rows), BF16), shape((REACH * 64, rows), BF16), shape((REACH * 64, width), BF16)],
+        [shape((slots, rows), BF16), shape((REACH * 64, rows), BF16), shape((REACH * 64, width), BF16)],
         10_000_000,
     )
     relayed = across(crossing, parts)
     high, low, halos, factors, part, outgoing = call(
         build_kernel,
-        (bounds.reshape(1, 3), potential.reshape(1, rows), stencil_table, held, own),
+        (bounds.reshape(1, 3), potential.reshape(1, rows), stencil_table, states, own),
         [VMEM] * 5,
         [
             shape((rows, rows), BF16),
@@ -260,7 +261,7 @@
         ],
         50_000_000,
     )
-    before, fields = None, held
+    before, fields = None, states
     for degree in range(DEGREE):
         if degree > 0:
             relayed = across(extra, parts)

time: 115 us -> 115 us (level)
  local copies, waits for them, and re-layouts: 2.44 us -> 0.87 us
    unnamed x10, local copies, waits for them, and re-layouts: 2.26 us -> 0.69 us
where the time goes in v6:
time: 115 us; the launch traced here: 114 us
  blocking collectives  90.2 us (78%)
  waiting for transfers between devices  10.3 us (9%)
  Pallas kernels  5.86 us (5%)
  starting transfers between devices  3.88 us (3%)
  other arithmetic  1.67 us (1%)
  between operations  1.46 us (1%)
    all_to_all x3, blocking collectives, exchanged(): lax.all_to_all(message, 'grid', 0, 0, axis_index_groups=groups, tiled=True)  47.5 us
    all_to_all x1, blocking collectives, on_device(): lax.all_to_all(partial_sums.reshape(parts, 2, bands * width), 'grid', 0,...  31.2 us
    ppermute x3, waiting for transfers between devices, across(): return lax.ppermute(crossing, 'grid', route)  10.3 us
    all_to_all x1, blocking collectives, on_device(): lax.all_to_all(extra, 'band', 0, 0, axis_index_groups=alike, tiled=True)  9.31 us
    pallas_call x9, Pallas kernels, call(): pl.pallas_call(kernel, out_shape=tuple(outs), in_specs=specs, out_specs=t...  5.86 us
    ppermute x3, starting transfers between devices, across(): return lax.ppermute(crossing, 'grid', route)  3.88 us
  transfers between devices with their start and end apart: 3, of which 3 were waited for; matrix products, arithmetic and copies ran while one was open for 0% of the time, Pallas kernels for 3%

profile of v6, /device:TPU:8, one launch (start us, length us, event | category | flops | bytes accessed | tf_op | source)
XLA Modules:
  0.0 114.2 jit_solution(12840211559612487333)
XLA Ops:
  0.6 0.0 copy-start.4
  0.6 0.0 copy-start
  0.7 1.0 convert_element_type.13.states_ref
  1.6 0.0 copy-done.4
  1.7 0.0 copy-start.1
  1.7 0.4 shard_map.77
  2.0 1.3 %collective-permute-start = (bf16[192,128]{1,0:T(8,128)(2,1)S(1)}, bf16[192,128]{1,0:T(8,128)(2,1)S(1)}, u32[]{:S(2)}, u32[]{:S(2)}) collective-permute-start(bf16[192,128]{1,0:T(8,128)(2,1)S(1)} %get-tuple-element.27), channel_id=1, source_target_pairs={{40,104},{48,112},{56,120},{64,0},{72,8},{80,16},{104,168},{112,17... | collective-permute-start | bytes 147464 | tf_op jit(solution)/shard_map/ppermute | solution.py:220
  3.4 0.1 pad.7.clone
  3.4 0.0 copy-start.2
  3.4 0.0 copy-start.3
  3.4 0.0 copy-done
  3.4 0.0 copy-done.1
  3.4 0.7 copy-done.2
  4.1 0.0 copy-done.3
  4.1 2.7 %shard_map.78 = (bf16[256,256]{1,0:T(8,128)(2,1)S(1)}, bf16[256,256]{1,0:T(8,128)(2,1)S(1)}, bf16[256,384]{1,0:T(8,128)(2,1)S(1)}, f32[6,8,128]{2,1,0:T(8,128)S(...) custom-call(f32[1,3]{1,0:T(1,128)S(1)} %bitcast.10, f32[1,256]{1,0:T(1,128)S(1)} %bitcast.9, ...), custom_call_target="tpu_custom_call" | custom-call | flops 50000000 | bytes 1176588 | tf_op jit(solution)/shard_map/pallas_call | solution.py:197
  6.8 1.6 %collective-permute-done = bf16[192,128]{1,0:T(8,128)(2,1)S(1)} collective-permute-done((bf16[192,128]{1,0:T(8,128)(2,1)S(1)}, bf16[192,128]{1,0:T(8,128)(2,1)S(1)}, u32[]{:S(2)}, u32[]{:S(2)}) %collective-permute-start) | collective-permute-done | bytes 49184 | tf_op jit(solution)/shard_map/ppermute | solution.py:220
  8.4 0.1 maximum_add_fusion
  8.5 21.0 %all_to_all.25.halo_ref = bf16[8,64,128]{2,1,0:T(8,128)(2,1)S(1)} all-to-all(bf16[8,64,128]{2,1,0:T(8,128)(2,1)S(1)} %bitcast.12), channel_id=1, replica_groups={{0,8,16,24,32,40,48,56},{64,72,80,88,96,104,112,120},{128,136,144,152,1..., dimensions={0} | all-to-all | bytes 262144 | tf_op jit(solution)/shard_map/all_to_all | solution.py:230
  29.5 0.4 shard_map.79
  30.0 1.3 %collective-permute-start.1 = (bf16[192,128]{1,0:T(8,128)(2,1)S(1)}, bf16[192,128]{1,0:T(8,128)(2,1)S(1)}, u32[]{:S(2)}, u32[]{:S(2)}) collective-permute-start(bf16[192,128]{1,0:T(8,128)(2,1)S(1)} %get-tuple-element.35), channel_id=1, source_target_pairs={{40,104},{48,112},{56,120},{64,0},{72,8},{80,16},{104,168},{112,17... | collective-permute-start | bytes 147464 | tf_op jit(solution)/shard_map/ppermute | solution.py:220
  31.9 0.3 shard_map.80
  32.2 4.0 %collective-permute-done.1 = bf16[192,128]{1,0:T(8,128)(2,1)S(1)} collective-permute-done((bf16[192,128]{1,0:T(8,128)(2,1)S(1)}, bf16[192,128]{1,0:T(8,128)(2,1)S(1)}, u32[]{:S(2)}, u32[]{:S(2)}) %collective-permute-start.1) | collective-permute-done | bytes 49184 | tf_op jit(solution)/shard_map/ppermute | solution.py:220
  36.3 0.1 maximum_add_fusion.1
  36.5 13.3 %all_to_all.26.halo_ref = bf16[8,64,128]{2,1,0:T(8,128)(2,1)S(1)} all-to-all(bf16[8,64,128]{2,1,0:T(8,128)(2,1)S(1)} %bitcast.13), channel_id=1, replica_groups={{0,8,16,24,32,40,48,56},{64,72,80,88,96,104,112,120},{128,136,144,152,1..., dimensions={0} | all-to-all | bytes 262144 | tf_op jit(solution)/shard_map/all_to_all | solution.py:230
  49.7 0.4 shard_map.81
  50.1 1.3 %collective-permute-start.2 = (bf16[192,128]{1,0:T(8,128)(2,1)S(1)}, bf16[192,128]{1,0:T(8,128)(2,1)S(1)}, u32[]{:S(2)}, u32[]{:S(2)}) collective-permute-start(bf16[192,128]{1,0:T(8,128)(2,1)S(1)} %get-tuple-element.40), channel_id=1, source_target_pairs={{40,104},{48,112},{56,120},{64,0},{72,8},{80,16},{104,168},{112,17... | collective-permute-start | bytes 147464 | tf_op jit(solution)/shard_map/ppermute | solution.py:220
  51.4 0.3 shard_map.82
  51.8 4.7 %collective-permute-done.2 = bf16[192,128]{1,0:T(8,128)(2,1)S(1)} collective-permute-done((bf16[192,128]{1,0:T(8,128)(2,1)S(1)}, bf16[192,128]{1,0:T(8,128)(2,1)S(1)}, u32[]{:S(2)}, u32[]{:S(2)}) %collective-permute-start.2) | collective-permute-done | bytes 49184 | tf_op jit(solution)/shard_map/ppermute | solution.py:220
  56.5 0.1 maximum_add_fusion.2
  56.6 13.2 %all_to_all.27.halo_ref = bf16[8,64,128]{2,1,0:T(8,128)(2,1)S(1)} all-to-all(bf16[8,64,128]{2,1,0:T(8,128)(2,1)S(1)} %bitcast.11), channel_id=1, replica_groups={{0,8,16,24,32,40,48,56},{64,72,80,88,96,104,112,120},{128,136,144,152,1..., dimensions={0} | all-to-all | bytes 262144 | tf_op jit(solution)/shard_map/all_to_all | solution.py:230
  69.8 0.2 shard_map.83
  70.1 9.3 %all_to_all.28 = bf16[4,256,128]{2,1,0:T(8,128)(2,1)S(1)} all-to-all(bf16[4,256,128]{2,1,0:T(8,128)(2,1)S(1)} %get-tuple-element.43), channel_id=1, replica_groups={{0,2,4,6},{1,3,5,7},{8,10,12,14},{9,11,13,15},{16,18,20,22},{17,19,21,2..., dimensions={0} | all-to-all | bytes 524288 | tf_op jit(solution)/shard_map/all_to_all | solution.py:299
  79.4 2.2 %all_gather.3.every_ref = bf16[8,256,128]{2,1,0:T(8,128)(2,1)S(1)} all-gather(bf16[4,256,128]{2,1,0:T(8,128)(2,1)S(1)} %all_to_all.28), channel_id=1, replica_groups={{0,1},{2,3},{4,5},{6,7},{8,9},{10,11},{12,13},{14,15},{16,17},{18,19},{..., dimensions={0}, use_global_device_ids=true | all-gather | bytes 786432 | tf_op jit(solution)/shard_map/all_gather | solution.py:300
  81.5 0.5 shard_map.84
  82.0 0.1 reshape.36
  82.1 31.2 %all_to_all.29 = bf16[64,2,1024]{2,1,0:T(2,128)(2,1)S(1)} all-to-all(bf16[64,2,1024]{2,1,0:T(2,128)(2,1)S(1)} %reshape.36), channel_id=1, replica_groups=mesh['grid'=64,'band'=8] {'grid'}, dimensions={0} | all-to-all | bytes 524288 | tf_op jit(solution)/shard_map/all_to_all | solution.py:308
  113.3 0.2 convert_reduce_fusion.summed_ref
  113.6 0.7 shard_map.85
  (5 shorter events, 0.0 us)
Async XLA Ops:
  0.6 1.0 copy-start.4
  0.6 2.8 %copy-start = (f32[256,128]{1,0:T(8,128)S(1)}, f32[256,128]{1,0:T(8,128)}, u32[]{:S(2)}) copy-start(f32[256,128]{1,0:T(8,128)} %states_ref.3) | copy-start | bytes 393220
  1.7 1.8 %copy-start.1 = (s32[36,256]{1,0:T(8,128)S(1)}, s32[36,256]{1,0:T(8,128)}, u32[]{:S(2)}) copy-start(s32[36,256]{1,0:T(8,128)} %table_ref.1) | copy-start | bytes 110596
  2.0 6.3 %collective-permute-start = (bf16[192,128]{1,0:T(8,128)(2,1)S(1)}, bf16[192,128]{1,0:T(8,128)(2,1)S(1)}, u32[]{:S(2)}, u32[]{:S(2)}) collective-permute-start(bf16[192,128]{1,0:T(8,128)(2,1)S(1)} %get-tuple-element.27), channel_id=1, source_target_pairs={{40,104},{48,112},{56,120},{64,0},{72,8},{80,16},{104,168},{112,17... | collective-permute-start | bytes 147464 | tf_op jit(solution)/shard_map/ppermute | solution.py:220
  3.4 0.7 copy-start.2
  3.4 0.7 copy-start.3
  30.0 6.3 %collective-permute-start.1 = (bf16[192,128]{1,0:T(8,128)(2,1)S(1)}, bf16[192,128]{1,0:T(8,128)(2,1)S(1)}, u32[]{:S(2)}, u32[]{:S(2)}) collective-permute-start(bf16[192,128]{1,0:T(8,128)(2,1)S(1)} %get-tuple-element.35), channel_id=1, source_target_pairs={{40,104},{48,112},{56,120},{64,0},{72,8},{80,16},{104,168},{112,17... | collective-permute-start | bytes 147464 | tf_op jit(solution)/shard_map/ppermute | solution.py:220
  50.1 6.3 %collective-permute-start.2 = (bf16[192,128]{1,0:T(8,128)(2,1)S(1)}, bf16[192,128]{1,0:T(8,128)(2,1)S(1)}, u32[]{:S(2)}, u32[]{:S(2)}) collective-permute-start(bf16[192,128]{1,0:T(8,128)(2,1)S(1)} %get-tuple-element.40), channel_id=1, source_target_pairs={{40,104},{48,112},{56,120},{64,0},{72,8},{80,16},{104,168},{112,17... | collective-permute-start | bytes 147464 | tf_op jit(solution)/shard_map/ppermute | solution.py:220

commit v7 on v6

--- a/solution.py
+++ b/solution.py
@@ -77,8 +77,8 @@
 
 
 def build_kernel(
-    bounds_ref, potential_ref, table_ref, states_ref, own_ref,
-    high_ref, low_ref, halos_ref, factors_ref, part_ref, outgoing_ref
+    bounds_ref, potential_ref, table_ref, states_ref, own_ref, cross_ref,
+    high_ref, low_ref, halos_ref, factors_ref, part_ref, outgoing_ref, reach_ref, base_ref
 ):
     rows = states_ref.shape[0]
     stencil = table_ref.shape[0]
@@ -126,48 +126,69 @@
         halos_ref[pl.ds(TILE, TILE), pl.ds(column, TILE)] = low
 
     local_part(states_ref[...], high_ref, low_ref, own_ref, part_ref, outgoing_ref)
-
-
-def masking_kernel(
-    count_ref, states_ref, fields_ref, high_ref, low_ref, own_ref, start_ref, masked_ref, part_ref, outgoing_ref
-):
-    live = lax.broadcasted_iota(jnp.int32, states_ref.shape, 0) < count_ref[0]
-    start_ref[...] = jnp.where(live, states_ref[...], 0.0)
-    masked_ref[...] = jnp.where(live, fields_ref[...], 0.0)
-    local_part(masked_ref[...], high_ref, low_ref, own_ref, part_ref, outgoing_ref)
-
-
-def local_kernel(fields_ref, high_ref, low_ref, own_ref, part_ref, outgoing_ref):
-    local_part(fields_ref[...], high_ref, low_ref, own_ref, part_ref, outgoing_ref)
-
-
-def update_kernel(degree, place_ref, factors_ref, part_ref, halo_ref, halos_ref, *rest):
-    refs = list(rest)
-    before_ref = refs.pop(0) if degree > 0 else None
-    cross_ref = refs.pop(0) if degree < DEGREE - 1 else None
-    fields_ref, extra_ref = refs
-    scale = factors_ref[2 * degree][:1]
-    carried = factors_ref[2 * degree + 1][:1]
-    rows = part_ref.shape[0]
+    crossing = cross_ref.shape[0]
+    for at in range(2):
+        named = dot(cross_ref[:, rows - TILE :], halos_ref[pl.ds(at * TILE, TILE), :])
+        reach_ref[pl.ds(at * crossing, crossing), :] = named.astype(BF16)
+    base_ref[...] = selected(cross_ref, part_ref[...] * factors_ref[0][:1])
+
+
+def selected(select_ref, values):
+    high, low = split(values)
+    return dot(select_ref[...], high) + dot(select_ref[...], low)
+
+
+def in_order(place_ref, halo_ref):
     blocks = []
     for slot in range(2 * REACH):
         offset = slot - REACH if slot < REACH else slot - REACH + 1
         blocks.append(halo_ref[jnp.bitwise_and(place_ref[0] - offset, GROUP - 1)])
-    reached = dot(halos_ref[...], jnp.concatenate(blocks, axis=0))
+    return jnp.concatenate(blocks, axis=0)
+
+
+def crossing_kernel(degree, place_ref, factors_ref, base_ref, halo_ref, reach_ref, crossing_ref):
+    rows = crossing_ref.shape[0]
+    reached = dot(reach_ref[...], in_order(place_ref, halo_ref))
+    reached = (reached[:rows] + reached[rows:]) * factors_ref[2 * degree][:1]
+    crossing_ref[...] = (base_ref[...] + reached).astype(BF16)
+
+
+def updated(degree, place_ref, factors_ref, part_ref, halo_ref, halos_ref, before_ref):
+    rows = part_ref.shape[0]
+    reached = dot(halos_ref[...], in_order(place_ref, halo_ref))
     reached = reached[:TILE] + reached[TILE:]
-    for at in range(0, rows, TILE):
-        image = part_ref[pl.ds(at, TILE), :]
-        if at == rows - TILE:
-            image = image + reached
-        image = image * scale
-        if degree > 0:
-            image = image - carried * before_ref[pl.ds(at, TILE), :]
-        fields_ref[pl.ds(at, TILE), :] = image
-        if degree == DEGREE - 1:
-            for copy in range(extra_ref.shape[0]):
-                extra_ref[copy, pl.ds(at, TILE), :] = image.astype(BF16)
-    if degree < DEGREE - 1:
-        extra_ref[...] = dot(cross_ref[...], fields_ref[...].astype(BF16)).astype(BF16)
+    image = jnp.concatenate([part_ref[pl.ds(0, rows - TILE), :], part_ref[pl.ds(rows - TILE, TILE), :] + reached], axis=0)
+    image = image * factors_ref[2 * degree][:1]
+    if degree > 0:
+        image = image - factors_ref[2 * degree + 1][:1] * before_ref[...]
+    return image
+
+
+def first_kernel(
+    place_ref, count_ref, factors_ref, old_ref, halo_ref, halos_ref, states_ref, high_ref, low_ref, own_ref, cross_ref,
+    fields_ref, part_ref, outgoing_ref, start_ref, base_ref
+):
+    live = lax.broadcasted_iota(jnp.int32, states_ref.shape, 0) < count_ref[0]
+    start_ref[...] = jnp.where(live, states_ref[...], 0.0)
+    fields_ref[...] = jnp.where(live, updated(0, place_ref, factors_ref, old_ref, halo_ref, halos_ref, None), 0.0)
+    local_part(fields_ref[...], high_ref, low_ref, own_ref, part_ref, outgoing_ref)
+    base_ref[...] = selected(
+        cross_ref, part_ref[...] * factors_ref[2][:1] - factors_ref[3][:1] * start_ref[...]
+    )
+
+
+def second_kernel(
+    place_ref, factors_ref, old_ref, halo_ref, halos_ref, start_ref, high_ref, low_ref, own_ref,
+    fields_ref, part_ref, outgoing_ref
+):
+    fields_ref[...] = updated(1, place_ref, factors_ref, old_ref, halo_ref, halos_ref, start_ref)
+    local_part(fields_ref[...], high_ref, low_ref, own_ref, part_ref, outgoing_ref)
+
+
+def last_kernel(place_ref, factors_ref, part_ref, halo_ref, halos_ref, before_ref, fields_ref, copies_ref):
+    fields_ref[...] = updated(2, place_ref, factors_ref, part_ref, halo_ref, halos_ref, before_ref)
+    for copy in range(copies_ref.shape[0]):
+        copies_ref[copy] = fields_ref[...].astype(BF16)
 
 
 def end_kernel(scaling, fields_ref, summed_ref, filtered_ref, margin_ref):
@@ -239,18 +260,19 @@
     place = jnp.bitwise_and(lax.axis_index("grid"), GROUP - 1).reshape(1)
     band = lax.axis_index("band").reshape(1)
 
+    rounded, send_rows = lax.optimization_barrier((states.astype(BF16), send_rows))
     own, cross, crossing = call(
         begin_kernel,
-        (place, band, send_rows[0].astype(BF16), states.astype(BF16)),
+        (place, band, send_rows[0].astype(BF16), rounded),
         [SMEM, SMEM, VMEM, VMEM],
         [shape((slots, rows), BF16), shape((REACH * 64, rows), BF16), shape((REACH * 64, width), BF16)],
         10_000_000,
     )
     relayed = across(crossing, parts)
-    high, low, halos, factors, part, outgoing = call(
+    high, low, halos, factors, part, outgoing, reach, base = call(
         build_kernel,
-        (bounds.reshape(1, 3), potential.reshape(1, rows), stencil_table, states, own),
-        [VMEM] * 5,
+        (bounds.reshape(1, 3), potential.reshape(1, rows), stencil_table, states, own, cross),
+        [VMEM] * 6,
         [
             shape((rows, rows), BF16),
             shape((rows, rows), BF16),
@@ -258,42 +280,50 @@
             shape((2 * DEGREE, 8, TILE)),
             shape((rows, width)),
             shape((slots, width), BF16),
+            shape((2 * REACH * 64, 2 * REACH * 64), BF16),
+            shape((REACH * 64, width)),
         ],
         50_000_000,
     )
-    before, fields = None, states
-    for degree in range(DEGREE):
-        if degree > 0:
-            relayed = across(extra, parts)
-            operands = [fields, high, low, own]
-            outs = [shape((rows, width)), shape((slots, width), BF16)]
-            if degree == 1:
-                before, fields, part, outgoing = call(
-                    masking_kernel,
-                    [point_count, before] + operands,
-                    [SMEM] + [VMEM] * 5,
-                    [shape((rows, width))] * 2 + outs,
-                    80_000_000,
-                )
-            else:
-                part, outgoing = call(local_kernel, operands, [VMEM] * 4, outs, 80_000_000)
-        halo = exchanged(outgoing, relayed, place[0], parts)
-        operands = [place, factors, part, halo, halos]
-        if degree > 0:
-            operands.append(before)
-        if degree < DEGREE - 1:
-            operands.append(cross)
-            after = shape((REACH * 64, width), BF16)
-        else:
-            after = shape((bands // 2, rows, width), BF16)
-        before = fields
-        fields, extra = call(
-            functools.partial(update_kernel, degree),
-            operands,
-            [SMEM] + [VMEM] * (len(operands) - 1),
-            [shape((rows, width)), after],
+    square = shape((rows, width))
+    outs = [square, square, shape((slots, width), BF16)]
+
+    def crossed(degree, base, halo):
+        (crossing,) = call(
+            functools.partial(crossing_kernel, degree),
+            (place, factors, base, halo, reach),
+            [SMEM] + [VMEM] * 4,
+            [shape((REACH * 64, width), BF16)],
             40_000_000,
         )
+        return across(crossing, parts)
+
+    halo = exchanged(outgoing, relayed, place[0], parts)
+    relayed = crossed(0, base, halo)
+    first, part, outgoing, start, base = call(
+        first_kernel,
+        (place, point_count, factors, part, halo, halos, states, high, low, own, cross),
+        [SMEM, SMEM] + [VMEM] * 9,
+        outs + [square, shape((REACH * 64, width))],
+        80_000_000,
+    )
+    halo = exchanged(outgoing, relayed, place[0], parts)
+    relayed = crossed(1, base, halo)
+    second, part, outgoing = call(
+        second_kernel,
+        (place, factors, part, halo, halos, start, high, low, own),
+        [SMEM] + [VMEM] * 8,
+        outs,
+        80_000_000,
+    )
+    halo = exchanged(outgoing, relayed, place[0], parts)
+    fields, extra = call(
+        last_kernel,
+        (place, factors, part, halo, halos, first),
+        [SMEM] + [VMEM] * 5,
+        [square, shape((bands // 2, rows, width), BF16)],
+        40_000_000,
+    )
     alike = [list(range(core, bands, 2)) for core in range(2)]
     chips = [[first, first + 1] for first in range(0, bands, 2)]
     alike_bands = lax.all_to_all(extra, "band", 0, 0, axis_index_groups=alike, tiled=True)

time: 115 us -> 114 us (level)
    ppermute x3, waiting for transfers between devices: 10.3 us -> 9.18 us  [across(): return lax.ppermute(crossing, 'grid', route)]
  transfers between devices with their start and end apart: 3 -> 3, of which waited for: 3 -> 3; matrix products, arithmetic and copies ran while one was open for 0% -> 0% of each run, Pallas kernels for 3% -> 4%
where the time goes in v7:
time: 114 us
  blocking collectives  90.2 us (79%)
  waiting for transfers between devices  9.18 us (8%)
  Pallas kernels  6.71 us (6%)
  starting transfers between devices  3.88 us (3%)
  other arithmetic  1.67 us (1%)
  between operations  1.46 us (1%)
    all_to_all x3, blocking collectives, exchanged(): lax.all_to_all(message, 'grid', 0, 0, axis_index_groups=groups, tiled=True)  47.6 us
    all_to_all x1, blocking collectives, on_device(): lax.all_to_all(partial_sums.reshape(parts, 2, bands * width), 'grid', 0,...  31.1 us
    all_to_all x1, blocking collectives, on_device(): lax.all_to_all(extra, 'band', 0, 0, axis_index_groups=alike, tiled=True)  9.31 us
    ppermute x3, waiting for transfers between devices, across(): return lax.ppermute(crossing, 'grid', route)  9.18 us
    pallas_call x9, Pallas kernels, call(): pl.pallas_call(kernel, out_shape=tuple(outs), in_specs=specs, out_specs=t...  6.71 us
    ppermute x3, starting transfers between devices, across(): return lax.ppermute(crossing, 'grid', route)  3.88 us
  transfers between devices with their start and end apart: 3, of which 3 were waited for; matrix products, arithmetic and copies ran while one was open for 0% of the time, Pallas kernels for 4%

profile of v7, /device:TPU:8, one launch (start us, length us, event | category | flops | bytes accessed | tf_op | source)
XLA Modules:
  0.0 113.9 jit_solution(12502771914206111853)
XLA Ops:
  0.6 0.0 copy-start.4
  0.6 0.0 copy-start
  0.7 1.0 convert_element_type.11.states_ref
  1.6 0.0 copy-done.4
  1.7 0.0 copy-start.1
  1.7 0.4 shard_map.77
  2.0 1.3 %collective-permute-start = (bf16[192,128]{1,0:T(8,128)(2,1)S(1)}, bf16[192,128]{1,0:T(8,128)(2,1)S(1)}, u32[]{:S(2)}, u32[]{:S(2)}) collective-permute-start(bf16[192,128]{1,0:T(8,128)(2,1)S(1)} %get-tuple-element.31), channel_id=1, source_target_pairs={{40,104},{48,112},{56,120},{64,0},{72,8},{80,16},{104,168},{112,17... | collective-permute-start | bytes 147464 | tf_op jit(solution)/shard_map/ppermute | solution.py:241
  3.4 0.1 pad.7.clone
  3.4 0.0 copy-start.2
  3.4 0.0 copy-start.3
  3.4 0.0 copy-done
  3.4 0.0 copy-done.1
  3.4 0.7 copy-done.2
  4.1 0.0 copy-done.3
  4.1 2.8 %shard_map.78 = (bf16[256,256]{1,0:T(8,128)(2,1)S(1)}, bf16[256,256]{1,0:T(8,128)(2,1)S(1)}, bf16[256,384]{1,0:T(8,128)(2,1)S(1)}, f32[6,8,128]{2,1,0:T(8,128)S(...) custom-call(f32[1,3]{1,0:T(1,128)S(1)} %bitcast.10, ...), custom_call_target="tpu_custom_call" | custom-call | flops 50000000 | bytes 1668108 | tf_op jit(solution)/shard_map/pallas_call | solution.py:218
  6.9 1.4 %collective-permute-done = bf16[192,128]{1,0:T(8,128)(2,1)S(1)} collective-permute-done((bf16[192,128]{1,0:T(8,128)(2,1)S(1)}, bf16[192,128]{1,0:T(8,128)(2,1)S(1)}, u32[]{:S(2)}, u32[]{:S(2)}) %collective-permute-start) | collective-permute-done | bytes 49184 | tf_op jit(solution)/shard_map/ppermute | solution.py:241
  8.4 0.1 maximum_add_fusion
  8.5 21.2 %all_to_all.25.halo_ref = bf16[8,64,128]{2,1,0:T(8,128)(2,1)S(1)} all-to-all(bf16[8,64,128]{2,1,0:T(8,128)(2,1)S(1)} %bitcast.12), channel_id=1, replica_groups={{0,8,16,24,32,40,48,56},{64,72,80,88,96,104,112,120},{128,136,144,152,1..., dimensions={0} | all-to-all | bytes 262144 | tf_op jit(solution)/shard_map/all_to_all | solution.py:251
  29.7 0.2 shard_map.80
  30.0 1.3 %collective-permute-start.1 = (bf16[192,128]{1,0:T(8,128)(2,1)S(1)}, bf16[192,128]{1,0:T(8,128)(2,1)S(1)}, u32[]{:S(2)}, u32[]{:S(2)}) collective-permute-start(bf16[192,128]{1,0:T(8,128)(2,1)S(1)} %shard_map.80), channel_id=1, source_target_pairs={{40,104},{48,112},{56,120},{64,0},{72,8},{80,16},{104,168},{112,17... | collective-permute-start | bytes 147464 | tf_op jit(solution)/shard_map/ppermute | solution.py:241
  31.9 0.7 shard_map.79
  32.6 3.7 %collective-permute-done.1 = bf16[192,128]{1,0:T(8,128)(2,1)S(1)} collective-permute-done((bf16[192,128]{1,0:T(8,128)(2,1)S(1)}, bf16[192,128]{1,0:T(8,128)(2,1)S(1)}, u32[]{:S(2)}, u32[]{:S(2)}) %collective-permute-start.1) | collective-permute-done | bytes 49184 | tf_op jit(solution)/shard_map/ppermute | solution.py:241
  36.3 0.1 maximum_add_fusion.1
  36.4 13.3 %all_to_all.26.halo_ref = bf16[8,64,128]{2,1,0:T(8,128)(2,1)S(1)} all-to-all(bf16[8,64,128]{2,1,0:T(8,128)(2,1)S(1)} %bitcast.13), channel_id=1, replica_groups={{0,8,16,24,32,40,48,56},{64,72,80,88,96,104,112,120},{128,136,144,152,1..., dimensions={0} | all-to-all | bytes 262144 | tf_op jit(solution)/shard_map/all_to_all | solution.py:251
  49.7 0.2 shard_map.82
  50.0 1.3 %collective-permute-start.2 = (bf16[192,128]{1,0:T(8,128)(2,1)S(1)}, bf16[192,128]{1,0:T(8,128)(2,1)S(1)}, u32[]{:S(2)}, u32[]{:S(2)}) collective-permute-start(bf16[192,128]{1,0:T(8,128)(2,1)S(1)} %shard_map.82), channel_id=1, source_target_pairs={{40,104},{48,112},{56,120},{64,0},{72,8},{80,16},{104,168},{112,17... | collective-permute-start | bytes 147464 | tf_op jit(solution)/shard_map/ppermute | solution.py:241
  51.3 0.9 shard_map.81
  52.2 4.1 %collective-permute-done.2 = bf16[192,128]{1,0:T(8,128)(2,1)S(1)} collective-permute-done((bf16[192,128]{1,0:T(8,128)(2,1)S(1)}, bf16[192,128]{1,0:T(8,128)(2,1)S(1)}, u32[]{:S(2)}, u32[]{:S(2)}) %collective-permute-start.2) | collective-permute-done | bytes 49184 | tf_op jit(solution)/shard_map/ppermute | solution.py:241
  56.3 0.1 maximum_add_fusion.2
  56.5 13.2 %all_to_all.27.halo_ref = bf16[8,64,128]{2,1,0:T(8,128)(2,1)S(1)} all-to-all(bf16[8,64,128]{2,1,0:T(8,128)(2,1)S(1)} %bitcast.11), channel_id=1, replica_groups={{0,8,16,24,32,40,48,56},{64,72,80,88,96,104,112,120},{128,136,144,152,1..., dimensions={0} | all-to-all | bytes 262144 | tf_op jit(solution)/shard_map/all_to_all | solution.py:251
  69.7 0.2 shard_map.83
  69.9 9.3 %all_to_all.28 = bf16[4,256,128]{2,1,0:T(8,128)(2,1)S(1)} all-to-all(bf16[4,256,128]{2,1,0:T(8,128)(2,1)S(1)} %get-tuple-element.45), channel_id=1, replica_groups={{0,2,4,6},{1,3,5,7},{8,10,12,14},{9,11,13,15},{16,18,20,22},{17,19,21,2..., dimensions={0} | all-to-all | bytes 524288 | tf_op jit(solution)/shard_map/all_to_all | solution.py:329
  79.2 2.2 %all_gather.3.every_ref = bf16[8,256,128]{2,1,0:T(8,128)(2,1)S(1)} all-gather(bf16[4,256,128]{2,1,0:T(8,128)(2,1)S(1)} %all_to_all.28), channel_id=1, replica_groups={{0,1},{2,3},{4,5},{6,7},{8,9},{10,11},{12,13},{14,15},{16,17},{18,19},{..., dimensions={0}, use_global_device_ids=true | all-gather | bytes 786432 | tf_op jit(solution)/shard_map/all_gather | solution.py:330
  81.4 0.5 shard_map.84
  81.9 0.1 reshape.36
  82.0 31.1 %all_to_all.29 = bf16[64,2,1024]{2,1,0:T(2,128)(2,1)S(1)} all-to-all(bf16[64,2,1024]{2,1,0:T(2,128)(2,1)S(1)} %reshape.36), channel_id=1, replica_groups=mesh['grid'=64,'band'=8] {'grid'}, dimensions={0} | all-to-all | bytes 524288 | tf_op jit(solution)/shard_map/all_to_all | solution.py:338
  113.0 0.2 convert_reduce_fusion.summed_ref
  113.3 0.7 shard_map.85
  (5 shorter events, 0.0 us)
Async XLA Ops:
  0.6 1.0 copy-start.4
  0.6 2.8 %copy-start = (f32[256,128]{1,0:T(8,128)S(1)}, f32[256,128]{1,0:T(8,128)}, u32[]{:S(2)}) copy-start(f32[256,128]{1,0:T(8,128)} %states_ref.3) | copy-start | bytes 393220
  1.7 1.8 %copy-start.1 = (s32[36,256]{1,0:T(8,128)S(1)}, s32[36,256]{1,0:T(8,128)}, u32[]{:S(2)}) copy-start(s32[36,256]{1,0:T(8,128)} %table_ref.1) | copy-start | bytes 110596
  2.0 6.3 %collective-permute-start = (bf16[192,128]{1,0:T(8,128)(2,1)S(1)}, bf16[192,128]{1,0:T(8,128)(2,1)S(1)}, u32[]{:S(2)}, u32[]{:S(2)}) collective-permute-start(bf16[192,128]{1,0:T(8,128)(2,1)S(1)} %get-tuple-element.31), channel_id=1, source_target_pairs={{40,104},{48,112},{56,120},{64,0},{72,8},{80,16},{104,168},{112,17... | collective-permute-start | bytes 147464 | tf_op jit(solution)/shard_map/ppermute | solution.py:241
  3.4 0.7 copy-start.2
  3.4 0.7 copy-start.3
  30.0 6.3 %collective-permute-start.1 = (bf16[192,128]{1,0:T(8,128)(2,1)S(1)}, bf16[192,128]{1,0:T(8,128)(2,1)S(1)}, u32[]{:S(2)}, u32[]{:S(2)}) collective-permute-start(bf16[192,128]{1,0:T(8,128)(2,1)S(1)} %shard_map.80), channel_id=1, source_target_pairs={{40,104},{48,112},{56,120},{64,0},{72,8},{80,16},{104,168},{112,17... | collective-permute-start | bytes 147464 | tf_op jit(solution)/shard_map/ppermute | solution.py:241
  50.0 6.3 %collective-permute-start.2 = (bf16[192,128]{1,0:T(8,128)(2,1)S(1)}, bf16[192,128]{1,0:T(8,128)(2,1)S(1)}, u32[]{:S(2)}, u32[]{:S(2)}) collective-permute-start(bf16[192,128]{1,0:T(8,128)(2,1)S(1)} %shard_map.82), channel_id=1, source_target_pairs={{40,104},{48,112},{56,120},{64,0},{72,8},{80,16},{104,168},{112,17... | collective-permute-start | bytes 147464 | tf_op jit(solution)/shard_map/ppermute | solution.py:241

commit v8 on v7

--- a/solution.py
+++ b/solution.py
@@ -202,15 +202,16 @@
     order = [band % 2 * (bands // 2) + band // 2 for band in range(bands)]
     row = lax.broadcasted_iota(jnp.int32, (wanted, width), 0)
     column = lax.broadcasted_iota(jnp.int32, (wanted, width), 1)
-    target = jnp.right_shift(row, 1) * wanted + 2 * band_ref[0] + jnp.bitwise_and(row, 1)
+    target = (bands - 1 - jnp.right_shift(row, 1)) * wanted + 2 * band_ref[0] + jnp.bitwise_and(row, 1)
     pick = jnp.where(column == target, 1.0, 0.0).astype(BF16)
     chosen = [
         lax.dot_general(pick, every_ref[order[band]], (((1,), (1,)), ((), ())), preferred_element_type=F32).astype(BF16)
-        for band in range(bands)
+        for band in reversed(range(bands))
     ]
     chosen = jnp.concatenate(chosen, axis=0)
-    for band in range(bands):
-        partial_ref[:, pl.ds(band * width, width)] = dot(chosen, every_ref[order[band]]).astype(BF16)
+    for band in range(0, bands, 2):
+        both = jnp.concatenate([every_ref[order[band]], every_ref[order[band + 1]]], axis=1)
+        partial_ref[:, pl.ds(band * width, 2 * width)] = dot(chosen, both).astype(BF16)
 
 
 def call(kernel, operands, specs, outs, flops, scratch=()):
@@ -335,7 +336,14 @@
         [shape((2 * parts, bands * width), BF16)],
         80_000_000,
     )
-    blocks = lax.all_to_all(partial_sums.reshape(parts, 2, bands * width), "grid", 0, 0, tiled=True)
+    blocks = lax.all_to_all(
+        partial_sums.reshape(parts, 2, bands * width),
+        "grid",
+        0,
+        0,
+        axis_index_groups=[list(reversed(range(parts)))],
+        tiled=True,
+    )
     summed = jnp.sum(blocks.astype(F32), axis=0)
     return call(
         functools.partial(end_kernel, 1.0 / (parts * rows)),

time: 114 us -> 114 us (level)
  the two profiles are of different devices: /device:TPU:8 before, /device:TPU:40 now
where the time goes in v8:
time: 114 us; the launch traced here: 113 us
  blocking collectives  101 us (89%)
  Pallas kernels  6.63 us (6%)
  starting transfers between devices  1.99 us (2%)
  other arithmetic  1.67 us (1%)
  between operations  1.47 us (1%)
    all_to_all x3, blocking collectives, exchanged(): lax.all_to_all(message, 'grid', 0, 0, axis_index_groups=groups, tiled=True)  54.5 us
    all_to_all x1, blocking collectives, on_device(): lax.all_to_all(partial_sums.reshape(parts, 2, bands * width), 'grid', 0,...  34.8 us
    all_to_all x1, blocking collectives, on_device(): lax.all_to_all(extra, 'band', 0, 0, axis_index_groups=alike, tiled=True)  9.31 us
    pallas_call x9, Pallas kernels, call(): pl.pallas_call(kernel, out_shape=tuple(outs), in_specs=specs, out_specs=t...  6.63 us
  transfers between devices with their start and end apart: 3, of which 0 were waited for; matrix products, arithmetic and copies ran while one was open for 0% of the time, Pallas kernels for 4%

profile of v8, /device:TPU:40, one launch (start us, length us, event | category | flops | bytes accessed | tf_op | source)
XLA Modules:
  0.0 113.5 jit_solution(3181611103819431713)
XLA Ops:
  0.6 0.0 copy-start.4
  0.6 0.0 copy-start
  0.7 1.0 convert_element_type.11.states_ref
  1.6 0.0 copy-done.4
  1.7 0.0 copy-start.1
  1.7 0.4 shard_map.77
  2.0 0.7 collective-permute-start
  2.7 0.1 pad.7.clone
  2.8 0.0 copy-start.2
  2.8 0.0 copy-start.3
  2.8 0.0 copy-done
  2.8 0.0 copy-done.1
  2.8 0.7 copy-done.2
  3.5 0.0 copy-done.3
  3.5 2.8 %shard_map.78 = (bf16[256,256]{1,0:T(8,128)(2,1)S(1)}, bf16[256,256]{1,0:T(8,128)(2,1)S(1)}, bf16[256,384]{1,0:T(8,128)(2,1)S(1)}, f32[6,8,128]{2,1,0:T(8,128)S(...) custom-call(f32[1,3]{1,0:T(1,128)S(1)} %bitcast.10, ...), custom_call_target="tpu_custom_call" | custom-call | flops 50000000 | bytes 1668108 | tf_op jit(solution)/shard_map/pallas_call | solution.py:219
  6.3 0.0 collective-permute-done
  6.3 0.1 maximum_add_fusion
  6.5 18.8 %all_to_all.25.halo_ref = bf16[8,64,128]{2,1,0:T(8,128)(2,1)S(1)} all-to-all(bf16[8,64,128]{2,1,0:T(8,128)(2,1)S(1)} %bitcast.12), channel_id=1, replica_groups={{0,8,16,24,32,40,48,56},{64,72,80,88,96,104,112,120},{128,136,144,152,1..., dimensions={0} | all-to-all | bytes 262144 | tf_op jit(solution)/shard_map/all_to_all | solution.py:252
  25.3 0.2 shard_map.80
  25.6 0.7 collective-permute-start.1
  26.9 0.7 shard_map.79
  27.6 0.0 collective-permute-done.1
  27.7 0.1 maximum_add_fusion.1
  27.8 17.5 %all_to_all.26.halo_ref = bf16[8,64,128]{2,1,0:T(8,128)(2,1)S(1)} all-to-all(bf16[8,64,128]{2,1,0:T(8,128)(2,1)S(1)} %bitcast.13), channel_id=1, replica_groups={{0,8,16,24,32,40,48,56},{64,72,80,88,96,104,112,120},{128,136,144,152,1..., dimensions={0} | all-to-all | bytes 262144 | tf_op jit(solution)/shard_map/all_to_all | solution.py:252
  45.4 0.2 shard_map.82
  45.6 0.7 collective-permute-start.2
  46.3 0.9 shard_map.81
  47.2 0.0 collective-permute-done.2
  47.2 0.1 maximum_add_fusion.2
  47.4 18.1 %all_to_all.27.halo_ref = bf16[8,64,128]{2,1,0:T(8,128)(2,1)S(1)} all-to-all(bf16[8,64,128]{2,1,0:T(8,128)(2,1)S(1)} %bitcast.11), channel_id=1, replica_groups={{0,8,16,24,32,40,48,56},{64,72,80,88,96,104,112,120},{128,136,144,152,1..., dimensions={0} | all-to-all | bytes 262144 | tf_op jit(solution)/shard_map/all_to_all | solution.py:252
  65.5 0.2 shard_map.83
  65.7 9.3 %all_to_all.28 = bf16[4,256,128]{2,1,0:T(8,128)(2,1)S(1)} all-to-all(bf16[4,256,128]{2,1,0:T(8,128)(2,1)S(1)} %get-tuple-element.45), channel_id=1, replica_groups={{0,2,4,6},{1,3,5,7},{8,10,12,14},{9,11,13,15},{16,18,20,22},{17,19,21,2..., dimensions={0} | all-to-all | bytes 524288 | tf_op jit(solution)/shard_map/all_to_all | solution.py:330
  75.0 2.2 %all_gather.3.every_ref = bf16[8,256,128]{2,1,0:T(8,128)(2,1)S(1)} all-gather(bf16[4,256,128]{2,1,0:T(8,128)(2,1)S(1)} %all_to_all.28), channel_id=1, replica_groups={{0,1},{2,3},{4,5},{6,7},{8,9},{10,11},{12,13},{14,15},{16,17},{18,19},{..., dimensions={0}, use_global_device_ids=true | all-gather | bytes 786432 | tf_op jit(solution)/shard_map/all_gather | solution.py:331
  77.2 0.4 shard_map.84
  77.6 0.1 reshape.36
  77.7 34.8 %all_to_all.29 = bf16[64,2,1024]{2,1,0:T(2,128)(2,1)S(1)} all-to-all(bf16[64,2,1024]{2,1,0:T(2,128)(2,1)S(1)} %reshape.36), channel_id=1, replica_groups={{504,496,488,480,472,464,456,448,440,432,424,416,408,400,392,384,376,36..., dimensions={0} | all-to-all | bytes 524288 | tf_op jit(solution)/shard_map/all_to_all | solution.py:339
  112.6 0.2 convert_reduce_fusion.summed_ref
  112.8 0.7 shard_map.85
  (5 shorter events, 0.0 us)
Async XLA Ops:
  0.6 1.0 copy-start.4
  0.6 2.2 %copy-start = (f32[256,128]{1,0:T(8,128)S(1)}, f32[256,128]{1,0:T(8,128)}, u32[]{:S(2)}) copy-start(f32[256,128]{1,0:T(8,128)} %states_ref.3) | copy-start | bytes 393220
  1.7 1.2 %copy-start.1 = (s32[36,256]{1,0:T(8,128)S(1)}, s32[36,256]{1,0:T(8,128)}, u32[]{:S(2)}) copy-start(s32[36,256]{1,0:T(8,128)} %table_ref.1) | copy-start | bytes 110596
  2.0 4.3 %collective-permute-start = (bf16[192,128]{1,0:T(8,128)(2,1)S(1)}, bf16[192,128]{1,0:T(8,128)(2,1)S(1)}, u32[]{:S(2)}, u32[]{:S(2)}) collective-permute-start(bf16[192,128]{1,0:T(8,128)(2,1)S(1)} %get-tuple-element.31), channel_id=1, source_target_pairs={{40,104},{48,112},{56,120},{64,0},{72,8},{80,16},{104,168},{112,17... | collective-permute-start | bytes 147464 | tf_op jit(solution)/shard_map/ppermute | solution.py:242
  2.8 0.7 copy-start.2
  2.8 0.7 copy-start.3
  25.6 2.1 %collective-permute-start.1 = (bf16[192,128]{1,0:T(8,128)(2,1)S(1)}, bf16[192,128]{1,0:T(8,128)(2,1)S(1)}, u32[]{:S(2)}, u32[]{:S(2)}) collective-permute-start(bf16[192,128]{1,0:T(8,128)(2,1)S(1)} %shard_map.80), channel_id=1, source_target_pairs={{40,104},{48,112},{56,120},{64,0},{72,8},{80,16},{104,168},{112,17... | collective-permute-start | bytes 147464 | tf_op jit(solution)/shard_map/ppermute | solution.py:242
  45.6 1.6 %collective-permute-start.2 = (bf16[192,128]{1,0:T(8,128)(2,1)S(1)}, bf16[192,128]{1,0:T(8,128)(2,1)S(1)}, u32[]{:S(2)}, u32[]{:S(2)}) collective-permute-start(bf16[192,128]{1,0:T(8,128)(2,1)S(1)} %shard_map.82), channel_id=1, source_target_pairs={{40,104},{48,112},{56,120},{64,0},{72,8},{80,16},{104,168},{112,17... | collective-permute-start | bytes 147464 | tf_op jit(solution)/shard_map/ppermute | solution.py:242

commit v9 on v8

--- a/solution.py
+++ b/solution.py
@@ -60,14 +60,13 @@
 
 
 def begin_kernel(
-    place_ref, band_ref, sends_ref, states_ref, own_ref, cross_ref, crossing_ref
+    place_ref, band_ref, sends_ref, states_ref, cross_ref, crossing_ref
 ):
     place = place_ref[0]
     rows = states_ref.shape[0]
     first = jnp.where(place >= 5, GROUP - place, -REACH - place)
     select_rows(cross_ref, sends_ref, [first + at for at in range(REACH)], rows)
     crossing_ref[...] = dot(cross_ref[...], states_ref[...]).astype(BF16)
-    select_rows(own_ref, sends_ref, [at - place for at in range(GROUP)], rows)
 
 
 def local_part(fields, high_ref, low_ref, own_ref, part_ref, outgoing_ref):
@@ -77,7 +76,7 @@
 
 
 def build_kernel(
-    bounds_ref, potential_ref, table_ref, states_ref, own_ref, cross_ref,
+    place_ref, bounds_ref, potential_ref, table_ref, states_ref, sends_ref, cross_ref, own_ref,
     high_ref, low_ref, halos_ref, factors_ref, part_ref, outgoing_ref, reach_ref, base_ref
 ):
     rows = states_ref.shape[0]
@@ -125,6 +124,7 @@
         halos_ref[pl.ds(0, TILE), pl.ds(column, TILE)] = high
         halos_ref[pl.ds(TILE, TILE), pl.ds(column, TILE)] = low
 
+    select_rows(own_ref, sends_ref, [at - place_ref[0] for at in range(GROUP)], rows)
     local_part(states_ref[...], high_ref, low_ref, own_ref, part_ref, outgoing_ref)
     crossing = cross_ref.shape[0]
     for at in range(2):
@@ -262,19 +262,21 @@
     band = lax.axis_index("band").reshape(1)
 
     rounded, send_rows = lax.optimization_barrier((states.astype(BF16), send_rows))
-    own, cross, crossing = call(
+    sends = send_rows[0].astype(BF16)
+    cross, crossing = call(
         begin_kernel,
-        (place, band, send_rows[0].astype(BF16), rounded),
+        (place, band, sends, rounded),
         [SMEM, SMEM, VMEM, VMEM],
-        [shape((slots, rows), BF16), shape((REACH * 64, rows), BF16), shape((REACH * 64, width), BF16)],
+        [shape((REACH * 64, rows), BF16), shape((REACH * 64, width), BF16)],
         10_000_000,
     )
     relayed = across(crossing, parts)
-    high, low, halos, factors, part, outgoing, reach, base = call(
+    own, high, low, halos, factors, part, outgoing, reach, base = call(
         build_kernel,
-        (bounds.reshape(1, 3), potential.reshape(1, rows), stencil_table, states, own, cross),
-        [VMEM] * 6,
+        (place, bounds.reshape(1, 3), potential.reshape(1, rows), stencil_table, states, sends, cross),
+        [SMEM] + [VMEM] * 6,
         [
+            shape((slots, rows), BF16),
             shape((rows, rows), BF16),
             shape((rows, rows), BF16),
             shape((2 * TILE, 2 * REACH * 64), BF16),

time: 114 us -> 114 us (level)
  no operation moved by 1% of the time
where the time goes in v9:
time: 114 us
  blocking collectives  101 us (89%)
  Pallas kernels  6.73 us (6%)
  starting transfers between devices  1.99 us (2%)
  other arithmetic  1.67 us (1%)
  between operations  1.48 us (1%)
    all_to_all x3, blocking collectives, exchanged(): lax.all_to_all(message, 'grid', 0, 0, axis_index_groups=groups, tiled=True)  54.5 us
    all_to_all x1, blocking collectives, on_device(): lax.all_to_all(partial_sums.reshape(parts, 2, bands * width), 'grid', 0,...  34.9 us
    all_to_all x1, blocking collectives, on_device(): lax.all_to_all(extra, 'band', 0, 0, axis_index_groups=alike, tiled=True)  9.31 us
    pallas_call x9, Pallas kernels, call(): pl.pallas_call(kernel, out_shape=tuple(outs), in_specs=specs, out_specs=t...  6.73 us
  transfers between devices with their start and end apart: 3, of which 0 were waited for; matrix products, arithmetic and copies ran while one was open for 0% of the time, Pallas kernels for 4%

profile of v9, /device:TPU:40, one launch (start us, length us, event | category | flops | bytes accessed | tf_op | source)
XLA Modules:
  0.0 113.6 jit_solution(11252582205667277085)
XLA Ops:
  0.6 0.0 copy-start.4
  0.6 0.0 copy-start
  0.7 1.0 convert_element_type.11.states_ref
  1.6 0.0 copy-done.4
  1.7 0.0 copy-start.1
  1.7 0.3 shard_map.77
  2.0 0.7 collective-permute-start
  2.7 0.1 pad.7.clone
  2.8 0.0 copy-start.2
  2.8 0.0 copy-start.3
  2.8 0.0 copy-done
  2.8 0.0 copy-done.1
  2.8 0.7 copy-done.2
  3.5 0.0 copy-done.3
  3.5 3.0 %shard_map.78 = (bf16[512,256]{1,0:T(8,128)(2,1)S(1)}, bf16[256,256]{1,0:T(8,128)(2,1)S(1)}, bf16[256,256]{1,0:T(8,128)(2,1)S(1)}, bf16[256,384]{1,0:T(8,128)(2,...) custom-call(s32[1]{0:T(128)} %bitcast.place_ref, ...), custom_call_target="tpu_custom_call" | custom-call | flops 50000000 | bytes 1668880 | tf_op jit(solution)/shard_map/pallas_call | solution.py:219
  6.4 0.0 collective-permute-done
  6.4 0.1 maximum_add_fusion
  6.6 18.8 %all_to_all.25.halo_ref = bf16[8,64,128]{2,1,0:T(8,128)(2,1)S(1)} all-to-all(bf16[8,64,128]{2,1,0:T(8,128)(2,1)S(1)} %bitcast.12), channel_id=1, replica_groups={{0,8,16,24,32,40,48,56},{64,72,80,88,96,104,112,120},{128,136,144,152,1..., dimensions={0} | all-to-all | bytes 262144 | tf_op jit(solution)/shard_map/all_to_all | solution.py:252
  25.4 0.2 shard_map.80
  25.7 0.7 collective-permute-start.1
  27.0 0.7 shard_map.79
  27.7 0.0 collective-permute-done.1
  27.8 0.1 maximum_add_fusion.1
  27.9 17.5 %all_to_all.26.halo_ref = bf16[8,64,128]{2,1,0:T(8,128)(2,1)S(1)} all-to-all(bf16[8,64,128]{2,1,0:T(8,128)(2,1)S(1)} %bitcast.13), channel_id=1, replica_groups={{0,8,16,24,32,40,48,56},{64,72,80,88,96,104,112,120},{128,136,144,152,1..., dimensions={0} | all-to-all | bytes 262144 | tf_op jit(solution)/shard_map/all_to_all | solution.py:252
  45.5 0.2 shard_map.82
  45.7 0.7 collective-permute-start.2
  46.4 1.0 shard_map.81
  47.3 0.0 collective-permute-done.2
  47.3 0.1 maximum_add_fusion.2
  47.5 18.1 %all_to_all.27.halo_ref = bf16[8,64,128]{2,1,0:T(8,128)(2,1)S(1)} all-to-all(bf16[8,64,128]{2,1,0:T(8,128)(2,1)S(1)} %bitcast.11), channel_id=1, replica_groups={{0,8,16,24,32,40,48,56},{64,72,80,88,96,104,112,120},{128,136,144,152,1..., dimensions={0} | all-to-all | bytes 262144 | tf_op jit(solution)/shard_map/all_to_all | solution.py:252
  65.6 0.2 shard_map.83
  65.8 9.3 %all_to_all.28 = bf16[4,256,128]{2,1,0:T(8,128)(2,1)S(1)} all-to-all(bf16[4,256,128]{2,1,0:T(8,128)(2,1)S(1)} %get-tuple-element.45), channel_id=1, replica_groups={{0,2,4,6},{1,3,5,7},{8,10,12,14},{9,11,13,15},{16,18,20,22},{17,19,21,2..., dimensions={0} | all-to-all | bytes 524288 | tf_op jit(solution)/shard_map/all_to_all | solution.py:332
  75.1 2.2 %all_gather.3.every_ref = bf16[8,256,128]{2,1,0:T(8,128)(2,1)S(1)} all-gather(bf16[4,256,128]{2,1,0:T(8,128)(2,1)S(1)} %all_to_all.28), channel_id=1, replica_groups={{0,1},{2,3},{4,5},{6,7},{8,9},{10,11},{12,13},{14,15},{16,17},{18,19},{..., dimensions={0}, use_global_device_ids=true | all-gather | bytes 786432 | tf_op jit(solution)/shard_map/all_gather | solution.py:333
  77.3 0.4 shard_map.84
  77.7 0.1 reshape.36
  77.8 34.9 %all_to_all.29 = bf16[64,2,1024]{2,1,0:T(2,128)(2,1)S(1)} all-to-all(bf16[64,2,1024]{2,1,0:T(2,128)(2,1)S(1)} %reshape.36), channel_id=1, replica_groups={{504,496,488,480,472,464,456,448,440,432,424,416,408,400,392,384,376,36..., dimensions={0} | all-to-all | bytes 524288 | tf_op jit(solution)/shard_map/all_to_all | solution.py:341
  112.7 0.2 convert_reduce_fusion.summed_ref
  112.9 0.7 shard_map.85
  (5 shorter events, 0.0 us)
Async XLA Ops:
  0.6 1.0 copy-start.4
  0.6 2.1 %copy-start = (f32[256,128]{1,0:T(8,128)S(1)}, f32[256,128]{1,0:T(8,128)}, u32[]{:S(2)}) copy-start(f32[256,128]{1,0:T(8,128)} %states_ref.3) | copy-start | bytes 393220
  1.7 1.1 copy-start.1
  2.0 4.4 %collective-permute-start = (bf16[192,128]{1,0:T(8,128)(2,1)S(1)}, bf16[192,128]{1,0:T(8,128)(2,1)S(1)}, u32[]{:S(2)}, u32[]{:S(2)}) collective-permute-start(bf16[192,128]{1,0:T(8,128)(2,1)S(1)} %get-tuple-element.30), channel_id=1, source_target_pairs={{40,104},{48,112},{56,120},{64,0},{72,8},{80,16},{104,168},{112,17... | collective-permute-start | bytes 147464 | tf_op jit(solution)/shard_map/ppermute | solution.py:242
  2.8 0.7 copy-start.2
  2.8 0.7 copy-start.3
  25.7 2.1 %collective-permute-start.1 = (bf16[192,128]{1,0:T(8,128)(2,1)S(1)}, bf16[192,128]{1,0:T(8,128)(2,1)S(1)}, u32[]{:S(2)}, u32[]{:S(2)}) collective-permute-start(bf16[192,128]{1,0:T(8,128)(2,1)S(1)} %shard_map.80), channel_id=1, source_target_pairs={{40,104},{48,112},{56,120},{64,0},{72,8},{80,16},{104,168},{112,17... | collective-permute-start | bytes 147464 | tf_op jit(solution)/shard_map/ppermute | solution.py:242
  45.7 1.6 %collective-permute-start.2 = (bf16[192,128]{1,0:T(8,128)(2,1)S(1)}, bf16[192,128]{1,0:T(8,128)(2,1)S(1)}, u32[]{:S(2)}, u32[]{:S(2)}) collective-permute-start(bf16[192,128]{1,0:T(8,128)(2,1)S(1)} %shard_map.82), channel_id=1, source_target_pairs={{40,104},{48,112},{56,120},{64,0},{72,8},{80,16},{104,168},{112,17... | collective-permute-start | bytes 147464 | tf_op jit(solution)/shard_map/ppermute | solution.py:242

commit v10 on v8

--- a/solution.py
+++ b/solution.py
@@ -243,11 +243,11 @@
 
 
 def exchanged(outgoing, relayed, place, parts):
-    zeros = jnp.zeros_like(relayed)
-    down = jnp.where(place >= 5, relayed, zeros)
-    up = jnp.where(place <= 2, relayed, zeros)
-    gap = jnp.zeros((outgoing.shape[0] - 2 * relayed.shape[0], relayed.shape[1]), BF16)
-    message = (outgoing + jnp.concatenate([down, gap, up], axis=0)).reshape(GROUP, -1, outgoing.shape[1])
+    size = relayed.shape[0]
+    gap = outgoing.shape[0] - size
+    down = jnp.pad(jnp.where(place >= 5, relayed, jnp.zeros_like(relayed)), ((0, gap), (0, 0)))
+    up = jnp.pad(jnp.where(place <= 2, relayed, jnp.zeros_like(relayed)), ((gap, 0), (0, 0)))
+    message = (outgoing + down + up).reshape(GROUP, -1, outgoing.shape[1])
     groups = [list(range(first, first + GROUP)) for first in range(0, parts, GROUP)]
     received = lax.all_to_all(message, "grid", 0, 0, axis_index_groups=groups, tiled=True)
     return received

time: 114 us -> 114 us (level)
  no operation moved by 1% of the time
where the time goes in v10:
time: 114 us; the launch traced here: 113 us
  blocking collectives  101 us (89%)
  Pallas kernels  6.63 us (6%)
  starting transfers between devices  1.99 us (2%)
  between operations  1.51 us (1%)
  other arithmetic  1.35 us (1%)
    all_to_all x3, blocking collectives, exchanged(): lax.all_to_all(message, 'grid', 0, 0, axis_index_groups=groups, tiled=True)  54.5 us
    all_to_all x1, blocking collectives, on_device(): lax.all_to_all(partial_sums.reshape(parts, 2, bands * width), 'grid', 0,...  34.8 us
    all_to_all x1, blocking collectives, on_device(): lax.all_to_all(extra, 'band', 0, 0, axis_index_groups=alike, tiled=True)  9.31 us
    pallas_call x9, Pallas kernels, call(): pl.pallas_call(kernel, out_shape=tuple(outs), in_specs=specs, out_specs=t...  6.63 us
  transfers between devices with their start and end apart: 3, of which 0 were waited for; matrix products, arithmetic and copies ran while one was open for 0% of the time, Pallas kernels for 4%

profile of v10, /device:TPU:40, one launch (start us, length us, event | category | flops | bytes accessed | tf_op | source)
XLA Modules:
  0.0 113.1 jit_solution(1897606201483907289)
XLA Ops:
  0.6 0.0 copy-start.4
  0.6 0.0 copy-start
  0.7 1.0 convert_element_type.19.states_ref
  1.6 0.0 copy-done.4
  1.7 0.0 copy-start.1
  1.7 0.4 shard_map.77
  2.0 0.7 collective-permute-start
  2.7 0.0 copy-start.2
  2.7 0.0 copy-start.3
  2.7 0.0 copy-done
  2.7 0.0 copy-done.1
  2.8 0.6 copy-done.2
  3.4 0.0 copy-done.3
  3.4 2.8 %shard_map.78 = (bf16[256,256]{1,0:T(8,128)(2,1)S(1)}, bf16[256,256]{1,0:T(8,128)(2,1)S(1)}, bf16[256,384]{1,0:T(8,128)(2,1)S(1)}, f32[6,8,128]{2,1,0:T(8,128)S(...) custom-call(f32[1,3]{1,0:T(1,128)S(1)} %bitcast.10, ...), custom_call_target="tpu_custom_call" | custom-call | flops 50000000 | bytes 1668108 | tf_op jit(solution)/shard_map/pallas_call | solution.py:219
  6.2 0.0 collective-permute-done
  6.3 18.8 %all_to_all.25.halo_ref = bf16[8,64,128]{2,1,0:T(8,128)(2,1)S(1)} all-to-all(bf16[8,64,128]{2,1,0:T(8,128)(2,1)S(1)} %bitcast.11), channel_id=1, replica_groups={{0,8,16,24,32,40,48,56},{64,72,80,88,96,104,112,120},{128,136,144,152,1..., dimensions={0} | all-to-all | bytes 262144 | tf_op jit(solution)/shard_map/all_to_all | solution.py:252
  25.1 0.2 shard_map.80
  25.4 0.7 collective-permute-start.1
  26.7 0.7 shard_map.79
  27.4 0.0 collective-permute-done.1
  27.5 17.5 %all_to_all.26.halo_ref = bf16[8,64,128]{2,1,0:T(8,128)(2,1)S(1)} all-to-all(bf16[8,64,128]{2,1,0:T(8,128)(2,1)S(1)} %bitcast.12), channel_id=1, replica_groups={{0,8,16,24,32,40,48,56},{64,72,80,88,96,104,112,120},{128,136,144,152,1..., dimensions={0} | all-to-all | bytes 262144 | tf_op jit(solution)/shard_map/all_to_all | solution.py:252
  45.1 0.2 shard_map.82
  45.3 0.7 collective-permute-start.2
  46.0 0.9 shard_map.81
  46.9 0.0 collective-permute-done.2
  47.0 18.1 %all_to_all.27.halo_ref = bf16[8,64,128]{2,1,0:T(8,128)(2,1)S(1)} all-to-all(bf16[8,64,128]{2,1,0:T(8,128)(2,1)S(1)} %bitcast.13), channel_id=1, replica_groups={{0,8,16,24,32,40,48,56},{64,72,80,88,96,104,112,120},{128,136,144,152,1..., dimensions={0} | all-to-all | bytes 262144 | tf_op jit(solution)/shard_map/all_to_all | solution.py:252
  65.1 0.2 shard_map.83
  65.3 9.3 %all_to_all.28 = bf16[4,256,128]{2,1,0:T(8,128)(2,1)S(1)} all-to-all(bf16[4,256,128]{2,1,0:T(8,128)(2,1)S(1)} %get-tuple-element.45), channel_id=1, replica_groups={{0,2,4,6},{1,3,5,7},{8,10,12,14},{9,11,13,15},{16,18,20,22},{17,19,21,2..., dimensions={0} | all-to-all | bytes 524288 | tf_op jit(solution)/shard_map/all_to_all | solution.py:330
  74.6 2.2 %all_gather.3.every_ref = bf16[8,256,128]{2,1,0:T(8,128)(2,1)S(1)} all-gather(bf16[4,256,128]{2,1,0:T(8,128)(2,1)S(1)} %all_to_all.28), channel_id=1, replica_groups={{0,1},{2,3},{4,5},{6,7},{8,9},{10,11},{12,13},{14,15},{16,17},{18,19},{..., dimensions={0}, use_global_device_ids=true | all-gather | bytes 786432 | tf_op jit(solution)/shard_map/all_gather | solution.py:331
  76.8 0.4 shard_map.84
  77.2 0.1 reshape.36
  77.3 34.8 %all_to_all.29 = bf16[64,2,1024]{2,1,0:T(2,128)(2,1)S(1)} all-to-all(bf16[64,2,1024]{2,1,0:T(2,128)(2,1)S(1)} %reshape.36), channel_id=1, replica_groups={{504,496,488,480,472,464,456,448,440,432,424,416,408,400,392,384,376,36..., dimensions={0} | all-to-all | bytes 524288 | tf_op jit(solution)/shard_map/all_to_all | solution.py:339
  112.2 0.2 convert_reduce_fusion.summed_ref
  112.4 0.7 shard_map.85
  (7 shorter events, 0.1 us)
Async XLA Ops:
  0.6 1.0 copy-start.4
  0.6 2.1 %copy-start = (f32[256,128]{1,0:T(8,128)S(1)}, f32[256,128]{1,0:T(8,128)}, u32[]{:S(2)}) copy-start(f32[256,128]{1,0:T(8,128)} %states_ref.3) | copy-start | bytes 393220
  1.7 1.1 copy-start.1
  2.0 4.2 %collective-permute-start = (bf16[192,128]{1,0:T(8,128)(2,1)S(1)}, bf16[192,128]{1,0:T(8,128)(2,1)S(1)}, u32[]{:S(2)}, u32[]{:S(2)}) collective-permute-start(bf16[192,128]{1,0:T(8,128)(2,1)S(1)} %get-tuple-element.31), channel_id=1, source_target_pairs={{40,104},{48,112},{56,120},{64,0},{72,8},{80,16},{104,168},{112,17... | collective-permute-start | bytes 147464 | tf_op jit(solution)/shard_map/ppermute | solution.py:242
  2.7 0.7 copy-start.2
  2.7 0.7 copy-start.3
  25.4 2.1 %collective-permute-start.1 = (bf16[192,128]{1,0:T(8,128)(2,1)S(1)}, bf16[192,128]{1,0:T(8,128)(2,1)S(1)}, u32[]{:S(2)}, u32[]{:S(2)}) collective-permute-start(bf16[192,128]{1,0:T(8,128)(2,1)S(1)} %shard_map.80), channel_id=1, source_target_pairs={{40,104},{48,112},{56,120},{64,0},{72,8},{80,16},{104,168},{112,17... | collective-permute-start | bytes 147464 | tf_op jit(solution)/shard_map/ppermute | solution.py:242
  45.3 1.6 %collective-permute-start.2 = (bf16[192,128]{1,0:T(8,128)(2,1)S(1)}, bf16[192,128]{1,0:T(8,128)(2,1)S(1)}, u32[]{:S(2)}, u32[]{:S(2)}) collective-permute-start(bf16[192,128]{1,0:T(8,128)(2,1)S(1)} %shard_map.82), channel_id=1, source_target_pairs={{40,104},{48,112},{56,120},{64,0},{72,8},{80,16},{104,168},{112,17... | collective-permute-start | bytes 147464 | tf_op jit(solution)/shard_map/ppermute | solution.py:242
